TPU v7x, 128 devices: a whole 4x4x4 slice. The times are simulated.
128 devices in a mesh: data: 1, graph: 128 (over z, y, x, core).
Axes of the slice: x: 4, y: 4, z: 4, core: 2. Of those that a mesh axis runs over, the one named last changes fastest.
Arguments:
- x_feat: bfloat16 [65536, 100], P(('data', 'graph'))
- dst_local: int32 [4194304], P(('data', 'graph'))
- src_slot: int32 [4194304], P(('data', 'graph'))
- edge_w: float32 [4194304], P(('data', 'graph'))
- send_idx: int32 [32768], P(('data', 'graph'))
- hub_ids: int32 [256], P('data')
- w_first: bfloat16 [100, 256], replicated
- b_first: float32 [256], replicated
- w_second: bfloat16 [256, 47], replicated
- grad_out: float32 [65536, 47], P(('data', 'graph'))
Outputs:
- output 1: float32 [65536, 100], P(('data', 'graph'))
- output 2: float32 [100, 256], P('data')
- output 3: float32 [256, 47], P('data')
- output 4: float32 [256], P('data')
- output 5: float32 [47], P('data')
All inputs are finite; a program needn't handle non-finite values.
Results may differ from a plain program's by a relative error of at most 0.00112444.
Values are sent between devices in bfloat16 or wider.
A program may use at most 1 GiB of HBM per device.

v0:
```python
import jax
import jax.numpy as jnp
from jax import lax
from jax.sharding import PartitionSpec as P

CONTRACT_ROWS = (((0,), (0,)), ((), ()))
CONTRACT_COLS = (((1,), (1,)), ((), ()))


def hub_collect(dev_rows, hub_owned, hub_row):
    picked = jnp.where(hub_owned[:, None], dev_rows[hub_row], jnp.zeros((), dev_rows.dtype))
    return lax.psum(picked, "graph")


def hub_return(dev_rows, hub_sum, hub_owned, hub_row):
    return dev_rows.at[hub_row].add(jnp.where(hub_owned[:, None], hub_sum, 0.0))


def propagate(features, graph_data, groups):
    send_loc, hub_owned, hub_row, dst_loc, src_loc, w_loc = graph_data
    num_nodes = features.shape[0]
    send_rows = send_loc.shape[0] // groups
    outgoing = features[send_loc].reshape(groups, send_rows, -1)
    halo_feat = lax.all_to_all(outgoing, "graph", 0, 0).reshape(groups * send_rows, -1)
    hub_feat = hub_collect(features, hub_owned, hub_row)
    feat_table = jnp.concatenate([features, halo_feat, hub_feat], axis=0)
    weighted = feat_table[src_loc].astype(jnp.float32) * w_loc[:, None]
    dev_sums = jax.ops.segment_sum(weighted, dst_loc, num_segments=num_nodes + hub_row.shape[0])
    hub_sum = lax.psum(dev_sums[num_nodes:], "graph")
    return hub_return(dev_sums[:num_nodes], hub_sum, hub_owned, hub_row)


def propagate_adjoint(grad_y, graph_data, groups):
    send_loc, hub_owned, hub_row, dst_loc, src_loc, w_loc = graph_data
    num_nodes = grad_y.shape[0]
    halo_rows = send_loc.shape[0]
    hub_grad = hub_collect(grad_y, hub_owned, hub_row)
    extended = jnp.concatenate([grad_y, hub_grad], axis=0)
    weighted = extended[dst_loc] * w_loc[:, None]
    table_grad = jax.ops.segment_sum(weighted, src_loc, num_segments=num_nodes + halo_rows + hub_row.shape[0])
    outgoing = table_grad[num_nodes:num_nodes + halo_rows].reshape(groups, halo_rows // groups, -1)
    returned = lax.all_to_all(outgoing, "graph", 0, 0).reshape(halo_rows, -1)
    grad_z = table_grad[:num_nodes].at[send_loc].add(returned)
    hub_back = lax.psum(table_grad[num_nodes + halo_rows:], "graph")
    return hub_return(grad_z, hub_back, hub_owned, hub_row)


def solution(mesh):
    groups = mesh.shape["graph"]
    vertex_spec = P(("data", "graph"))
    vertex_rows = P(("data", "graph"), None)
    part_spec = P("data")
    part_rows = P("data", None)
    replicated = P()

    def device_step(x_loc, dst_loc, src_loc, w_loc, send_loc, hub_ids, w_first, b_first, w_second, dy_out):
        num_nodes = x_loc.shape[0]
        my_index = lax.axis_index("graph")
        hub_owned = (hub_ids // num_nodes) == my_index
        hub_row = hub_ids % num_nodes
        graph_data = (send_loc, hub_owned, hub_row, dst_loc, src_loc, w_loc)
        z_first = jnp.dot(x_loc, w_first, preferred_element_type=jnp.float32).astype(jnp.bfloat16)
        pre_act = propagate(z_first, graph_data, groups) + b_first
        hidden = jax.nn.relu(pre_act).astype(jnp.bfloat16)
        grad_z2 = propagate_adjoint(dy_out, graph_data, groups).astype(jnp.bfloat16)
        grad_w2 = lax.psum(lax.dot_general(hidden, grad_z2, CONTRACT_ROWS, preferred_element_type=jnp.float32), "graph")
        grad_h = lax.dot_general(grad_z2, w_second, CONTRACT_COLS, preferred_element_type=jnp.float32)
        grad_pre = jnp.where(pre_act > 0, grad_h, 0.0)
        grad_b1 = lax.psum(grad_pre.sum(axis=0), "graph")
        grad_z1 = propagate_adjoint(grad_pre, graph_data, groups).astype(jnp.bfloat16)
        grad_w1 = lax.psum(lax.dot_general(x_loc, grad_z1, CONTRACT_ROWS, preferred_element_type=jnp.float32), "graph")
        grad_x = lax.dot_general(grad_z1, w_first, CONTRACT_COLS, preferred_element_type=jnp.float32)
        grad_b2 = lax.psum(dy_out.sum(axis=0), "graph")
        return grad_x, grad_w1, grad_w2, grad_b1, grad_b2

    return jax.shard_map(
        device_step,
        mesh=mesh,
        in_specs=(vertex_rows, vertex_spec, vertex_spec, vertex_spec, vertex_spec, part_spec, replicated, replicated, replicated, vertex_rows),
        out_specs=(vertex_rows, part_rows, part_rows, part_spec, part_spec),
        check_vma=False,
    )
```

profile of v0, /device:TPU:1, one launch (start us, length us, event | category | flops | bytes accessed | tf_op | source)
XLA Modules:
  0.0 1765.9 jit_solution(6649699718761519744)
XLA Ops:
  8.7 1.1 convolution_convert_fusion
  9.8 1.2 gather_fusion.1
  12.8 69.2 %psum.72 = f32[256,47]{1,0:T(8,128)S(1)} all-reduce(f32[256,47]{1,0:T(8,128)S(1)} %broadcast_select_fusion.2), channel_id=1, replica_groups=mesh['data'=1,'graph'=128] {'graph'}, use_global_device_ids=true, to_apply=%region_4.5 | all-reduce | flops 12032 | bytes 96256 | tf_op jit(solution)/shard_map/psum | solution.py:12
  82.1 277.1 %scatter_custom_fusion.2 = f32[1024,47]{1,0:T(8,128)S(1)} fusion(s32[32768]{0:T(1024)S(1)} %copy-done.6, f32[32768]{0:T(1024)S(1)} %copy-done.2, f32[]{:T(128)} %constant.20.clone.1, f32[768,47]{1,0:T(8,128)S(1)} %pad_maximum_fusion.2, s32[32768]{0:T(1024)S(1)} %fusion.20), kind=kCustom, calls=%fused_computation.20 | custom fusion | flops 3080192 | bytes 847876 | tf_op jit(solution)/shard_map/scatter-add | solution.py:40
  359.8 43.2 %all-to-all-start.1 = ((f32[128,2,47]{2,1,0:T(2,128)}), f32[128,2,47]{2,1,0:T(2,128)S(1)}, u32[]{:S(2)}, u32[]{:S(2)}) async-start(f32[128,2,47]{2,1,0:T(2,128)} %bitcast), calls=%async_computation.1 | async-start | bytes 262144 | tf_op jit(solution)/shard_map/all_to_all | solution.py:42
  403.1 1.2 gather_fusion
  405.0 8.2 all-to-all-done.1
  413.2 4.2 all-to-all-start
  417.5 67.6 %psum.73 = f32[256,47]{1,0:T(8,128)S(1)} all-reduce(f32[256,47]{1,0:T(8,128)S(1)} %get-tuple-element.10), channel_id=1, replica_groups=mesh['data'=1,'graph'=128] {'graph'}, use_global_device_ids=true, to_apply=%region_7.8 | all-reduce | flops 12032 | bytes 96256 | tf_op jit(solution)/shard_map/psum | solution.py:44
  485.1 2.0 scatter_fusion
  487.2 2.3 scatter_custom_fusion.4
  490.6 294.7 %scatter_custom_fusion = f32[768,256]{1,0:T(8,128)S(1)} fusion(s32[32768]{0:T(1024)S(1)} %copy-done.5, f32[32768]{0:T(1024)S(1)} %copy-done.2, f32[]{:T(128)} %constant.20.clone.1, bf16[1024,256]{1,0:T(8,128)(2,1)S(1)} %pad_maximum_fusion.1, s32[32768]{0:T(1024)S(1)} %fusion.19), kind=kCustom, calls=%fused_computation.17 | custom fusion | flops 25165824 | bytes 1572868 | tf_op jit(solution)/shard_map/scatter-add | solution.py:28
  786.1 181.3 %all-reduce.9.cloned.1.call-done = f32[256,256]{1,0:T(8,128)} async-done(((f32[256,256]{1,0:T(8,128)}), f32[256,256]{1,0:T(8,128)}) %all-reduce.9.cloned.1.call-update) | async-done | bytes 262160 | tf_op jit(solution)/shard_map/psum | solution.py:29
  967.5 2.7 scatter_custom_fusion.1
  972.4 145.1 %all-reduce.11.cloned.1.call-done = f32[256,256]{1,0:T(8,128)} async-done(((f32[256,256]{1,0:T(8,128)}), f32[256,256]{1,0:T(8,128)}) %all-reduce.11.cloned.1.call-update) | async-done | bytes 262160 | tf_op jit(solution)/shard_map/psum | solution.py:12
  1117.5 1.0 pad_maximum_fusion
  1118.5 306.0 %scatter_custom_fusion.5 = f32[1024,256]{1,0:T(8,128)S(1)} fusion(s32[32768]{0:T(1024)S(1)} %copy-done.6, f32[32768]{0:T(1024)S(1)} %copy-done.2, f32[]{:T(128)} %constant.20.clone.1, f32[768,256]{1,0:T(8,128)S(1)} %pad_maximum_fusion, s32[32768]{0:T(1024)S(1)} %fusion.20), kind=kCustom, calls=%fused_computation.15 | custom fusion | flops 16777216 | bytes 2097156 | tf_op jit(solution)/shard_map/scatter-add | solution.py:40
  1426.2 44.2 %all-to-all-start.2 = ((f32[128,2,256]{2,1,0:T(2,128)}), f32[128,2,256]{2,1,0:T(2,128)S(1)}, u32[]{:S(2)}, u32[]{:S(2)}) async-start(f32[128,2,256]{2,1,0:T(2,128)} %reshape.35), calls=%async_computation.2 | async-start | bytes 524288 | tf_op jit(solution)/shard_map/all_to_all | solution.py:42
  1470.7 68.3 %all-reduce = (f32[256,47]{0,1:T(8,128)}, f32[256]{0:T(256)}, f32[47]{0:T(128)}) all-reduce(f32[256,47]{0,1:T(8,128)S(1)} %fusion.12, f32[256]{0:T(256)S(1)} %get-tuple-element.12, f32[47]{0:T(128)S(1)} %reduce_sum.19), channel_id=1, replica_groups=mesh['data'=1,'graph'=128] {'graph'}, use_global_device_ids=true, to_apply=%region_15.16 | all-reduce | flops 12335 | bytes 98680 | tf_op jit(solution)/shard_map/psum | solution.py:66
  1540.0 2.2 scatter_fusion.1
  1542.2 65.9 %all-reduce.13.cloned.1.call-done = f32[256,256]{1,0:T(8,128)} async-done(((f32[256,256]{1,0:T(8,128)}), f32[256,256]{1,0:T(8,128)}) %all-reduce.13.cloned.1.call-update) | async-done | bytes 262160 | tf_op jit(solution)/shard_map/psum | solution.py:44
  1608.1 2.7 scatter_custom_fusion.7
  1612.5 145.3 %all-reduce.15.cloned.1.call-done = f32[100,256]{1,0:T(8,128)} async-done(((f32[100,256]{1,0:T(8,128)}), f32[100,256]{1,0:T(8,128)}) %all-reduce.15.cloned.1.call-update) | async-done | bytes 102416 | tf_op jit(solution)/shard_map/psum | solution.py:71
  1757.8 1.5 copy.32
  (64 shorter events, 13.5 us)
Async XLA Ops:
  7.2 1.5 copy-start
  7.2 4.5 copy-start.5
  7.2 482.4 %all-reduce.7.cloned.1.call-start = ((), (), s32[]{:S(2)}) async-start(), calls=%async_computation.3 | async-start | bytes 262144 | tf_op jit(solution)/shard_map/psum | solution.py:12
  8.7 3.1 copy-start.3
  11.9 70.1 %copy-start.2 = (f32[32768]{0:T(1024)S(1)}, f32[32768]{0:T(1024)}, u32[]{:S(2)}) copy-start(f32[32768]{0:T(1024)} %param.13) | copy-start | bytes 393220
  11.9 70.1 %copy-start.6 = (s32[32768]{0:T(1024)S(1)}, s32[32768]{0:T(1024)}, u32[]{:S(2)}) copy-start(s32[32768]{0:T(1024)} %param.12) | copy-start | bytes 393220
  82.1 321.0 %copy-start.9 = (s32[256]{0:T(256)S(1)}, s32[256]{0:T(256)}, u32[]{:S(2)}) copy-start(s32[256]{0:T(256)} %param.14) | copy-start | bytes 3076
  359.8 53.4 %all-to-all-start.1 = ((f32[128,2,47]{2,1,0:T(2,128)}), f32[128,2,47]{2,1,0:T(2,128)S(1)}, u32[]{:S(2)}, u32[]{:S(2)}) async-start(f32[128,2,47]{2,1,0:T(2,128)} %bitcast), calls=%async_computation.1 | async-start | bytes 262144 | tf_op jit(solution)/shard_map/all_to_all | solution.py:42
  413.2 76.3 %all-to-all-start = ((bf16[128,2,256]{2,1,0:T(2,128)(2,1)}), bf16[128,2,256]{2,1,0:T(2,128)(2,1)S(1)}, u32[]{:S(2)}, u32[]{:S(2)}) async-start(bf16[128,2,256]{2,1,0:T(2,128)(2,1)} %reshape.31), calls=%async_computation | async-start | bytes 262144 | tf_op jit(solution)/shard_map/all_to_all | solution.py:24
  417.4 550.1 %all-reduce.9.cloned.1.call-start = ((), (), s32[]{:S(2)}) async-start(), calls=%async_computation.4 | async-start | bytes 524288 | tf_op jit(solution)/shard_map/psum | solution.py:29
  490.6 295.5 %copy-start.8 = (f32[256]{0:T(256)S(1)}, f32[256]{0:T(256)}, u32[]{:S(2)}) copy-start(f32[256]{0:T(256)} %param.17) | copy-start | bytes 3076
  786.0 184.2 %copy-start.7 = (bf16[256,47]{0,1:T(8,128)(2,1)S(1)}, bf16[256,47]{0,1:T(8,128)(2,1)}, u32[]{:S(2)}) copy-start(bf16[256,47]{0,1:T(8,128)(2,1)} %param.18) | copy-start | bytes 72196
  786.0 331.5 %all-reduce.11.cloned.1.call-start = ((), (), s32[]{:S(2)}) async-start(), calls=%async_computation.5 | async-start | bytes 524288 | tf_op jit(solution)/shard_map/psum | solution.py:12
  972.2 635.9 %all-reduce.13.cloned.1.call-start = ((), (), s32[]{:S(2)}) async-start(), calls=%async_computation.6 | async-start | bytes 524288 | tf_op jit(solution)/shard_map/psum | solution.py:44
  1424.5 114.5 %copy-start.1 = (f32[1024,256]{1,0:T(8,128)}, f32[1024,256]{1,0:T(8,128)S(1)}, u32[]{:S(2)}) copy-start(f32[1024,256]{1,0:T(8,128)S(1)} %scatter_custom_fusion.5) | copy-start | bytes 3145732
  1426.2 112.8 %all-to-all-start.2 = ((f32[128,2,256]{2,1,0:T(2,128)}), f32[128,2,256]{2,1,0:T(2,128)S(1)}, u32[]{:S(2)}, u32[]{:S(2)}) async-start(f32[128,2,256]{2,1,0:T(2,128)} %reshape.35), calls=%async_computation.2 | async-start | bytes 524288 | tf_op jit(solution)/shard_map/all_to_all | solution.py:42
  1470.4 287.4 %all-reduce.15.cloned.1.call-start = ((), (), s32[]{:S(2)}) async-start(), calls=%async_computation.7 | async-start | bytes 212992 | tf_op jit(solution)/shard_map/psum | solution.py:71
  1539.0 1.0 slice-start
  1542.2 69.5 %copy-start.4 = (bf16[100,256]{1,0:T(8,128)(2,1)S(1)}, bf16[100,256]{1,0:T(8,128)(2,1)}, u32[]{:S(2)}) copy-start(bf16[100,256]{1,0:T(8,128)(2,1)} %param.16) | copy-start | bytes 153604
Sparse Core Ops, SparseCore 0:
  12.7 149.4 all-reduce.6
  786.1 181.2 all-reduce.8
  972.3 145.1 all-reduce.10
  1425.5 182.5 all-reduce.12
  1613.2 144.5 all-reduce.14
where the time goes:
time: 1770 us
  other arithmetic  895 us (51%)
  waiting for transfers between devices  546 us (31%)
  blocking collectives  205 us (12%)
  starting transfers between devices  91.9 us (5%)
    scatter-add x2, other arithmetic, propagate_adjoint(): jax.ops.segment_sum(weighted, src_loc, num_segments=num_nodes + halo_rows...  583 us
    scatter-add x1, other arithmetic, propagate(): jax.ops.segment_sum(weighted, dst_loc, num_segments=num_nodes + hub_row.s...  295 us
    psum x1, waiting for transfers between devices, propagate(): hub_sum = lax.psum(dev_sums[num_nodes:], 'graph')  181 us
    psum x1, waiting for transfers between devices, device_step(): lax.psum(lax.dot_general(x_loc, grad_z1, CONTRACT_ROWS, preferred_element...  145 us
    psum x2, waiting for transfers between devices, hub_collect(): return lax.psum(picked, 'graph')  145 us
    all_to_all x2, starting transfers between devices, propagate_adjoint(): returned = lax.all_to_all(outgoing, 'graph', 0, 0).reshape(halo_rows, -1)  87.5 us
    psum x1, blocking collectives, hub_collect(): return lax.psum(picked, 'graph')  69.2 us
    psum x1, blocking collectives, device_step(): lax.psum(lax.dot_general(hidden, grad_z2, CONTRACT_ROWS, preferred_elemen...  68.3 us
  transfers between devices with their start and end apart: 8, of which 5 were waited for; matrix products, arithmetic and copies ran while one was open for 16% of the time, Pallas kernels for 0%

commit v1 on v0

v1 whole, which is shorter than its diff:
```python
import functools

import jax
import jax.numpy as jnp
from jax import lax
from jax.experimental import pallas as pl
from jax.experimental.pallas import tpu as pltpu
from jax.sharding import PartitionSpec as P

BF16 = jnp.bfloat16
F32 = jnp.float32
HI = lax.Precision.HIGHEST
LANES = 128
MESH = pl.DeviceIdType.MESH


def exchange_kernel(groups, kinds, *refs):
    count = len(kinds)
    ins, outs, sems = refs[:count], refs[count:2 * count], refs[2 * count:]
    send_sems, recv_sems = sems[:count], sems[count:]
    me = lax.axis_index("graph")
    barrier = pltpu.get_barrier_semaphore()

    def greet(i, carry):
        pl.semaphore_signal(barrier, inc=1, device_id=(0, jnp.bitwise_xor(me, i)), device_id_type=MESH)
        return carry

    lax.fori_loop(1, groups, greet, 0)
    pl.semaphore_wait(barrier, groups - 1)

    def send(i, carry):
        peer = jnp.bitwise_xor(me, i)
        for kind, src, dst, send_sem, recv_sem in zip(kinds, ins, outs, send_sems, recv_sems):
            pltpu.make_async_remote_copy(
                src_ref=src.at[peer] if kind == "a" else src,
                dst_ref=dst.at[me],
                send_sem=send_sem,
                recv_sem=recv_sem,
                device_id=(0, peer),
                device_id_type=MESH,
            ).start()
        return carry

    lax.fori_loop(1, groups, send, 0)
    for kind, src, dst, recv_sem in zip(kinds, ins, outs, recv_sems):
        pltpu.make_async_copy(src.at[me] if kind == "a" else src, dst.at[me], recv_sem).start()
    for dst, send_sem, recv_sem in zip(outs, send_sems, recv_sems):
        pltpu.make_async_copy(dst, dst, recv_sem).wait()
        part = dst.at[pl.ds(0, groups - 1)]
        pltpu.make_async_copy(part, part, send_sem).wait()


def exchange(groups, kinds, arrays, collective_id):
    outs = []
    for kind, arr in zip(kinds, arrays):
        shape = arr.shape if kind == "a" else (groups,) + arr.shape
        outs.append(jax.ShapeDtypeStruct(shape, arr.dtype))
    vmem = pl.BlockSpec(memory_space=pltpu.VMEM)
    return pl.pallas_call(
        functools.partial(exchange_kernel, groups, kinds),
        out_shape=outs,
        in_specs=[vmem] * len(arrays),
        out_specs=[vmem] * len(arrays),
        scratch_shapes=[pltpu.SemaphoreType.DMA] * (2 * len(arrays)),
        compiler_params=pltpu.CompilerParams(collective_id=collective_id, has_side_effects=True),
        name=f"exchange_{collective_id}",
    )(*arrays)


def keys_kernel(own, dst_ref, src_ref, tab_ref, key_ref, lane_ref):
    tables = tab_ref.shape[0]
    dst_rows = own // LANES
    slots = own + (tables - 2 * dst_rows) * LANES + 0

    def body(i, carry):
        rows = pl.ds(pl.multiple_of(i * 8, 8), 8)
        dst = dst_ref[rows, :]
        src = src_ref[rows, :]
        dlane = jnp.bitwise_and(dst, LANES - 1)
        slane = jnp.bitwise_and(src, LANES - 1)
        dblk = jnp.right_shift(dst, 7)
        sblk = jnp.right_shift(src, 7)
        for t in range(tables):
            row = jnp.broadcast_to(tab_ref[t:t + 1, :], (8, LANES))
            if t < dst_rows:
                dst = jnp.where(dblk == t, jnp.take_along_axis(row, dlane, axis=1), dst)
            else:
                src = jnp.where(sblk == t - dst_rows, jnp.take_along_axis(row, slane, axis=1), src)
        key_ref[rows, :] = jnp.right_shift(dst, 7) * 1024 + src
        lane_ref[rows, :] = jnp.bitwise_and(dst, LANES - 1)
        return carry

    lax.fori_loop(0, dst_ref.shape[0] // 8, body, 0)


def edge_keys(dst, src, tables, own):
    rows = dst.shape[0] // LANES
    shape = jax.ShapeDtypeStruct((rows, LANES), jnp.int32)
    return pl.pallas_call(
        functools.partial(keys_kernel, own),
        out_shape=(shape, shape),
        name="edge_keys",
    )(dst.reshape(rows, LANES), src.reshape(rows, LANES), tables)


def build_kernel(slots, dsts, key_ref, lane_ref, w_ref, out_ref, *bufs):
    cells = slots * (dsts // LANES)
    chunk = 64

    def clear(i, carry):
        for buf in bufs:
            buf[pl.ds(pl.multiple_of(i * chunk, chunk), chunk), :] = jnp.zeros((chunk, LANES), F32)
        return carry

    lax.fori_loop(0, cells // chunk, clear, 0)
    lane_iota = lax.broadcasted_iota(jnp.int32, (8, LANES), 1)
    pick = lax.broadcasted_iota(jnp.int32, (8, LANES), 0) * 16

    def step(it, carry):
        lanes = jnp.broadcast_to(lane_ref[pl.ds(it, 1), :], (8, LANES))
        weights = jnp.broadcast_to(w_ref[pl.ds(it, 1), :], (8, LANES))
        vals = []
        for j in range(16):
            lane = jnp.take_along_axis(lanes, pick + j, axis=1)
            weight = jnp.take_along_axis(weights, pick + j, axis=1)
            vals.append(jnp.where(lane == lane_iota, weight, 0.0))
        for j in range(16):
            rows = [key_ref[it, s * 16 + j] for s in range(8)]
            sums = [bufs[s][pl.ds(rows[s], 1), :] + vals[j][s:s + 1, :] for s in range(8)]
            for s in range(8):
                bufs[s][pl.ds(rows[s], 1), :] = sums[s]
        return carry

    lax.fori_loop(0, key_ref.shape[0], step, 0)

    for blk in range(dsts // LANES):
        def finish(i, carry):
            rows = pl.ds(pl.multiple_of(blk * slots + i * chunk, chunk), chunk)
            total = bufs[0][rows, :]
            for buf in bufs[1:]:
                total = total + buf[rows, :]
            out_ref[pl.ds(pl.multiple_of(i * chunk, chunk), chunk), blk * LANES:(blk + 1) * LANES] = total
            return carry

        lax.fori_loop(0, slots // chunk, finish, 0)


def build_adjacency(keys, lanes, weights, slots, dsts):
    cells = slots * (dsts // LANES)
    vmem = pl.BlockSpec(memory_space=pltpu.VMEM)
    return pl.pallas_call(
        functools.partial(build_kernel, slots, dsts),
        out_shape=jax.ShapeDtypeStruct((slots, dsts), F32),
        in_specs=[pl.BlockSpec(memory_space=pltpu.SMEM), vmem, vmem],
        out_specs=vmem,
        scratch_shapes=[pltpu.VMEM((cells, LANES), F32)] * 8,
        compiler_params=pltpu.CompilerParams(vmem_limit_bytes=48 * 2 ** 20),
        name="build_adjacency",
    )(keys, lanes, weights.reshape(keys.shape))


def dot(a, b, ca=1, cb=0, precision=None):
    return lax.dot_general(a, b, (((ca,), (cb,)), ((), ())), precision=precision, preferred_element_type=F32)


def pad_cols(a):
    return jnp.pad(a, ((0, 0), (0, LANES - a.shape[1])))


def solution(mesh):
    groups = mesh.shape["graph"]

    def device_step(x, dst, src, w, send, hub_ids, w_first, b_first, w_second, dy):
        own, feat_in = x.shape
        feat_out = dy.shape[1]
        hid = w_first.shape[1]
        halo, hubs = send.shape[0], hub_ids.shape[0]
        slots, dsts = own + halo + hubs, own + hubs
        me = lax.axis_index("graph")
        own_iota = jnp.arange(own, dtype=jnp.int32)
        is_hub = (hub_ids - me * own)[:, None] == own_iota[None, :]
        code = jnp.sum(jnp.where(is_hub, jnp.arange(1, hubs + 1, dtype=jnp.int32)[:, None], 0), axis=0)
        hub_f = is_hub.astype(F32)
        hub_b = is_hub.astype(BF16)
        pick_b = (send[:, None] == own_iota[None, :]).astype(BF16)
        pick_f = pick_b.astype(F32)
        plain = (code == 0)[:, None]

        x_pad = jnp.concatenate([x, code[:, None].astype(BF16), jnp.zeros((own, LANES - feat_in - 1), BF16)], axis=1)
        dy_pad = pad_cols(dy)
        halo_x = dot(pick_b, x_pad).astype(BF16)
        hub_x = dot(hub_b, x_pad).astype(BF16)
        hub_d = dot(hub_f, dy_pad, precision=HI)
        halo_x, hub_x, hub_d = exchange(
            groups, "aaa", [v.reshape(groups, -1, LANES) for v in (halo_x, hub_x, hub_d)], 0)
        halo_x = halo_x.reshape(halo, LANES)
        home_x = hub_x.astype(F32).sum(axis=0).astype(BF16)
        hub_x, hub_d = exchange(groups, "bb", [home_x, hub_d.sum(axis=0)], 1)
        hub_x, hub_d = hub_x.reshape(hubs, LANES), hub_d.reshape(hubs, LANES)

        halo_code = halo_x[:, feat_in].astype(jnp.int32)
        hub_base = own + halo - 1
        tables = jnp.concatenate([
            jnp.where(code > 0, own - 1 + code, own_iota),
            jnp.where(code > 0, hub_base + code, own_iota),
            jnp.where(halo_code > 0, hub_base + halo_code, own + jnp.arange(halo, dtype=jnp.int32)),
        ]).reshape(-1, LANES)
        keys, lanes = edge_keys(dst, src, tables, own)
        adj = build_adjacency(keys, lanes, w, slots, dsts)

        w1_pad = jnp.pad(w_first, ((0, LANES - feat_in), (0, 0)))
        w2_pad = pad_cols(w_second)
        z = dot(jnp.concatenate([x_pad, halo_x, hub_x], axis=0), w1_pad).astype(BF16)
        y = dot(adj, z.astype(F32), 0, 0, precision=HI)
        g2 = dot(adj, jnp.concatenate([dy_pad, hub_d], axis=0), precision=HI)
        msg = jnp.concatenate([
            g2[own:own + halo].reshape(groups, -1, LANES),
            y[own:].reshape(groups, -1, LANES),
            g2[own + halo:].reshape(groups, -1, LANES),
        ], axis=1)
        (got,) = exchange(groups, "a", [msg], 2)
        per = hubs // groups
        back = got[:, :per].reshape(halo, LANES)
        dz2_own = g2[:own] + dot(pick_f, back, 0, 0, precision=HI)
        home = got[:, per:].sum(axis=0)
        y_rows = per * hid // LANES
        pre = jnp.concatenate([y[:own], home[:y_rows].reshape(per, hid)], axis=0) + b_first
        dz2 = jnp.concatenate([dz2_own, home[y_rows:]], axis=0).astype(BF16)
        keep = jnp.concatenate([plain, jnp.ones((per, 1), bool)], axis=0)
        hidden = jnp.where(keep, jax.nn.relu(pre), 0.0).astype(BF16)
        gw2 = dot(hidden, dz2, 0, 0)
        dh1 = dot(dz2, w2_pad, 1, 1)
        dy1 = jnp.where(keep & (pre > 0), dh1, 0.0)
        bias = jnp.concatenate([dy1.sum(axis=0), dy_pad.sum(axis=0)]).reshape(-1, LANES)
        hub_y, gw2, bias = exchange(
            groups, "bab", [dy1[own:].reshape(-1, LANES), gw2.reshape(groups, -1, LANES), bias], 3)
        bias = bias.sum(axis=0)
        g1 = dot(adj, jnp.concatenate([dy1[:own], hub_y.reshape(hubs, hid)], axis=0), precision=HI)
        msg = jnp.concatenate([
            g1[own:own + halo].reshape(groups, -1, LANES), g1[own + halo:].reshape(groups, -1, LANES)], axis=1)
        (got,) = exchange(groups, "a", [msg], 4)
        back = got[:, :y_rows].reshape(halo, hid)
        dz1_own = (g1[:own] + dot(pick_f, back, 0, 0, precision=HI)).astype(BF16)
        dz1_home = got[:, y_rows:].sum(axis=0).reshape(per, hid).astype(BF16)
        dz1 = jnp.concatenate([jnp.where(plain, dz1_own, jnp.zeros((), BF16)), dz1_home], axis=0)
        gw1 = dot(dz1, jnp.concatenate([x_pad, home_x], axis=0), 0, 0)
        dx = dot(dz1, w1_pad, 1, 1)
        gw1, hub_dx, gw2 = exchange(
            groups, "abb", [gw1.reshape(groups, -1, LANES), dx[own:], gw2.sum(axis=0)], 5)
        (gw1,) = exchange(groups, "b", [gw1.sum(axis=0)], 6)
        dx = jnp.where(plain, dx[:own], dot(hub_f, hub_dx.reshape(hubs, LANES), 0, 0, precision=HI))
        return (
            dx[:, :feat_in],
            gw1.reshape(hid, LANES)[:, :feat_in].T,
            gw2.reshape(hid, LANES)[:, :feat_out],
            bias[:hid // LANES].reshape(-1),
            bias[-1, :feat_out],
        )

    rows, flat = P(("data", "graph"), None), P(("data", "graph"))
    return jax.shard_map(
        device_step,
        mesh=mesh,
        in_specs=(rows, flat, flat, flat, flat, P("data"), P(), P(), P(), rows),
        out_specs=(rows, P("data", None), P("data", None), P("data"), P("data")),
        check_vma=False,
    )
```

time: 1770 us -> 246 us (0.14)
  other arithmetic: 895 us -> 15.7 us
  waiting for transfers between devices: 546 us -> 0 us
  blocking collectives: 205 us -> 0 us
  Pallas kernels: 0 us -> 184 us
  starting transfers between devices: 91.9 us -> 0 us
  matrix products: 3.26 us -> 25.1 us
    scatter-add x8 -> x0, other arithmetic: 890 us -> none  [the longest x2 583 us: propagate_adjoint(): jax.ops.segment_sum(weighted, src_loc, num_segments=num_nodes + halo_rows...]
    psum x5 -> x0, waiting for transfers between devices: 538 us -> none  [the longest x1 181 us: propagate(): hub_sum = lax.psum(dev_sums[num_nodes:], 'graph')]
    psum x3 -> x0, blocking collectives: 205 us -> none  [the longest x1 69.2 us: hub_collect(): return lax.psum(picked, 'graph')]
    pallas_call x0 -> x9, Pallas kernels: none -> 184 us  [the longest x7 123 us: exchange(): pl.pallas_call(functools.partial(exchange_kernel, groups, kinds), out_sha...]
    all_to_all x3 -> x0, starting transfers between devices: 91.7 us -> none  [the longest x2 87.5 us: propagate_adjoint(): returned = lax.all_to_all(outgoing, 'graph', 0, 0).reshape(halo_rows, -1)]
    dot_general x5 -> x14, matrix products: 3.26 us -> 25.1 us  [dot(): lax.dot_general(a, b, (((ca,), (cb,)), ((), ())), precision=precision, pr...]
  transfers between devices with their start and end apart: 8 -> 0, of which waited for: 5 -> 0; matrix products, arithmetic and copies ran while one was open for 16% -> 0% of each run, Pallas kernels for 0% -> 0%
where the time goes in v1:
time: 246 us; the launch traced here: 245 us
  Pallas kernels  184 us (75%)
  matrix products  25.1 us (10%)
  local copies, waits for them, and re-layouts  19.6 us (8%)
  other arithmetic  15.7 us (6%)
    pallas_call x7, Pallas kernels, exchange(): pl.pallas_call(functools.partial(exchange_kernel, groups, kinds), out_sha...  123 us
    pallas_call x1, Pallas kernels, build_adjacency(): pl.pallas_call(functools.partial(build_kernel, slots, dsts), out_shape=ja...  56.3 us
    dot_general x14, matrix products, dot(): lax.dot_general(a, b, (((ca,), (cb,)), ((), ())), precision=precision, pr...  25.1 us
    unnamed x33, local copies, waits for them, and re-layouts  5.95 us

profile of v1, /device:TPU:1, one launch (start us, length us, event | category | flops | bytes accessed | tf_op | source)
XLA Modules:
  0.0 245.0 jit_solution(10297231618923347707)
XLA Ops:
  2.2 1.8 convolution_convert_fusion.1
  4.0 1.8 convolution_convert_fusion.2
  5.8 2.0 fusion.8
  7.8 21.5 %exchange_0.1 = (bf16[128,2,128]{2,1,0:T(2,128)(2,1)}, bf16[128,2,128]{2,1,0:T(2,128)(2,1)}, f32[128,2,128]{2,1,0:T(2,128)}) custom-call(bf16[128,2,128]{2,1,0:T(2,128)(2,1)} %bitcast.53, bf16[128,2,128]{2,1,0:T(2,128)(2,1)} %bitcast.52, f32[128,2,128]{2,1,0:T(2,128)} %bitcast.47), custom_call_target="tpu_custom_call" | custom-call | tf_op jit(solution)/shard_map/exchange_0/pallas_call | solution.py:59
  31.3 1.6 reduce_sum.95.refs_1_
  34.2 15.4 %exchange_1.1 = (bf16[128,2,128]{2,1,0:T(2,128)(2,1)}, f32[128,2,128]{2,1,0:T(2,128)}) custom-call(bf16[2,128]{1,0:T(2,128)(2,1)} %copy-done.10, f32[2,128]{1,0:T(2,128)} %reduce_sum.95.refs_1_), custom_call_target="tpu_custom_call" | custom-call | tf_op jit(solution)/shard_map/exchange_1/pallas_call | solution.py:59
  51.6 4.4 %edge_keys.1 = (s32[256,128]{1,0:T(8,128)}, s32[256,128]{1,0:T(8,128)}) custom-call(s32[256,128]{1,0:T(8,128)} %bitcast.42, s32[256,128]{1,0:T(8,128)} %bitcast.43, s32[10,128]{1,0:T(8,128)} %add_bitcast_fusion.tab_ref), custom_call_target="tpu_custom_call" | custom-call | tf_op jit(solution)/shard_map/edge_keys/pallas_call | solution.py:99
  59.2 56.3 %build_adjacency.1 = f32[1024,768]{1,0:T(8,128)S(1)} custom-call(s32[256,128]{1,0:T(8,128)S(1)} %copy-done.1, s32[256,128]{1,0:T(8,128)S(1)} %copy-done.2, f32[256,128]{1,0:T(8,128)S(1)} %bitcast.36), custom_call_target="tpu_custom_call" | custom-call | tf_op jit(solution)/shard_map/build_adjacency/pallas_call | solution.py:151
  115.5 3.4 %fusion.9 = f32[1024,128]{1,0:T(8,128)} fusion(f32[1024,768]{1,0:T(8,128)S(1)} %build_adjacency.1, f32[256,128]{0,1:T(8,128)S(1)} %copy.35, f32[512,128]{0,1:T(8,128)S(1)} %get-tuple-element.53), kind=kOutput, calls=%fused_computation.23 | convolution fusion | flops 1208057856 | bytes 4063232 | tf_op jit(solution)/shard_map/dot_general | solution.py:163
  118.9 2.6 %fusion.63 = f32[768,256]{1,0:T(8,128)S(1)} fusion(f32[1024,768]{1,0:T(8,128)S(1)} %build_adjacency.1, bf16[1024,256]{1,0:T(8,128)(2,1)S(1)} %convolution_convert_fusion), kind=kOutput, calls=%fused_computation.97 | convolution fusion | flops 2415919104 | bytes 4456448 | tf_op jit(solution)/shard_map/dot_general | solution.py:163
  124.2 1.9 pad_maximum_fusion.refs_0_
  126.1 19.4 %exchange_2.1 = f32[128,8,128]{2,1,0:T(8,128)} custom-call(f32[128,8,128]{2,1,0:T(8,128)} %pad_maximum_fusion.refs_0_), custom_call_target="tpu_custom_call" | custom-call | tf_op jit(solution)/shard_map/exchange_2/pallas_call | solution.py:59
  147.8 1.6 fusion.2
  149.5 2.1 fusion.13
  155.0 18.4 %exchange_3.1 = (f32[128,4,128]{2,1,0:T(4,128)}, f32[128,2,128]{2,1,0:T(2,128)}, f32[128,3,128]{2,1,0:T(4,128)}) custom-call(f32[4,128]{1,0:T(4,128)} %reshape.138.refs_0_, f32[128,2,128]{2,1,0:T(2,128)} %bitcast.44, f32[3,128]{1,0:T(4,128)} %maximum_bitcast_fusion.refs_2_), custom_call_target="tpu_custom_call" | custom-call | tf_op jit(solution)/shard_map/exchange_3/pallas_call | solution.py:59
  174.5 4.6 %fusion.3 = f32[1024,256]{1,0:T(8,128)} fusion(f32[1024,768]{1,0:T(8,128)S(1)} %build_adjacency.1, f32[256,256]{1,0:T(8,128)S(1)} %reshape.141, f32[512,256]{1,0:T(8,128)} %slice.103), kind=kOutput, calls=%fused_computation.9 | convolution fusion | flops 2416115712 | bytes 4980736 | tf_op jit(solution)/shard_map/dot_general | solution.py:163
  179.2 1.7 reduce_sum.100.refs_2_
  185.3 17.2 %exchange_4.1 = f32[128,8,128]{2,1,0:T(8,128)} custom-call(f32[128,8,128]{2,1,0:T(8,128)} %pad_maximum_fusion.1.refs_0_), custom_call_target="tpu_custom_call" | custom-call | tf_op jit(solution)/shard_map/exchange_4/pallas_call | solution.py:59
  206.6 17.4 %exchange_5.1 = (f32[128,2,128]{2,1,0:T(2,128)}, f32[128,2,128]{2,1,0:T(2,128)}, f32[128,2,128]{2,1,0:T(2,128)}) custom-call(f32[128,2,128]{2,1,0:T(2,128)} %bitcast.45, f32[2,128]{1,0:T(2,128)} %slice.109.refs_1_, f32[2,128]{1,0:T(2,128)} %reduce_sum.100.refs_2_), custom_call_target="tpu_custom_call" | custom-call | tf_op jit(solution)/shard_map/exchange_5/pallas_call | solution.py:59
  224.0 1.6 reduce_sum.101.refs_0_
  225.6 1.6 copy.43
  227.3 13.5 %exchange_6.1 = f32[128,2,128]{2,1,0:T(2,128)} custom-call(f32[2,128]{1,0:T(2,128)} %reduce_sum.101.refs_0_), custom_call_target="tpu_custom_call" | custom-call | tf_op jit(solution)/shard_map/exchange_6/pallas_call | solution.py:59
  240.8 1.7 copy.42
  242.5 1.6 fusion.7
  (82 shorter events, 28.7 us)
Async XLA Ops:
  0.6 56.4 %copy-start.13 = (bf16[512,100]{0,1:T(8,128)(2,1)S(1)}, bf16[512,100]{0,1:T(8,128)(2,1)}, u32[]{:S(2)}) copy-start(bf16[512,100]{0,1:T(8,128)(2,1)} %param.10) | copy-start | bytes 307204
  0.6 56.4 %copy-start.4 = (bf16[100,256]{1,0:T(8,128)(2,1)S(1)}, bf16[100,256]{1,0:T(8,128)(2,1)}, u32[]{:S(2)}) copy-start(bf16[100,256]{1,0:T(8,128)(2,1)} %param.16) | copy-start | bytes 153604
  0.7 56.7 %copy-start = (f32[32768]{0:T(1024)S(1)}, f32[32768]{0:T(1024)}, u32[]{:S(2)}) copy-start(f32[32768]{0:T(1024)} %param.13) | copy-start | bytes 393220
  2.1 113.3 %copy-start.11 = (bf16[512,1]{0,1:T(2,128)(2,1)}, bf16[512,1]{0,1:T(2,128)(2,1)S(1)}, u32[]{:S(2)}) copy-start(bf16[512,1]{0,1:T(2,128)(2,1)S(1)} %convert_element_type.54) | copy-start | bytes 3076
  2.1 54.9 %copy-start.6 = (bf16[512,27]{0,1:T(8,128)(2,1)}, bf16[512,27]{0,1:T(8,128)(2,1)S(1)}, u32[]{:S(2)}) copy-start(bf16[512,27]{0,1:T(8,128)(2,1)S(1)} %broadcast_in_dim.57) | copy-start | bytes 82948
  31.2 3.0 %copy-start.10 = (bf16[2,128]{1,0:T(2,128)(2,1)}, bf16[2,128]{1,0:T(2,128)(2,1)S(1)}, u32[]{:S(2)}) copy-start(bf16[2,128]{1,0:T(2,128)(2,1)S(1)} %reduce_sum.94.refs_0_) | copy-start | bytes 1540
  57.4 0.9 copy-start.1
  58.3 0.9 copy-start.2
  121.5 26.3 %copy-start.9 = (s32[256]{0:T(256)S(1)}, s32[256]{0:T(256)}, u32[]{:S(2)}) copy-start(s32[256]{0:T(256)} %param.14) | copy-start | bytes 3076
  179.1 25.0 %copy-start.3 = (f32[1024,256]{1,0:T(8,128)S(1)}, f32[1024,256]{1,0:T(8,128)}, u32[]{:S(2)}) copy-start(f32[1024,256]{1,0:T(8,128)} %fusion.3) | copy-start | bytes 3145732
  183.0 21.8 %copy-start.7 = (bf16[512,27]{0,1:T(8,128)(2,1)S(1)}, bf16[512,27]{0,1:T(8,128)(2,1)}, u32[]{:S(2)}) copy-start(bf16[512,27]{0,1:T(8,128)(2,1)} %copy-done.6) | copy-start | bytes 82948
  183.0 21.8 %copy-start.8 = (bf16[2,128]{0,1:T(8,128)(2,1)S(1)}, bf16[2,128]{0,1:T(8,128)(2,1)}, u32[]{:S(2)}) copy-start(bf16[2,128]{0,1:T(8,128)(2,1)} %copy.36) | copy-start | bytes 1540
  183.0 21.8 %copy-start.12 = (bf16[512,1]{0,1:T(2,128)(2,1)S(1)}, bf16[512,1]{0,1:T(2,128)(2,1)}, u32[]{:S(2)}) copy-start(bf16[512,1]{0,1:T(2,128)(2,1)} %copy-done.11) | copy-start | bytes 3076
  183.0 21.8 %copy-start.14 = (bf16[512,100]{0,1:T(8,128)(2,1)S(1)}, bf16[512,100]{0,1:T(8,128)(2,1)}, u32[]{:S(2)}) copy-start(bf16[512,100]{0,1:T(8,128)(2,1)} %param.10) | copy-start | bytes 307204
  184.3 21.6 %copy-start.5 = (bf16[100,256]{1,0:T(8,128)(2,1)S(1)}, bf16[100,256]{1,0:T(8,128)(2,1)}, u32[]{:S(2)}) copy-start(bf16[100,256]{1,0:T(8,128)(2,1)} %param.16) | copy-start | bytes 153604

commit v2 on v1

--- a/solution.py
+++ b/solution.py
@@ -12,6 +12,10 @@
 HI = lax.Precision.HIGHEST
 LANES = 128
 MESH = pl.DeviceIdType.MESH
+
+
+def dot(a, b, ca=1, cb=0, precision=None):
+    return lax.dot_general(a, b, (((ca,), (cb,)), ((), ())), precision=precision, preferred_element_type=F32)
 
 
 def exchange_kernel(groups, kinds, *refs):
@@ -65,6 +69,13 @@
         compiler_params=pltpu.CompilerParams(collective_id=collective_id, has_side_effects=True),
         name=f"exchange_{collective_id}",
     )(*arrays)
+
+
+def split3(a):
+    hi = a.astype(BF16)
+    rest = a - hi.astype(F32)
+    mid = rest.astype(BF16)
+    return hi, mid, (rest - mid.astype(F32)).astype(BF16)
 
 
 def keys_kernel(own, dst_ref, src_ref, tab_ref, key_ref, lane_ref):
@@ -103,7 +114,7 @@
     )(dst.reshape(rows, LANES), src.reshape(rows, LANES), tables)
 
 
-def build_kernel(slots, dsts, key_ref, lane_ref, w_ref, out_ref, *bufs):
+def build_kernel(slots, dsts, key_ref, lane_ref, w_ref, hi_ref, mid_ref, low_ref, *bufs):
     cells = slots * (dsts // LANES)
     chunk = 64
 
@@ -139,7 +150,8 @@
             total = bufs[0][rows, :]
             for buf in bufs[1:]:
                 total = total + buf[rows, :]
-            out_ref[pl.ds(pl.multiple_of(i * chunk, chunk), chunk), blk * LANES:(blk + 1) * LANES] = total
+            for ref, piece in zip((hi_ref, mid_ref, low_ref), split3(total)):
+                ref[pl.ds(pl.multiple_of(i * chunk, chunk), chunk), blk * LANES:(blk + 1) * LANES] = piece
             return carry
 
         lax.fori_loop(0, slots // chunk, finish, 0)
@@ -150,17 +162,193 @@
     vmem = pl.BlockSpec(memory_space=pltpu.VMEM)
     return pl.pallas_call(
         functools.partial(build_kernel, slots, dsts),
-        out_shape=jax.ShapeDtypeStruct((slots, dsts), F32),
+        out_shape=[jax.ShapeDtypeStruct((slots, dsts), BF16)] * 3,
         in_specs=[pl.BlockSpec(memory_space=pltpu.SMEM), vmem, vmem],
-        out_specs=vmem,
+        out_specs=[vmem] * 3,
         scratch_shapes=[pltpu.VMEM((cells, LANES), F32)] * 8,
         compiler_params=pltpu.CompilerParams(vmem_limit_bytes=48 * 2 ** 20),
         name="build_adjacency",
     )(keys, lanes, weights.reshape(keys.shape))
 
 
-def dot(a, b, ca=1, cb=0, precision=None):
-    return lax.dot_general(a, b, (((ca,), (cb,)), ((), ())), precision=precision, preferred_element_type=F32)
+def exact3(sel, pieces, ca=1):
+    return dot(sel, pieces[2], ca) + dot(sel, pieces[1], ca) + dot(sel, pieces[0], ca)
+
+
+def full6(a, b):
+    low = dot(a[0], b[2]) + dot(a[2], b[0]) + dot(a[1], b[1])
+    return low + (dot(a[0], b[1]) + dot(a[1], b[0])) + dot(a[0], b[0])
+
+
+def wait_all(groups, buf, sem, whole):
+    part = buf if whole else buf.at[pl.ds(0, groups - 1)]
+    pltpu.make_async_copy(part, part, sem).wait()
+
+
+def send_all(groups, me, items):
+    def send(i, carry):
+        peer = jnp.bitwise_xor(me, i)
+        for kind, src, dst, send_sem, recv_sem in items:
+            pltpu.make_async_remote_copy(
+                src_ref=src.at[peer] if kind == "a" else src,
+                dst_ref=dst.at[me],
+                send_sem=send_sem,
+                recv_sem=recv_sem,
+                device_id=(0, peer),
+                device_id_type=MESH,
+            ).start()
+        return carry
+
+    lax.fori_loop(1, groups, send, 0)
+    for kind, src, dst, _, recv_sem in items:
+        pltpu.make_async_copy(src.at[me] if kind == "a" else src, dst.at[me], recv_sem).start()
+
+
+def main_kernel(groups, own, halo, hubs, hi_ref, mid_ref, low_ref, zt_ref, d_ref, pick_ref, sel_ref, plain_ref, b1_ref,
+                w1_ref, w2_ref, x_ref, home_x_ref,
+                dx_ref, gw1_ref, gw2_ref, bias_ref,
+                s1, s2, s3, s4, s5, s6, s7, s8, r1, r2, r3, r4, r5, r6, r7, pre_ref, g2_ref, g1_ref, dy_ref, *sems):
+    snd, rcv = sems[:8], sems[8:]
+    adj = (hi_ref, mid_ref, low_ref)
+    per = hubs // groups
+    hid = b1_ref.shape[1]
+    first_hub = own + halo
+    me = lax.axis_index("graph")
+    barrier = pltpu.get_barrier_semaphore()
+
+    def greet(i, carry):
+        pl.semaphore_signal(barrier, inc=1, device_id=(0, jnp.bitwise_xor(me, i)), device_id_type=MESH)
+        return carry
+
+    lax.fori_loop(1, groups, greet, 0)
+    lane = lax.broadcasted_iota(jnp.int32, (1, LANES), 1)
+    half = lane < LANES // 2
+
+    def forward(cols):
+        zt = zt_ref[...]
+        return dot(zt, low_ref[:, cols]) + dot(zt, mid_ref[:, cols]) + dot(zt, hi_ref[:, cols])
+
+    dh, dm, dl = split3(d_ref[...])
+    d_two = (dh.astype(F32) + pltpu.roll(dm.astype(F32), LANES // 2, 1)).astype(BF16)
+    d_four = jnp.concatenate([d_two, dl], axis=1)
+
+    def grad_out_sums(rows):
+        a = dot(hi_ref[rows, :], d_four)
+        t = a[:, :LANES] + a[:, LANES:] + dot(mid_ref[rows, :], d_two) + dot(low_ref[rows, :], dh)
+        return jnp.where(half, t + pltpu.roll(t, LANES // 2, 1), 0.0)
+
+    y_hub = forward(slice(own, own + hubs)).T
+    s1[:, :, LANES:] = y_hub.reshape(groups, per, hid)
+    g2_halo = grad_out_sums(slice(own, first_hub))
+    g2_hub = grad_out_sums(slice(first_hub, first_hub + hubs))
+    s1[:, :, :LANES] = (g2_halo + pltpu.roll(g2_hub, LANES // 2, 1)).reshape(groups, per, LANES)
+    pl.semaphore_wait(barrier, groups - 1)
+    send_all(groups, me, [("a", s1, r1, snd[0], rcv[0])])
+
+    b1 = b1_ref[...]
+    plain = plain_ref[...] > 0
+    pre_ref[...] = forward(slice(0, own)).T + b1
+    g2_ref[...] = grad_out_sums(slice(0, own))
+    wait_all(groups, r1, rcv[0], True)
+    home = r1[...].sum(axis=0)
+    pad = jnp.zeros((8 - per, LANES), F32)
+    home_g = jnp.where(half, pltpu.roll(jnp.concatenate([home[:, :LANES], pad], axis=0), LANES // 2, 1), 0.0)
+    home_pre = jnp.concatenate([home[:, LANES:] + b1, jnp.zeros((8 - per, hid), F32)], axis=0)
+    home_dz2 = home_g.astype(BF16)
+    w2 = w2_ref[...]
+    home_dy = jnp.where(home_pre > 0, dot(home_dz2, w2, 1, 1), 0.0)
+    s2[...] = home_dy[:per]
+    send_all(groups, me, [("b", s2, r2, snd[1], rcv[1])])
+
+    back = jnp.where(half, r1[:, :, :LANES].reshape(halo, LANES), 0.0)
+    dz2 = (g2_ref[...] + exact3(pick_ref[...], split3(back))).astype(BF16)
+    pre = pre_ref[...]
+    dy1 = jnp.where(plain & (pre > 0), dot(dz2, w2, 1, 1), 0.0)
+    hidden = jnp.where(plain, jax.nn.relu(pre), 0.0).astype(BF16)
+    home_hidden = jax.nn.relu(home_pre).astype(BF16)
+    gw2 = dot(hidden, dz2, 0, 0) + dot(home_hidden, home_dz2, 0, 0)
+    s3[...] = gw2.reshape(groups, per, LANES)
+    s4[:, :hid] = dy1.sum(axis=0, keepdims=True) + home_dy.sum(axis=0, keepdims=True)
+    s4[:, hid:] = d_ref[:own, :].sum(axis=0, keepdims=True)
+    send_all(groups, me, [("a", s3, r3, snd[2], rcv[2]), ("b", s4, r4, snd[3], rcv[3])])
+    for ref, piece in zip(range(3), split3(dy1)):
+        dy_ref[ref, :own, :] = piece
+    chunk = 256
+
+    def own_part(i, carry):
+        rows = pl.ds(pl.multiple_of(i * chunk, chunk), chunk)
+        g1_ref[rows, :] = full6([a[rows, :own] for a in adj], [dy_ref[p, :own, :] for p in range(3)])
+        return carry
+
+    lax.fori_loop(0, (first_hub + hubs) // chunk, own_part, 0)
+    wait_all(groups, r2, rcv[1], True)
+    for ref, piece in zip(range(3), split3(r2[...].reshape(hubs, hid))):
+        dy_ref[ref, own:, :] = piece
+
+    def hub_part(rows):
+        return g1_ref[rows, :] + full6([a[rows, own:] for a in adj], [dy_ref[p, own:, :] for p in range(3)])
+
+    s5[:, :per, :] = hub_part(slice(own, first_hub)).reshape(groups, per, hid)
+    s5[:, per:, :] = hub_part(slice(first_hub, first_hub + hubs)).reshape(groups, per, hid)
+    send_all(groups, me, [("a", s5, r5, snd[4], rcv[4])])
+
+    g1_ref[:chunk, :] = hub_part(slice(0, chunk))
+    g1_ref[chunk:own, :] = hub_part(slice(chunk, own))
+    wait_all(groups, r3, rcv[2], True)
+    wait_all(groups, r4, rcv[3], True)
+    bias_ref[...] = r4[...].sum(axis=0)
+    s7[per:, :] = r3[...].sum(axis=0)
+    wait_all(groups, r5, rcv[4], True)
+    home_dz1 = jnp.concatenate([r5[:, per:, :].sum(axis=0), jnp.zeros((8 - per, hid), F32)], axis=0).astype(BF16)
+    w1 = w1_ref[...]
+    s7[:per, :] = dot(home_dz1, w1, 1, 1)[:per]
+    back = r5[:, :per, :].reshape(halo, hid)
+    dz1 = g1_ref[:own, :] + exact3(pick_ref[...], split3(back))
+    dz1 = jnp.where(plain, dz1, 0.0).astype(BF16)
+    gw1 = dot(dz1, x_ref[...], 0, 0) + dot(home_dz1, home_x_ref[...], 0, 0)
+    s6[...] = gw1.reshape(groups, per, LANES)
+    send_all(groups, me, [("a", s6, r6, snd[5], rcv[5]), ("b", s7, r7, snd[6], rcv[6])])
+
+    dx = dot(dz1, w1, 1, 1)
+    wait_all(groups, r6, rcv[5], True)
+    s8[...] = r6[...].sum(axis=0)
+    send_all(groups, me, [("b", s8, gw1_ref, snd[7], rcv[7])])
+
+    wait_all(groups, r7, rcv[6], True)
+    gw2_ref[...] = r7[:, per:, :]
+    dx_ref[...] = dx + exact3(sel_ref[...], split3(r7[:, :per, :].reshape(hubs, LANES)))
+    for buf, sem in zip((r1, r2, r3, r4, r5, r6, r7, gw1_ref), snd):
+        wait_all(groups, buf, sem, False)
+    wait_all(groups, gw1_ref, rcv[7], True)
+
+
+def main_call(groups, own, halo, hubs, *args):
+    hid = args[8].shape[1]
+    per = hubs // groups
+    vmem = pl.BlockSpec(memory_space=pltpu.VMEM)
+    blocks = [(per, LANES + hid), (per, hid), (per, LANES), (1, hid + LANES), (2 * per, hid), (per, LANES), (2 * per, LANES), (per, LANES)]
+    kinds = "ababaabb"
+    sends = [pltpu.VMEM(((groups,) if k == "a" else ()) + b, F32) for k, b in zip(kinds, blocks)]
+    recvs = [pltpu.VMEM((groups,) + b, F32) for b in blocks[:-1]]
+    return pl.pallas_call(
+        functools.partial(main_kernel, groups, own, halo, hubs),
+        out_shape=[
+            jax.ShapeDtypeStruct((own, LANES), F32),
+            jax.ShapeDtypeStruct((groups, per, LANES), F32),
+            jax.ShapeDtypeStruct((groups, per, LANES), F32),
+            jax.ShapeDtypeStruct((1, hid + LANES), F32),
+        ],
+        in_specs=[vmem] * len(args),
+        out_specs=[vmem] * 4,
+        scratch_shapes=sends + recvs + [
+            pltpu.VMEM((own, hid), F32),
+            pltpu.VMEM((own, LANES), F32),
+            pltpu.VMEM((own + halo + hubs, hid), F32),
+            pltpu.VMEM((3, own + hubs, hid), BF16),
+        ] + [pltpu.SemaphoreType.DMA] * 16,
+        compiler_params=pltpu.CompilerParams(collective_id=2, has_side_effects=True, vmem_limit_bytes=56 * 2 ** 20),
+        name="main_exchange",
+    )(*args)
 
 
 def pad_cols(a):
@@ -183,7 +371,6 @@
         hub_f = is_hub.astype(F32)
         hub_b = is_hub.astype(BF16)
         pick_b = (send[:, None] == own_iota[None, :]).astype(BF16)
-        pick_f = pick_b.astype(F32)
         plain = (code == 0)[:, None]
 
         x_pad = jnp.concatenate([x, code[:, None].astype(BF16), jnp.zeros((own, LANES - feat_in - 1), BF16)], axis=1)
@@ -210,51 +397,19 @@
 
         w1_pad = jnp.pad(w_first, ((0, LANES - feat_in), (0, 0)))
         w2_pad = pad_cols(w_second)
-        z = dot(jnp.concatenate([x_pad, halo_x, hub_x], axis=0), w1_pad).astype(BF16)
-        y = dot(adj, z.astype(F32), 0, 0, precision=HI)
-        g2 = dot(adj, jnp.concatenate([dy_pad, hub_d], axis=0), precision=HI)
-        msg = jnp.concatenate([
-            g2[own:own + halo].reshape(groups, -1, LANES),
-            y[own:].reshape(groups, -1, LANES),
-            g2[own + halo:].reshape(groups, -1, LANES),
-        ], axis=1)
-        (got,) = exchange(groups, "a", [msg], 2)
-        per = hubs // groups
-        back = got[:, :per].reshape(halo, LANES)
-        dz2_own = g2[:own] + dot(pick_f, back, 0, 0, precision=HI)
-        home = got[:, per:].sum(axis=0)
-        y_rows = per * hid // LANES
-        pre = jnp.concatenate([y[:own], home[:y_rows].reshape(per, hid)], axis=0) + b_first
-        dz2 = jnp.concatenate([dz2_own, home[y_rows:]], axis=0).astype(BF16)
-        keep = jnp.concatenate([plain, jnp.ones((per, 1), bool)], axis=0)
-        hidden = jnp.where(keep, jax.nn.relu(pre), 0.0).astype(BF16)
-        gw2 = dot(hidden, dz2, 0, 0)
-        dh1 = dot(dz2, w2_pad, 1, 1)
-        dy1 = jnp.where(keep & (pre > 0), dh1, 0.0)
-        bias = jnp.concatenate([dy1.sum(axis=0), dy_pad.sum(axis=0)]).reshape(-1, LANES)
-        hub_y, gw2, bias = exchange(
-            groups, "bab", [dy1[own:].reshape(-1, LANES), gw2.reshape(groups, -1, LANES), bias], 3)
-        bias = bias.sum(axis=0)
-        g1 = dot(adj, jnp.concatenate([dy1[:own], hub_y.reshape(hubs, hid)], axis=0), precision=HI)
-        msg = jnp.concatenate([
-            g1[own:own + halo].reshape(groups, -1, LANES), g1[own + halo:].reshape(groups, -1, LANES)], axis=1)
-        (got,) = exchange(groups, "a", [msg], 4)
-        back = got[:, :y_rows].reshape(halo, hid)
-        dz1_own = (g1[:own] + dot(pick_f, back, 0, 0, precision=HI)).astype(BF16)
-        dz1_home = got[:, y_rows:].sum(axis=0).reshape(per, hid).astype(BF16)
-        dz1 = jnp.concatenate([jnp.where(plain, dz1_own, jnp.zeros((), BF16)), dz1_home], axis=0)
-        gw1 = dot(dz1, jnp.concatenate([x_pad, home_x], axis=0), 0, 0)
-        dx = dot(dz1, w1_pad, 1, 1)
-        gw1, hub_dx, gw2 = exchange(
-            groups, "abb", [gw1.reshape(groups, -1, LANES), dx[own:], gw2.sum(axis=0)], 5)
-        (gw1,) = exchange(groups, "b", [gw1.sum(axis=0)], 6)
-        dx = jnp.where(plain, dx[:own], dot(hub_f, hub_dx.reshape(hubs, LANES), 0, 0, precision=HI))
+        zt = dot(w1_pad, jnp.concatenate([x_pad, halo_x, hub_x], axis=0), 0, 1).astype(BF16)
+        d_ext = jnp.concatenate([dy_pad, hub_d], axis=0)
+        pick_t = (own_iota[:, None] == send[None, :]).astype(BF16)
+        sel_t = (own_iota[:, None] == (hub_ids - me * own)[None, :]).astype(BF16)
+        dx, gw1, gw2, bias = main_call(
+            groups, own, halo, hubs, *adj, zt, d_ext, pick_t, sel_t, plain.astype(jnp.int32), b_first[None, :],
+            w1_pad, w2_pad, x_pad, jnp.pad(home_x, ((0, 8 - home_x.shape[0]), (0, 0))))
         return (
             dx[:, :feat_in],
             gw1.reshape(hid, LANES)[:, :feat_in].T,
             gw2.reshape(hid, LANES)[:, :feat_out],
-            bias[:hid // LANES].reshape(-1),
-            bias[-1, :feat_out],
+            bias[0, :hid],
+            bias[0, hid:hid + feat_out],
         )
 
     rows, flat = P(("data", "graph"), None), P(("data", "graph"))

time: 246 us -> 190 us (0.77)
  Pallas kernels: 184 us -> 156 us
  matrix products: 25.1 us -> 5.02 us
  other arithmetic: 15.7 us -> 9.53 us
    pallas_call x7 -> x2, Pallas kernels: 123 us -> 36.7 us  [exchange(): pl.pallas_call(functools.partial(exchange_kernel, groups, kinds), out_sha...]
    pallas_call x1 -> x2, Pallas kernels: 56.3 us -> 115 us  [the longest x1 63.2 us: main_call(): pl.pallas_call(functools.partial(main_kernel, groups, own, halo, hubs), o...]
    dot_general x14 -> x4, matrix products: 25.1 us -> 5.02 us  [dot(): lax.dot_general(a, b, (((ca,), (cb,)), ((), ())), precision=precision, pr...]
    reduce_sum x5 -> x0, other arithmetic: 6.59 us -> none  [the longest x1 1.7 us: device_step(): gw2.sum(axis=0)]
    unnamed x33 -> x28, local copies, waits for them, and re-layouts: 5.95 us -> 12.4 us
    reshape x11 -> x0, local copies, waits for them, and re-layouts: 6.33 us -> none  [the longest x2 1.94 us: device_step(): hub_x, hub_d = (hub_x.reshape(hubs, LANES), hub_d.reshape(hubs, LANES))]
    slice x11 -> x1, local copies, waits for them, and re-layouts: 5.45 us -> 1.23 us  [device_step(): bias[0, :hid]]
    pad x0 -> x4, local copies, waits for them, and re-layouts: none -> 2.67 us  [the longest x1 1.43 us: device_step(): w1_pad = jnp.pad(w_first, ((0, LANES - feat_in), (0, 0)))]
where the time goes in v2:
time: 190 us
  Pallas kernels  156 us (82%)
  local copies, waits for them, and re-layouts  18.4 us (10%)
  other arithmetic  9.53 us (5%)
  matrix products  5.02 us (3%)
    pallas_call x1, Pallas kernels, main_call(): pl.pallas_call(functools.partial(main_kernel, groups, own, halo, hubs), o...  63.2 us
    pallas_call x1, Pallas kernels, build_adjacency(): pl.pallas_call(functools.partial(build_kernel, slots, dsts), out_shape=[j...  51.5 us
    pallas_call x2, Pallas kernels, exchange(): pl.pallas_call(functools.partial(exchange_kernel, groups, kinds), out_sha...  36.7 us
    unnamed x28, local copies, waits for them, and re-layouts  12.4 us
    dot_general x4, matrix products, dot(): lax.dot_general(a, b, (((ca,), (cb,)), ((), ())), precision=precision, pr...  5.02 us
    pallas_call x1, Pallas kernels, edge_keys(): pl.pallas_call(functools.partial(keys_kernel, own), out_shape=(shape, sha...  4.44 us

profile of v2, /device:TPU:1, one launch (start us, length us, event | category | flops | bytes accessed | tf_op | source)
XLA Modules:
  0.0 189.6 jit_solution(14586600246087317588)
XLA Ops:
  3.0 1.4 pad.17.w1_ref
  4.6 1.0 copy.29
  5.8 0.9 convolution_convert_fusion.1
  6.8 0.9 convolution_convert_fusion.2
  8.7 1.1 fusion
  9.8 21.5 %exchange_0.1 = (bf16[128,2,128]{2,1,0:T(2,128)(2,1)}, bf16[128,2,128]{2,1,0:T(2,128)(2,1)}, f32[128,2,128]{2,1,0:T(2,128)}) custom-call(bf16[128,2,128]{2,1,0:T(2,128)(2,1)} %bitcast.37, bf16[128,2,128]{2,1,0:T(2,128)(2,1)} %bitcast.36, f32[128,2,128]{2,1,0:T(2,128)} %bitcast.25), custom_call_target="tpu_custom_call" | custom-call | tf_op jit(solution)/shard_map/exchange_0/pallas_call | solution.py:63
  31.3 1.0 reduce_sum.31.refs_0_
  32.3 1.1 fusion.16
  33.4 1.0 fusion.15
  34.4 1.6 reduce_sum.32.refs_1_
  37.2 15.2 %exchange_1.1 = (bf16[128,2,128]{2,1,0:T(2,128)(2,1)}, f32[128,2,128]{2,1,0:T(2,128)}) custom-call(bf16[2,128]{1,0:T(2,128)(2,1)} %copy-done.9, f32[2,128]{1,0:T(2,128)} %reduce_sum.32.refs_1_), custom_call_target="tpu_custom_call" | custom-call | tf_op jit(solution)/shard_map/exchange_1/pallas_call | solution.py:63
  52.4 2.1 %convolution_convert_fusion.zt_ref = bf16[256,1024]{1,0:T(8,128)(2,1)} fusion(bf16[256,128]{1,0:T(8,128)(2,1)} %bitcast.41, bf16[256,128]{1,0:T(8,128)(2,1)} %bitcast.29, bf16[512,27]{1,0:T(8,128)(2,1)S(1)} %broadcast_in_dim.18, bf16[512,1]{1,0:T(8,128)(2,1)S(1)} %convert_element_type.62, bf16[512,100]{1,0:T(8,128)(2,1)S(1)} %copy.29, ...), kind=kOutput, calls=%fused_computation | convolution fusion | flops 68681728 | bytes 837632 | tf_op jit(solution)/shard_map/dot_general | solution.py:18
  54.6 1.7 pad_maximum_fusion.d_ref
  56.2 4.4 %edge_keys.1 = (s32[256,128]{1,0:T(8,128)}, s32[256,128]{1,0:T(8,128)}) custom-call(s32[256,128]{1,0:T(8,128)} %bitcast.30, s32[256,128]{1,0:T(8,128)} %bitcast.31, s32[10,128]{1,0:T(8,128)} %add_bitcast_fusion.tab_ref), custom_call_target="tpu_custom_call" | custom-call | tf_op jit(solution)/shard_map/edge_keys/pallas_call | solution.py:110
  64.0 51.5 %build_adjacency.1 = (bf16[1024,768]{1,0:T(8,128)(2,1)S(1)}, bf16[1024,768]{1,0:T(8,128)(2,1)S(1)}, bf16[1024,768]{1,0:T(8,128)(2,1)S(1)}) custom-call(s32[256,128]{1,0:T(8,128)S(1)} %copy-done.4, s32[256,128]{1,0:T(8,128)S(1)} %copy-done.5, f32[256,128]{1,0:T(8,128)S(1)} %bitcast.24), custom_call_target="tpu_custom_call" | custom-call | tf_op jit(solution)/shard_map/build_adjacency/pallas_call | solution.py:163
  115.5 1.2 copy-done
  116.7 1.2 copy-done.1
  117.8 1.1 copy-done.2
  119.0 63.2 %main_exchange.1 = (f32[512,128]{1,0:T(8,128)}, f32[128,2,128]{2,1,0:T(2,128)}, f32[128,2,128]{2,1,0:T(2,128)}, f32[1,384]{1,0:T(1,128)}) custom-call(bf16[1024,768]{1,0:T(8,128)(2,1)} %copy-done, bf16[1024,768]{1,0:T(8,128)(2,1)} %copy-done.1, bf16[1024,768]{1,0:T(8,128)(2,1)} %copy-done.2, bf16[256,1024]{1,0:T(8,128)(2,1)} %convolution_convert_fusion.zt_ref, ...), custom_call_target="tpu_custom_call" | custom-call | tf_op jit(solution)/shard_map/main_exchange/pallas_call | solution.py:333
  182.2 1.8 copy.36
  184.0 1.7 copy.37
  185.6 1.1 slice_bitcast_fusion
  186.7 1.2 slice.22
  188.0 1.6 copy.38
  (36 shorter events, 8.3 us)
Async XLA Ops:
  0.6 6.1 %copy-start.10 = (s32[256]{0:T(256)S(1)}, s32[256]{0:T(256)}, u32[]{:S(2)}) copy-start(s32[256]{0:T(256)} %param.14) | copy-start | bytes 3076
  0.6 7.9 %copy-start.7 = (f32[512,47]{0,1:T(8,128)S(1)}, f32[512,47]{0,1:T(8,128)}, u32[]{:S(2)}) copy-start(f32[512,47]{0,1:T(8,128)} %param.19) | copy-start | bytes 288772
  5.7 46.8 %copy-start.8 = (bf16[100,256]{1,0:T(8,128)(2,1)S(1)}, bf16[100,256]{1,0:T(8,128)(2,1)}, u32[]{:S(2)}) copy-start(bf16[100,256]{1,0:T(8,128)(2,1)} %param.16) | copy-start | bytes 153604
  5.8 48.7 %copy-start.6 = (bf16[512,128]{1,0:T(8,128)(2,1)}, bf16[512,128]{1,0:T(8,128)(2,1)S(1)}, u32[]{:S(2)}) copy-start(bf16[512,128]{1,0:T(8,128)(2,1)S(1)} %pad_maximum_fusion.1.x_ref) | copy-start | bytes 393220
  32.3 4.9 %copy-start.9 = (bf16[2,128]{1,0:T(2,128)(2,1)}, bf16[2,128]{1,0:T(2,128)(2,1)S(1)}, u32[]{:S(2)}) copy-start(bf16[2,128]{1,0:T(2,128)(2,1)S(1)} %reduce_sum.31.refs_0_) | copy-start | bytes 1540
  32.3 29.9 %copy-start.3 = (f32[32768]{0:T(1024)S(1)}, f32[32768]{0:T(1024)}, u32[]{:S(2)}) copy-start(f32[32768]{0:T(1024)} %param.13) | copy-start | bytes 393220
  62.2 0.9 copy-start.4
  63.1 0.9 copy-start.5
  115.5 1.2 copy-start
  116.7 1.2 copy-start.1
  117.8 1.2 copy-start.2

commit v3 on v2

v3 whole, which is shorter than its diff:
```python
import functools

import jax
import jax.numpy as jnp
from jax import lax
from jax.experimental import pallas as pl
from jax.experimental.pallas import tpu as pltpu
from jax.sharding import PartitionSpec as P

BF16 = jnp.bfloat16
F32 = jnp.float32
HI = lax.Precision.HIGHEST
LANES = 128
MESH = pl.DeviceIdType.MESH


def dot(a, b, ca=1, cb=0, precision=None):
    return lax.dot_general(a, b, (((ca,), (cb,)), ((), ())), precision=precision, preferred_element_type=F32)


def split3(a):
    hi = a.astype(BF16)
    rest = a - hi.astype(F32)
    mid = rest.astype(BF16)
    return hi, mid, (rest - mid.astype(F32)).astype(BF16)


def exact3(sel, pieces, ca=1):
    return dot(sel, pieces[2], ca) + dot(sel, pieces[1], ca) + dot(sel, pieces[0], ca)


def full6(a, b):
    low = dot(a[0], b[2]) + dot(a[2], b[0]) + dot(a[1], b[1])
    return low + (dot(a[0], b[1]) + dot(a[1], b[0])) + dot(a[0], b[0])


def wait_all(groups, buf, sem, whole):
    part = buf if whole else buf.at[pl.ds(0, groups - 1)]
    pltpu.make_async_copy(part, part, sem).wait()


def send_all(groups, me, items):
    def send(i, carry):
        peer = jnp.bitwise_xor(me, i)
        for kind, src, dst, send_sem, recv_sem in items:
            pltpu.make_async_remote_copy(
                src_ref=src.at[peer] if kind == "a" else src,
                dst_ref=dst.at[me],
                send_sem=send_sem,
                recv_sem=recv_sem,
                device_id=(0, peer),
                device_id_type=MESH,
            ).start()
        return carry

    lax.fori_loop(1, groups, send, 0)
    for kind, src, dst, _, recv_sem in items:
        pltpu.make_async_copy(src.at[me] if kind == "a" else src, dst.at[me], recv_sem).start()


def greet_all(groups, me):
    barrier = pltpu.get_barrier_semaphore()

    def greet(i, carry):
        pl.semaphore_signal(barrier, inc=1, device_id=(0, jnp.bitwise_xor(me, i)), device_id_type=MESH)
        return carry

    lax.fori_loop(1, groups, greet, 0)
    return barrier


def padded(ref, rows, cols):
    a = ref[...]
    if cols > a.shape[1]:
        a = jnp.concatenate([a, jnp.zeros((a.shape[0], cols - a.shape[1]), a.dtype)], axis=1)
    if rows > a.shape[0]:
        a = jnp.concatenate([a, jnp.zeros((rows - a.shape[0], cols), a.dtype)], axis=0)
    return a


def rows_to_blocks(a, groups):
    return a.reshape(groups, a.shape[0] // groups, a.shape[1])


SRC_BLOCK, DST_BLOCK = 128, 256
BUCKET = SRC_BLOCK * DST_BLOCK


def first_kernel(groups, own, halo, hubs, x_ref, dy_ref, send_ref, hub_ref, w1_ref, dst_ref, src_ref,
                 key_ref, bound_ref, zt_ref, d_ref, xp_ref, home_ref,
                 sx, sd, hx, hd, rx, rd, gx, gd, *sems):
    snd, rcv = sems[:4], sems[4:]
    per = hubs // groups
    feat_in = x_ref.shape[1]
    me = lax.axis_index("graph")
    barrier = greet_all(groups, me)
    lane = lax.broadcasted_iota(jnp.int32, (1, LANES), 1)
    own_row = lax.broadcasted_iota(jnp.int32, (own, 1), 0)
    pick_t = (own_row == send_ref[...]).astype(F32).astype(BF16)
    is_hub = own_row == hub_ref[...] - me * own
    sel_t = is_hub.astype(F32).astype(BF16)
    number = lax.broadcasted_iota(jnp.int32, (1, hubs), 1) + 1
    code = jnp.sum(jnp.where(is_hub, number, 0).astype(F32), axis=1, keepdims=True)
    x = padded(x_ref, own, LANES)
    x = jnp.where(lane == feat_in, code, x.astype(F32)).astype(BF16)
    xp_ref[...] = x
    dy = padded(dy_ref, own, LANES)
    d_ref[:own, :] = dy
    picked = dot(jnp.concatenate([pick_t, sel_t], axis=1), jnp.concatenate((x,) + split3(dy), axis=1), 0, 0)
    hub_d = picked[halo:, 3 * LANES:] + picked[halo:, 2 * LANES:3 * LANES] + picked[halo:, LANES:2 * LANES]
    sx[:, :per, :] = rows_to_blocks(picked[:halo, :LANES], groups).astype(BF16)
    sx[:, per:, :] = rows_to_blocks(picked[halo:, :LANES], groups).astype(BF16)
    sd[...] = rows_to_blocks(hub_d, groups)
    pl.semaphore_wait(barrier, groups - 1)
    send_all(groups, me, [("a", sx, rx, snd[0], rcv[0]), ("a", sd, rd, snd[1], rcv[1])])

    numbers = jnp.broadcast_to(number.astype(F32), (8, hubs)).astype(BF16)
    code_row = dot(numbers, sel_t, 1, 1)[:1].astype(jnp.int32)
    w1_t = padded(w1_ref, LANES, w1_ref.shape[1]).T
    zt_ref[:, :own] = dot(w1_t, x, 1, 1).astype(BF16)
    wait_all(groups, rx, rcv[0], True)
    wait_all(groups, rd, rcv[1], True)
    got = rx[...].astype(F32)
    home_x = got[:, per:, :].sum(axis=0)
    hx[...] = home_x.astype(BF16)
    hd[...] = rd[...].sum(axis=0)
    send_all(groups, me, [("b", hx, gx, snd[2], rcv[2]), ("b", hd, gd, snd[3], rcv[3])])

    home_ref[...] = jnp.concatenate([home_x, jnp.zeros((8 - per, LANES), F32)], axis=0).astype(BF16)
    halo_x = got[:, :per, :].reshape(halo, LANES).astype(BF16)
    zt_ref[:, own:own + halo] = dot(w1_t, halo_x, 1, 1).astype(BF16)
    column = jnp.broadcast_to(jnp.where(lane == feat_in, 1.0, 0.0), (8, LANES)).astype(BF16)
    halo_code = dot(column, halo_x, 1, 1)[:1].astype(jnp.int32)
    hub_base = own + halo - 1
    own_ids = lax.broadcasted_iota(jnp.int32, (1, own), 1)
    halo_ids = lax.broadcasted_iota(jnp.int32, (1, halo), 1) + own
    dst_table = jnp.where(code_row > 0, own - 1 + code_row, own_ids)
    src_table = jnp.concatenate([
        jnp.where(code_row > 0, hub_base + code_row, own_ids),
        jnp.where(halo_code > 0, hub_base + halo_code, halo_ids)], axis=1)
    block = 32
    steps = dst_ref.shape[0] // block
    tops = (own + hubs) // DST_BLOCK
    buckets = (own + halo + hubs) // SRC_BLOCK * tops

    def rename(ids, table):
        at = jnp.bitwise_and(ids, LANES - 1)
        top = jnp.right_shift(ids, 7)
        out = ids
        for t in range(table.shape[1] // LANES):
            row = jnp.broadcast_to(table[:, t * LANES:(t + 1) * LANES], ids.shape)
            out = jnp.where(top == t, jnp.take_along_axis(row, at, axis=1), out)
        return out

    def keys(i, carry):
        rows = pl.ds(pl.multiple_of(i * block, block), block)
        dst = rename(dst_ref[rows, :], dst_table)
        src = rename(src_ref[rows, :], src_table)
        bucket = jnp.right_shift(src, 7) * tops + jnp.right_shift(dst, 8)
        key = bucket * BUCKET + jnp.bitwise_and(src, SRC_BLOCK - 1) * DST_BLOCK + jnp.bitwise_and(dst, DST_BLOCK - 1)
        key_ref[rows, :] = key
        return tuple(
            c + jnp.sum(jnp.where(bucket < b, 1, 0).reshape(block // 8, 8, LANES), axis=0) for b, c in enumerate(carry))

    counts = lax.fori_loop(0, steps, keys, tuple(jnp.zeros((8, LANES), jnp.int32) for _ in range(buckets + 1)))
    bounds = jnp.zeros((8, LANES), F32)
    for b, c in enumerate(counts):
        total = jnp.sum(jnp.sum(c.astype(F32), axis=0, keepdims=True), axis=1, keepdims=True)
        bounds = jnp.where(lane == b, total, bounds)
    bound_ref[...] = bounds.astype(jnp.int32)
    wait_all(groups, gx, rcv[2], True)
    wait_all(groups, gd, rcv[3], True)
    hub_x = gx[...].astype(F32).reshape(hubs, LANES).astype(BF16)
    zt_ref[:, own + halo:] = dot(w1_t, hub_x, 1, 1).astype(BF16)
    d_ref[own:, :] = gd[...].reshape(hubs, LANES)
    for buf, sem in zip((rx, rd, gx, gd), snd):
        wait_all(groups, buf, sem, False)


def first_call(groups, own, halo, hubs, hid, *args):
    per = hubs // groups
    edge_rows = args[-1].shape[0]
    vmem = pl.BlockSpec(memory_space=pltpu.VMEM)
    shape = jax.ShapeDtypeStruct
    return pl.pallas_call(
        functools.partial(first_kernel, groups, own, halo, hubs),
        out_shape=[
            shape((edge_rows, LANES), jnp.int32),
            shape((8, LANES), jnp.int32),
            shape((hid, own + halo + hubs), BF16),
            shape((own + hubs, LANES), F32),
            shape((own, LANES), BF16),
            shape((8, LANES), BF16),
        ],
        in_specs=[vmem] * len(args),
        out_specs=[vmem] * 6,
        scratch_shapes=[
            pltpu.VMEM((groups, 2 * per, LANES), BF16),
            pltpu.VMEM((groups, per, LANES), F32),
            pltpu.VMEM((per, LANES), BF16),
            pltpu.VMEM((per, LANES), F32),
            pltpu.VMEM((groups, 2 * per, LANES), BF16),
            pltpu.VMEM((groups, per, LANES), F32),
            pltpu.VMEM((groups, per, LANES), BF16),
            pltpu.VMEM((groups, per, LANES), F32),
        ] + [pltpu.SemaphoreType.DMA] * 8,
        compiler_params=pltpu.CompilerParams(collective_id=0, has_side_effects=True),
        name="first_exchange",
    )(*args)


CHUNK_ROWS, UNROLL = 2, 8


def adjacency_kernel(slots, dsts, bound_ref, key_ref, w_ref, hi_ref, mid_ref, low_ref, acc_ref, pair_ref):
    tops = dsts // DST_BLOCK
    buckets = slots // SRC_BLOCK * tops
    size = CHUNK_ROWS * LANES
    src_ids = lax.broadcasted_iota(jnp.int32, (SRC_BLOCK, LANES), 0).astype(F32).astype(BF16)
    dst_ids = lax.broadcasted_iota(jnp.int32, (DST_BLOCK, LANES), 0).astype(F32).astype(BF16)
    one, zero = jnp.ones((), BF16), jnp.zeros((), BF16)

    def clear(i, carry):
        acc_ref[pl.ds(pl.multiple_of(i * SRC_BLOCK, SRC_BLOCK), SRC_BLOCK), :] = jnp.zeros((SRC_BLOCK, DST_BLOCK), F32)
        return carry

    lax.fori_loop(0, buckets, clear, 0)

    def list_pairs(b, at):
        low, high = bound_ref[0, b], bound_ref[0, b + 1]
        start = low // size
        count = jnp.where(high > low, (high + size - 1) // size - start, 0)

        def put(i, carry):
            pair_ref[at + i] = b * 1024 + start + i
            return carry

        lax.fori_loop(0, count, put, 0)
        return at + count

    total = lax.fori_loop(0, buckets, list_pairs, 0)
    for i in range(UNROLL - 1):
        pair_ref[total + i] = buckets * 1024

    def step(it, carry):
        work = []
        for u in range(UNROLL):
            pair = pair_ref[it * UNROLL + u]
            b, c = jnp.right_shift(pair, 10), jnp.bitwise_and(pair, 1023)
            lhs, rhs = [], []
            for r in range(CHUNK_ROWS):
                rel = key_ref[pl.ds(c * CHUNK_ROWS + r, 1), :] - b * BUCKET
                weight = w_ref[pl.ds(c * CHUNK_ROWS + r, 1), :]
                src = jnp.right_shift(rel, 8)
                src = jnp.where((src >= 0) & (src < SRC_BLOCK), src, 512).astype(F32).astype(BF16)
                dst = jnp.bitwise_and(rel, DST_BLOCK - 1).astype(F32).astype(BF16)
                hit = src_ids == jnp.broadcast_to(src, src_ids.shape)
                lhs.append(jnp.concatenate(
                    [jnp.where(hit, jnp.broadcast_to(p, src_ids.shape), zero) for p in split3(weight)], axis=0))
                rhs.append(jnp.where(dst_ids == jnp.broadcast_to(dst, dst_ids.shape), one, zero))
            work.append((b, jnp.concatenate(lhs, axis=1), jnp.concatenate(rhs, axis=1)))
        outs = [dot(lhs, rhs, 1, 1) for _, lhs, rhs in work]
        for (b, _, _), out in zip(work, outs):
            rows = pl.ds(pl.multiple_of(b * SRC_BLOCK, SRC_BLOCK), SRC_BLOCK)
            acc_ref[rows, :] += out[2 * SRC_BLOCK:] + out[SRC_BLOCK:2 * SRC_BLOCK] + out[:SRC_BLOCK]
        return carry

    lax.fori_loop(0, (total + UNROLL - 1) // UNROLL, step, 0)
    for b in range(buckets):
        rows = slice(b // tops * SRC_BLOCK, (b // tops + 1) * SRC_BLOCK)
        cols = slice(b % tops * DST_BLOCK, (b % tops + 1) * DST_BLOCK)
        for ref, piece in zip((hi_ref, mid_ref, low_ref), split3(acc_ref[b * SRC_BLOCK:(b + 1) * SRC_BLOCK, :])):
            ref[rows, cols] = piece


def adjacency(bounds, keys, weights, slots, dsts):
    edges = weights.shape[0]
    buckets = slots // SRC_BLOCK * (dsts // DST_BLOCK)
    vmem = pl.BlockSpec(memory_space=pltpu.VMEM)
    return pl.pallas_call(
        functools.partial(adjacency_kernel, slots, dsts),
        out_shape=[jax.ShapeDtypeStruct((slots, dsts), BF16)] * 3,
        in_specs=[pl.BlockSpec(memory_space=pltpu.SMEM), vmem, vmem],
        out_specs=[vmem] * 3,
        scratch_shapes=[
            pltpu.VMEM(((buckets + 1) * SRC_BLOCK, DST_BLOCK), F32),
            pltpu.SMEM((edges // (CHUNK_ROWS * LANES) + buckets + UNROLL,), jnp.int32),
        ],
        name="adjacency",
    )(bounds, keys.reshape(-1, LANES), weights.reshape(-1, LANES))


def main_kernel(groups, own, halo, hubs, hi_ref, mid_ref, low_ref, zt_ref, d_ref, send_ref, hub_ref, b1_ref,
                w1_ref, w2_ref, x_ref, home_x_ref,
                dx_ref, gw1_ref, gw2_ref, bias_ref,
                s1, s2, s3, s4, s5, s6, s7, s8, r1, r2, r3, r4, r5, r6, r7, pre_ref, g2_ref, g1_ref, dy_ref, *sems):
    snd, rcv = sems[:8], sems[8:]
    adj = (hi_ref, mid_ref, low_ref)
    per = hubs // groups
    hid = b1_ref.shape[1]
    first_hub = own + halo
    me = lax.axis_index("graph")
    barrier = greet_all(groups, me)
    lane = lax.broadcasted_iota(jnp.int32, (1, LANES), 1)
    half = lane < LANES // 2

    def forward(cols):
        zt = zt_ref[...]
        return dot(zt, low_ref[:, cols]) + dot(zt, mid_ref[:, cols]) + dot(zt, hi_ref[:, cols])

    dh, dm, dl = split3(d_ref[...])
    d_two = (dh.astype(F32) + pltpu.roll(dm.astype(F32), LANES // 2, 1)).astype(BF16)
    d_four = jnp.concatenate([d_two, dl], axis=1)

    def grad_out_sums(rows):
        a = dot(hi_ref[rows, :], d_four)
        t = a[:, :LANES] + a[:, LANES:] + dot(mid_ref[rows, :], d_two) + dot(low_ref[rows, :], dh)
        return jnp.where(half, t + pltpu.roll(t, LANES // 2, 1), 0.0)

    y_hub = forward(slice(own, own + hubs)).T
    s1[:, :, LANES:] = y_hub.reshape(groups, per, hid)
    g2_halo = grad_out_sums(slice(own, first_hub))
    g2_hub = grad_out_sums(slice(first_hub, first_hub + hubs))
    s1[:, :, :LANES] = (g2_halo + pltpu.roll(g2_hub, LANES // 2, 1)).reshape(groups, per, LANES)
    pl.semaphore_wait(barrier, groups - 1)
    send_all(groups, me, [("a", s1, r1, snd[0], rcv[0])])

    b1 = b1_ref[...]
    own_row = lax.broadcasted_iota(jnp.int32, (own, 1), 0)
    pick_t = (own_row == send_ref[...]).astype(F32).astype(BF16)
    sel_f = (own_row == hub_ref[...] - me * own).astype(F32)
    sel_t = sel_f.astype(BF16)
    plain = jnp.sum(sel_f, axis=1, keepdims=True) == 0
    pre_ref[...] = forward(slice(0, own)).T + b1
    g2_ref[...] = grad_out_sums(slice(0, own))
    wait_all(groups, r1, rcv[0], True)
    home = r1[...].sum(axis=0)
    pad = jnp.zeros((8 - per, LANES), F32)
    home_g = jnp.where(half, pltpu.roll(jnp.concatenate([home[:, :LANES], pad], axis=0), LANES // 2, 1), 0.0)
    home_pre = jnp.concatenate([home[:, LANES:] + b1, jnp.zeros((8 - per, hid), F32)], axis=0)
    home_dz2 = home_g.astype(BF16)
    w2 = padded(w2_ref, hid, LANES)
    home_dy = jnp.where(home_pre > 0, dot(home_dz2, w2, 1, 1), 0.0)
    s2[...] = home_dy[:per]
    send_all(groups, me, [("b", s2, r2, snd[1], rcv[1])])

    back = jnp.where(half, r1[:, :, :LANES].reshape(halo, LANES), 0.0)
    dz2 = (g2_ref[...] + exact3(pick_t, split3(back))).astype(BF16)
    pre = pre_ref[...]
    dy1 = jnp.where(plain & (pre > 0), dot(dz2, w2, 1, 1), 0.0)
    hidden = jnp.where(plain, jax.nn.relu(pre), 0.0).astype(BF16)
    home_hidden = jax.nn.relu(home_pre).astype(BF16)
    gw2 = dot(hidden, dz2, 0, 0) + dot(home_hidden, home_dz2, 0, 0)
    s3[...] = gw2.reshape(groups, per, LANES)
    s4[:, :hid] = dy1.sum(axis=0, keepdims=True) + home_dy.sum(axis=0, keepdims=True)
    s4[:, hid:] = d_ref[:own, :].sum(axis=0, keepdims=True)
    send_all(groups, me, [("a", s3, r3, snd[2], rcv[2]), ("b", s4, r4, snd[3], rcv[3])])
    for ref, piece in zip(range(3), split3(dy1)):
        dy_ref[ref, :own, :] = piece
    chunk = 256

    def own_part(i, carry):
        rows = pl.ds(pl.multiple_of(i * chunk, chunk), chunk)
        g1_ref[rows, :] = full6([a[rows, :own] for a in adj], [dy_ref[p, :own, :] for p in range(3)])
        return carry

    lax.fori_loop(0, (first_hub + hubs) // chunk, own_part, 0)
    wait_all(groups, r2, rcv[1], True)
    for ref, piece in zip(range(3), split3(r2[...].reshape(hubs, hid))):
        dy_ref[ref, own:, :] = piece

    def hub_part(rows):
        return g1_ref[rows, :] + full6([a[rows, own:] for a in adj], [dy_ref[p, own:, :] for p in range(3)])

    s5[:, :per, :] = hub_part(slice(own, first_hub)).reshape(groups, per, hid)
    s5[:, per:, :] = hub_part(slice(first_hub, first_hub + hubs)).reshape(groups, per, hid)
    send_all(groups, me, [("a", s5, r5, snd[4], rcv[4])])

    g1_ref[:chunk, :] = hub_part(slice(0, chunk))
    g1_ref[chunk:own, :] = hub_part(slice(chunk, own))
    wait_all(groups, r3, rcv[2], True)
    wait_all(groups, r4, rcv[3], True)
    bias_ref[...] = r4[...].sum(axis=0)
    s7[per:, :] = r3[...].sum(axis=0)
    wait_all(groups, r5, rcv[4], True)
    home_dz1 = jnp.concatenate([r5[:, per:, :].sum(axis=0), jnp.zeros((8 - per, hid), F32)], axis=0).astype(BF16)
    w1 = padded(w1_ref, LANES, hid)
    s7[:per, :] = dot(home_dz1, w1, 1, 1)[:per]
    back = r5[:, :per, :].reshape(halo, hid)
    dz1 = g1_ref[:own, :] + exact3(pick_t, split3(back))
    dz1 = jnp.where(plain, dz1, 0.0).astype(BF16)
    gw1 = dot(dz1, x_ref[...], 0, 0) + dot(home_dz1, home_x_ref[...], 0, 0)
    s6[...] = gw1.reshape(groups, per, LANES)
    send_all(groups, me, [("a", s6, r6, snd[5], rcv[5]), ("b", s7, r7, snd[6], rcv[6])])

    dx = dot(dz1, w1, 1, 1)
    wait_all(groups, r6, rcv[5], True)
    s8[...] = r6[...].sum(axis=0)
    send_all(groups, me, [("b", s8, gw1_ref, snd[7], rcv[7])])

    wait_all(groups, r7, rcv[6], True)
    gw2_ref[...] = r7[:, per:, :]
    dx_ref[...] = dx + exact3(sel_t, split3(r7[:, :per, :].reshape(hubs, LANES)))
    for buf, sem in zip((r1, r2, r3, r4, r5, r6, r7, gw1_ref), snd):
        wait_all(groups, buf, sem, False)
    wait_all(groups, gw1_ref, rcv[7], True)


def main_call(groups, own, halo, hubs, *args):
    hid = args[7].shape[1]
    per = hubs // groups
    vmem = pl.BlockSpec(memory_space=pltpu.VMEM)
    blocks = [(per, LANES + hid), (per, hid), (per, LANES), (1, hid + LANES), (2 * per, hid), (per, LANES), (2 * per, LANES), (per, LANES)]
    kinds = "ababaabb"
    sends = [pltpu.VMEM(((groups,) if k == "a" else ()) + b, F32) for k, b in zip(kinds, blocks)]
    recvs = [pltpu.VMEM((groups,) + b, F32) for b in blocks[:-1]]
    return pl.pallas_call(
        functools.partial(main_kernel, groups, own, halo, hubs),
        out_shape=[
            jax.ShapeDtypeStruct((own, LANES), F32),
            jax.ShapeDtypeStruct((groups, per, LANES), F32),
            jax.ShapeDtypeStruct((groups, per, LANES), F32),
            jax.ShapeDtypeStruct((1, hid + LANES), F32),
        ],
        in_specs=[vmem] * len(args),
        out_specs=[vmem] * 4,
        scratch_shapes=sends + recvs + [
            pltpu.VMEM((own, hid), F32),
            pltpu.VMEM((own, LANES), F32),
            pltpu.VMEM((own + halo + hubs, hid), F32),
            pltpu.VMEM((3, own + hubs, hid), BF16),
        ] + [pltpu.SemaphoreType.DMA] * 16,
        compiler_params=pltpu.CompilerParams(collective_id=2, has_side_effects=True, vmem_limit_bytes=56 * 2 ** 20),
        name="main_exchange",
    )(*args)


def output_kernel(dx_ref, gw1_ref, gw2_ref, bias_ref, dx_out, gw1_out, gw2_out, b1_out, b2_out):
    feat_in, feat_out, hid = dx_out.shape[1], gw2_out.shape[1], gw2_out.shape[0]
    dx_out[...] = dx_ref[:, :feat_in]
    gw1_out[...] = gw1_ref[...].reshape(hid, LANES).T[:feat_in, :]
    gw2_out[...] = gw2_ref[...].reshape(hid, LANES)[:, :feat_out]
    b1_out[...] = bias_ref[:, :hid]
    b2_out[...] = bias_ref[:, hid:hid + feat_out]


def solution(mesh):
    groups = mesh.shape["graph"]

    def device_step(x, dst, src, w, send, hub_ids, w_first, b_first, w_second, dy):
        own, feat_in = x.shape
        feat_out = dy.shape[1]
        hid = w_first.shape[1]
        halo, hubs = send.shape[0], hub_ids.shape[0]
        slots, dsts = own + halo + hubs, own + hubs
        send, hub_ids = send[None, :], hub_ids[None, :]
        keys, bounds, zt, d_ext, x_pad, home_x = first_call(
            groups, own, halo, hubs, hid, x, dy, send, hub_ids, w_first, dst.reshape(-1, LANES), src.reshape(-1, LANES))
        keys, weights = lax.sort((keys.reshape(-1), w), num_keys=1, is_stable=False)
        adj = adjacency(bounds, keys, weights, slots, dsts)
        raw = main_call(
            groups, own, halo, hubs, *adj, zt, d_ext, send, hub_ids, b_first[None, :], w_first, w_second, x_pad, home_x)
        dx, gw1, gw2, gb1, gb2 = pl.pallas_call(
            output_kernel,
            out_shape=[jax.ShapeDtypeStruct(shape, F32) for shape in (
                (own, feat_in), (feat_in, hid), (hid, feat_out), (1, hid), (1, feat_out))],
            name="outputs",
        )(*raw)
        return dx, gw1, gw2, gb1[0], gb2[0]

    rows, flat = P(("data", "graph"), None), P(("data", "graph"))
    return jax.shard_map(
        device_step,
        mesh=mesh,
        in_specs=(rows, flat, flat, flat, flat, P("data"), P(), P(), P(), rows),
        out_specs=(rows, P("data", None), P("data", None), P("data"), P("data")),
        check_vma=False,
    )
```

time: 190 us -> 124 us (0.65)
  Pallas kernels: 156 us -> 105 us
  local copies, waits for them, and re-layouts: 18.4 us -> 8.25 us
  matrix products: 5.02 us -> 0 us
    pallas_call x4 -> x3, Pallas kernels: 92.6 us -> 50.1 us  [the longest x1 30.9 us: first_call(): pl.pallas_call(functools.partial(first_kernel, groups, own, halo, hubs),...]
    sort x0 -> x1, other arithmetic: none -> 9.48 us  [device_step(): keys, weights = lax.sort((keys.reshape(-1), w), num_keys=1, is_stable=False)]
    pallas_call x1, Pallas kernels: 63.2 us -> 54.8 us  [main_call(): pl.pallas_call(functools.partial(main_kernel, groups, own, halo, hubs), o...]
    dot_general x4 -> x0, matrix products: 5.02 us -> none  [dot(): lax.dot_general(a, b, (((ca,), (cb,)), ((), ())), precision=precision, pr...]
    unnamed x28 -> x5, local copies, waits for them, and re-layouts: 12.4 us -> 8.25 us
    reduce_sum x3 -> x0, other arithmetic: 2.75 us -> none  [the longest x1 1.61 us: device_step(): hub_x, hub_d = exchange(groups, 'bb', [home_x, hub_d.sum(axis=0)], 1)]
    pad x4 -> x0, local copies, waits for them, and re-layouts: 2.67 us -> none  [the longest x1 1.43 us: device_step(): w1_pad = jnp.pad(w_first, ((0, LANES - feat_in), (0, 0)))]
where the time goes in v3:
time: 124 us; the launch traced here: 123 us
  Pallas kernels  105 us (85%)
  other arithmetic  9.48 us (8%)
  local copies, waits for them, and re-layouts  8.25 us (7%)
    pallas_call x1, Pallas kernels, main_call(): pl.pallas_call(functools.partial(main_kernel, groups, own, halo, hubs), o...  54.8 us
    pallas_call x1, Pallas kernels, first_call(): pl.pallas_call(functools.partial(first_kernel, groups, own, halo, hubs),...  30.9 us
    pallas_call x1, Pallas kernels, adjacency(): pl.pallas_call(functools.partial(adjacency_kernel, slots, dsts), out_shap...  17.3 us
    sort x1, other arithmetic, device_step(): keys, weights = lax.sort((keys.reshape(-1), w), num_keys=1, is_stable=False)  9.48 us
    unnamed x5, local copies, waits for them, and re-layouts  8.25 us

profile of v3, /device:TPU:1, one launch (start us, length us, event | category | flops | bytes accessed | tf_op | source)
XLA Modules:
  0.0 123.2 jit_solution(3381212395307021800)
XLA Ops:
  0.6 1.5 %copy.17.w2_ref = bf16[256,47]{1,0:T(8,128)(2,1)} copy(bf16[256,47]{0,1:T(8,128)(2,1)} %param.18) | data formatting | bytes 48128 | tf_op args[8]
  2.1 1.7 %copy.15.x_ref = bf16[512,100]{1,0:T(8,128)(2,1)} copy(bf16[512,100]{0,1:T(8,128)(2,1)} %param.10) | data formatting | bytes 204800 | tf_op args[0]
  3.8 1.7 %copy.16.dy_ref = f32[512,47]{1,0:T(8,128)} copy(f32[512,47]{0,1:T(8,128)} %param.19) | data formatting | bytes 192512 | tf_op args[9]
  5.5 30.9 %first_exchange.1 = (s32[256,128]{1,0:T(8,128)}, s32[8,128]{1,0:T(8,128)}, bf16[256,1024]{1,0:T(8,128)(2,1)}, f32[768,128]{1,0:T(8,128)}, bf16[512,128]{1,0:T(8,128)(2,1)}, /*index=5*/bf16[8,128]{1,0:T(8,128)(2,1)}) custom-call(bf16[512,100]{1,0:T(8,128)(2,1)} %copy.15.x_ref, f32[512,47]{1,0:T(8,128)} %copy.16.dy_ref, s32[1,256]{1,0:T(1,128)} %bitcast.15, ...), custom_call_target="tpu_custom_call" | custom-call | tf_op jit(solution)/shard_map/first_exchange/pallas_call | solution.py:185
  36.4 9.5 %sort.15 = (s32[32768]{0:T(1024)}, f32[32768]{0:T(1024)}) sort(s32[32768]{0:T(1024)} %bitcast.10, f32[32768]{0:T(1024)} %param.13), dimensions={0}, to_apply=%region_0.0 | sort | flops 491520 | bytes 524288 | tf_op jit(solution)/shard_map/sort | solution.py:459
  45.9 17.3 %adjacency.1 = (bf16[1024,768]{1,0:T(8,128)(2,1)}, bf16[1024,768]{1,0:T(8,128)(2,1)}, bf16[1024,768]{1,0:T(8,128)(2,1)}) custom-call(s32[8,128]{1,0:T(8,128)} %get-tuple-element.25.bound_ref, s32[256,128]{1,0:T(8,128)} %bitcast.11, f32[256,128]{1,0:T(8,128)} %bitcast.12), custom_call_target="tpu_custom_call" | custom-call | tf_op jit(solution)/shard_map/adjacency/pallas_call | solution.py:280
  63.2 54.8 %main_exchange.1 = (f32[512,128]{1,0:T(8,128)}, f32[128,2,128]{2,1,0:T(2,128)}, f32[128,2,128]{2,1,0:T(2,128)}, f32[1,384]{1,0:T(1,128)}) custom-call(bf16[1024,768]{1,0:T(8,128)(2,1)} %get-tuple-element.29.hi_ref, bf16[1024,768]{1,0:T(8,128)(2,1)} %get-tuple-element.30.mid_ref, bf16[1024,768]{1,0:T(8,128)(2,1)} %get-tuple-element.31.low_ref, ...), custom_call_target="tpu_custom_call" | custom-call | tf_op jit(solution)/shard_map/main_exchange/pallas_call | solution.py:417
  118.0 1.9 %outputs.1 = (f32[512,100]{1,0:T(8,128)}, f32[100,256]{1,0:T(8,128)}, f32[256,47]{1,0:T(8,128)}, f32[1,256]{1,0:T(1,128)}, f32[1,47]{1,0:T(1,128)}) custom-call(f32[512,128]{1,0:T(8,128)} %get-tuple-element.36.dx_ref, f32[128,2,128]{2,1,0:T(2,128)} %get-tuple-element.37.gw1_ref, f32[128,2,128]{2,1,0:T(2,128)} %get-tuple-element.38.gw2_ref, ...), custom_call_target="tpu_custom_call" | custom-call | tf_op jit(solution)/shard_map/outputs/pallas_call | solution.py:463
  119.9 1.8 %copy.18 = f32[512,100]{0,1:T(8,128)} copy(f32[512,100]{1,0:T(8,128)} %get-tuple-element.45) | data formatting | bytes 409600
  121.6 1.6 %copy.19 = f32[256,47]{0,1:T(8,128)} copy(f32[256,47]{1,0:T(8,128)} %get-tuple-element.47) | data formatting | bytes 96256

commit v4 on v3

v4 whole, which is shorter than its diff:
```python
import functools

import jax
import jax.numpy as jnp
from jax import lax
from jax.experimental import pallas as pl
from jax.experimental.pallas import tpu as pltpu
from jax.sharding import PartitionSpec as P

BF16 = jnp.bfloat16
F32 = jnp.float32
HI = lax.Precision.HIGHEST
LANES = 128
MESH = pl.DeviceIdType.MESH


def dot(a, b, ca=1, cb=0, precision=None):
    return lax.dot_general(a, b, (((ca,), (cb,)), ((), ())), precision=precision, preferred_element_type=F32)


def split3(a):
    hi = a.astype(BF16)
    rest = a - hi.astype(F32)
    mid = rest.astype(BF16)
    return hi, mid, (rest - mid.astype(F32)).astype(BF16)


def exact3(sel, pieces, ca=1):
    return dot(sel, pieces[2], ca) + dot(sel, pieces[1], ca) + dot(sel, pieces[0], ca)


def exact3_right(pieces, sel):
    return dot(pieces[2], sel) + dot(pieces[1], sel) + dot(pieces[0], sel)


def sum3(pieces):
    return pieces[2].astype(F32) + pieces[1].astype(F32) + pieces[0].astype(F32)


def full6(a, b):
    low = dot(a[0], b[2]) + dot(a[2], b[0]) + dot(a[1], b[1])
    return low + (dot(a[0], b[1]) + dot(a[1], b[0])) + dot(a[0], b[0])


def partner(groups, me, i):
    low = sum(2 << k for k in range(0, groups.bit_length() - 2, 2))
    t = jnp.bitwise_xor(i - 1, 2 * low + 1)
    high = jnp.bitwise_and(jnp.right_shift(t, 1), low)
    return jnp.bitwise_xor(me, jnp.bitwise_xor(t, jnp.bitwise_xor(high, low)))


def wait_all(groups, buf, sem, whole):
    part = buf if whole else buf.at[pl.ds(0, groups - 1)]
    pltpu.make_async_copy(part, part, sem).wait()


def send_all(groups, me, items):
    def send(i, carry):
        peer = partner(groups, me, i)
        for kind, src, dst, send_sem, recv_sem in items:
            pltpu.make_async_remote_copy(
                src_ref=src.at[peer] if kind == "a" else src,
                dst_ref=dst.at[me],
                send_sem=send_sem,
                recv_sem=recv_sem,
                device_id=(0, peer),
                device_id_type=MESH,
            ).start()
        return carry

    lax.fori_loop(1, groups, send, 0)
    for kind, src, dst, _, recv_sem in items:
        pltpu.make_async_copy(src.at[me] if kind == "a" else src, dst.at[me], recv_sem).start()


def greet_all(groups, me):
    barrier = pltpu.get_barrier_semaphore()

    def greet(i, carry):
        pl.semaphore_signal(barrier, inc=1, device_id=(0, partner(groups, me, i)), device_id_type=MESH)
        return carry

    lax.fori_loop(1, groups, greet, 0)
    return barrier


def padded(ref, rows, cols):
    a = ref[...]
    if cols > a.shape[1]:
        a = jnp.concatenate([a, jnp.zeros((a.shape[0], cols - a.shape[1]), a.dtype)], axis=1)
    if rows > a.shape[0]:
        a = jnp.concatenate([a, jnp.zeros((rows - a.shape[0], cols), a.dtype)], axis=0)
    return a


SRC_BLOCK, DST_BLOCK = 128, 256
BUCKET = SRC_BLOCK * DST_BLOCK
CHUNK_ROWS, UNROLL = 2, 8


def adjacency_kernel(slots, dsts, key_ref, w_ref, acc_ref, pair_ref, bound_ref):
    tops = dsts // DST_BLOCK
    buckets = slots // SRC_BLOCK * tops
    size = CHUNK_ROWS * LANES
    src_ids = lax.broadcasted_iota(jnp.int32, (SRC_BLOCK, LANES), 0).astype(F32).astype(BF16)
    dst_ids = lax.broadcasted_iota(jnp.int32, (DST_BLOCK, LANES), 0).astype(F32).astype(BF16)
    one, zero = jnp.ones((), BF16), jnp.zeros((), BF16)

    def clear(i, carry):
        acc_ref[pl.ds(pl.multiple_of(i * SRC_BLOCK, SRC_BLOCK), SRC_BLOCK), :] = jnp.zeros((SRC_BLOCK, DST_BLOCK), F32)
        return carry

    lax.fori_loop(0, buckets, clear, 0)

    def count(i, carry):
        bucket = jnp.right_shift(key_ref[pl.ds(pl.multiple_of(i * 8, 8), 8), :], BUCKET.bit_length() - 1)
        return tuple(c + jnp.where(bucket < b + 1, 1, 0) for b, c in enumerate(carry))

    zeros = jnp.zeros((8, LANES), jnp.int32)
    counts = lax.fori_loop(0, key_ref.shape[0] // 8, count, (zeros,) * buckets)
    bound_ref[0] = 0
    for b, c in enumerate(counts):
        bound_ref[b + 1] = jnp.sum(c.astype(F32)).astype(jnp.int32)

    def list_pairs(b, at):
        low, high = bound_ref[b], bound_ref[b + 1]
        start = low // size
        count = jnp.where(high > low, (high + size - 1) // size - start, 0)

        def put(i, carry):
            pair_ref[at + i] = b * 1024 + start + i
            return carry

        lax.fori_loop(0, count, put, 0)
        return at + count

    total = lax.fori_loop(0, buckets, list_pairs, 0)
    for i in range(UNROLL - 1):
        pair_ref[total + i] = buckets * 1024

    def step(it, carry):
        work = []
        for u in range(UNROLL):
            pair = pair_ref[it * UNROLL + u]
            b, c = jnp.right_shift(pair, 10), jnp.bitwise_and(pair, 1023)
            lhs, rhs = [], []
            for r in range(CHUNK_ROWS):
                rel = key_ref[pl.ds(c * CHUNK_ROWS + r, 1), :] - b * BUCKET
                weight = w_ref[pl.ds(c * CHUNK_ROWS + r, 1), :]
                src = jnp.right_shift(rel, 8)
                src = jnp.where((src >= 0) & (src < SRC_BLOCK), src, 512).astype(F32).astype(BF16)
                dst = jnp.bitwise_and(rel, DST_BLOCK - 1).astype(F32).astype(BF16)
                hit = src_ids == jnp.broadcast_to(src, src_ids.shape)
                lhs.append(jnp.concatenate(
                    [jnp.where(hit, jnp.broadcast_to(p, src_ids.shape), zero) for p in split3(weight)], axis=0))
                rhs.append(jnp.where(dst_ids == jnp.broadcast_to(dst, dst_ids.shape), one, zero))
            work.append((b, jnp.concatenate(lhs, axis=1), jnp.concatenate(rhs, axis=1)))
        outs = [dot(lhs, rhs, 1, 1) for _, lhs, rhs in work]
        for (b, _, _), out in zip(work, outs):
            rows = pl.ds(pl.multiple_of(b * SRC_BLOCK, SRC_BLOCK), SRC_BLOCK)
            acc_ref[rows, :] += out[2 * SRC_BLOCK:] + out[SRC_BLOCK:2 * SRC_BLOCK] + out[:SRC_BLOCK]
        return carry

    lax.fori_loop(0, (total + UNROLL - 1) // UNROLL, step, 0)


def adjacency(keys, weights, slots, dsts):
    edges = weights.shape[0]
    buckets = slots // SRC_BLOCK * (dsts // DST_BLOCK)
    vmem = pl.BlockSpec(memory_space=pltpu.VMEM)
    return pl.pallas_call(
        functools.partial(adjacency_kernel, slots, dsts),
        out_shape=jax.ShapeDtypeStruct(((buckets + 1) * SRC_BLOCK, DST_BLOCK), F32),
        in_specs=[vmem, vmem],
        out_specs=vmem,
        scratch_shapes=[
            pltpu.SMEM((edges // (CHUNK_ROWS * LANES) + buckets + UNROLL,), jnp.int32),
            pltpu.SMEM((buckets + 1,), jnp.int32),
        ],
        name="adjacency",
    )(keys.reshape(-1, LANES), weights.reshape(-1, LANES))


def rows_to_blocks(a, groups):
    return a.reshape(groups, a.shape[0] // groups, a.shape[1])


def main_kernel(groups, own, halo, hubs, cells_ref, xt_ref, dyt_ref, send_ref, hub_ref, b1_ref, w1_ref, w2t_ref,
                dxt_ref, gw_ref, bias_ref,
                sx, sd, hx, hd, s1, s2, s3, s4, s5, s6, s7, s8,
                rx, rd, gx, gd, r1, r2, r3, r4, r5, r6, r7,
                raw_ref, hi_ref, mid_ref, low_ref, hubrow_ref, pt_ref, g2_ref, g1_ref, dy_ref, zt_ref, load_sem, *sems):
    count = len(sems) // 2
    snd, rcv = sems[:count], sems[count:]
    adj = (hi_ref, mid_ref, low_ref)
    per = hubs // groups
    hid = b1_ref.shape[1]
    feat_in = xt_ref.shape[0]
    first_hub = own + halo
    slots, dsts = own + halo + hubs, own + hubs
    tops = dsts // DST_BLOCK
    me = lax.axis_index("graph")
    barrier = greet_all(groups, me)
    load = pltpu.make_async_copy(cells_ref.at[pl.ds(0, raw_ref.shape[0])], raw_ref, load_sem)
    load.start()

    lane = lax.broadcasted_iota(jnp.int32, (1, LANES), 1)
    half = lane < LANES // 2
    own_row = lax.broadcasted_iota(jnp.int32, (own, 1), 0)
    pick_t = (own_row == send_ref[...]).astype(F32).astype(BF16)
    sel_f = (own_row == hub_ref[...] - me * own).astype(F32)
    sel_t = sel_f.astype(BF16)
    plain = jnp.sum(sel_f, axis=1, keepdims=True) == 0
    number = lax.broadcasted_iota(jnp.int32, (1, hubs), 1) + 1
    numbers = jnp.broadcast_to(number.astype(F32), (8, hubs)).astype(BF16)
    code_row = dot(numbers, sel_t, 1, 1)[:1]
    plain_row = code_row == 0
    xt = padded(xt_ref, LANES, own)
    feature = lax.broadcasted_iota(jnp.int32, (LANES, 1), 0)
    xt = jnp.where(feature == feat_in, code_row, xt.astype(F32)).astype(BF16)
    dyt = padded(dyt_ref, LANES, own)
    picked = dot(jnp.concatenate((xt,) + split3(dyt), axis=0), jnp.concatenate([pick_t, sel_t], axis=1))
    hub_dt = picked[3 * LANES:, halo:] + picked[2 * LANES:3 * LANES, halo:] + picked[LANES:2 * LANES, halo:]
    sx[:, :per, :] = rows_to_blocks(picked[:LANES, :halo].T, groups).astype(BF16)
    sx[:, per:, :] = rows_to_blocks(picked[:LANES, halo:].T, groups).astype(BF16)
    sd[...] = rows_to_blocks(hub_dt.T, groups)
    pl.semaphore_wait(barrier, groups - 1)
    send_all(groups, me, [("a", sx, rx, snd[0], rcv[0]), ("a", sd, rd, snd[1], rcv[1])])

    w1 = padded(w1_ref, LANES, hid)
    w1_t = w1.astype(F32).T.astype(BF16)
    zt_ref[:, :own] = dot(w1_t, xt).astype(BF16)
    dy = dyt.T
    load.wait()

    def rename(i, carry):
        cell = [raw_ref[pl.ds(pl.multiple_of((i * tops + j) * SRC_BLOCK, SRC_BLOCK), SRC_BLOCK), :] for j in range(tops)]
        mine = jnp.concatenate(cell[:own // DST_BLOCK], axis=1)
        hub = jnp.concatenate(cell[own // DST_BLOCK:], axis=1) + exact3_right(split3(mine), sel_t)
        rows = pl.ds(pl.multiple_of(i * SRC_BLOCK, SRC_BLOCK), SRC_BLOCK)
        new = jnp.concatenate([jnp.where(plain_row, mine, 0.0), hub], axis=1)
        for ref, piece in zip(adj, split3(new)):
            ref[rows, :] = piece
        return carry

    lax.fori_loop(0, slots // SRC_BLOCK, rename, 0)
    sel = sel_f.T.astype(BF16)
    for j in range(tops):
        cols = slice(j * DST_BLOCK, (j + 1) * DST_BLOCK)
        base = first_hub // SRC_BLOCK
        old = jnp.concatenate(
            [sum3([a[(base + k) * SRC_BLOCK:(base + k + 1) * SRC_BLOCK, cols] for a in adj])
             for k in range(hubs // SRC_BLOCK)], axis=0)
        hubrow_ref[:, cols] = old + exact3(sel, [a[:own, cols] for a in adj])
    for a in adj:
        a[:own, :] = jnp.where(plain, a[:own, :].astype(F32), 0.0).astype(BF16)
    wait_all(groups, rx, rcv[0], True)
    wait_all(groups, rd, rcv[1], True)
    got = rx[...].astype(F32)
    home_x = got[:, per:, :].sum(axis=0)
    hx[...] = home_x.astype(BF16)
    hd[...] = rd[...].sum(axis=0)
    send_all(groups, me, [("b", hx, gx, snd[2], rcv[2]), ("b", hd, gd, snd[3], rcv[3])])

    home_x = jnp.concatenate([home_x, jnp.zeros((8 - per, LANES), F32)], axis=0).astype(BF16)
    halo_x = got[:, :per, :].reshape(halo, LANES)
    halo_code = halo_x[:, feat_in:feat_in + 1]
    halo_x = halo_x.astype(BF16)
    zt_ref[:, own:first_hub] = dot(w1_t, halo_x, 1, 1).astype(BF16)
    column = jnp.broadcast_to(jnp.where(lane == feat_in, 1.0, 0.0), (8, LANES)).astype(BF16)
    halo_row = dot(column, halo_x, 1, 1)[:1].astype(jnp.int32)
    halo_sel = (lax.broadcasted_iota(jnp.int32, (hubs, 1), 0) + 1 == halo_row).astype(F32).astype(BF16)
    for j in range(tops):
        cols = slice(j * DST_BLOCK, (j + 1) * DST_BLOCK)
        new = hubrow_ref[:, cols] + exact3(halo_sel, [a[own:first_hub, cols] for a in adj])
        for a, piece in zip(adj, split3(new)):
            a[first_hub:, cols] = piece
    for a in adj:
        a[own:first_hub, :] = jnp.where(halo_code == 0, a[own:first_hub, :].astype(F32), 0.0).astype(BF16)

    def forward(rows, cols):
        zt = zt_ref[:, rows]
        return dot(zt, low_ref[rows, cols]) + dot(zt, mid_ref[rows, cols]) + dot(zt, hi_ref[rows, cols])

    def pack(d):
        dh, dm, dl = split3(d)
        d_two = (dh.astype(F32) + pltpu.roll(dm.astype(F32), LANES // 2, 1)).astype(BF16)
        return jnp.concatenate([d_two, dl], axis=1), d_two, dh

    def grad_out_sums(rows, cols, packed):
        a = dot(hi_ref[rows, cols], packed[0])
        t = a[:, :LANES] + a[:, LANES:] + dot(mid_ref[rows, cols], packed[1]) + dot(low_ref[rows, cols], packed[2])
        return jnp.where(half, t + pltpu.roll(t, LANES // 2, 1), 0.0)

    own_cols, hub_cols = slice(0, own), slice(own, dsts)
    pt_ref[...] = forward(slice(0, first_hub), slice(0, dsts))
    d_own = pack(dy)
    g2_ref[...] = grad_out_sums(slice(0, slots), own_cols, d_own)
    wait_all(groups, gx, rcv[2], True)
    wait_all(groups, gd, rcv[3], True)
    hub_x = gx[...].astype(F32).reshape(hubs, LANES).astype(BF16)
    zt_ref[:, first_hub:] = dot(w1_t, hub_x, 1, 1).astype(BF16)
    d_hub = pack(gd[...].reshape(hubs, LANES))
    hub_slots = slice(first_hub, slots)
    y_hub = (pt_ref[:, own:] + forward(hub_slots, hub_cols)).T
    s1[:, :, LANES:] = rows_to_blocks(y_hub, groups)
    g2_halo = g2_ref[own:first_hub, :] + grad_out_sums(slice(own, first_hub), hub_cols, d_hub)
    g2_hub = g2_ref[first_hub:, :] + grad_out_sums(hub_slots, hub_cols, d_hub)
    s1[:, :, :LANES] = rows_to_blocks(g2_halo + pltpu.roll(g2_hub, LANES // 2, 1), groups)
    send_all(groups, me, [("a", s1, r1, snd[4], rcv[4])])

    b1 = b1_ref[...]
    w2t = padded(w2t_ref, LANES, hid)
    pre = (pt_ref[:, :own] + forward(hub_slots, own_cols)).T + b1
    g2_own = g2_ref[:own, :] + grad_out_sums(slice(0, own), hub_cols, d_hub)
    hidden = jnp.where(plain, jax.nn.relu(pre), 0.0).astype(BF16)
    live = plain & (pre > 0)
    wait_all(groups, r1, rcv[4], True)
    home = r1[...].sum(axis=0)
    pad = jnp.zeros((8 - per, LANES), F32)
    home_g = jnp.where(half, pltpu.roll(jnp.concatenate([home[:, :LANES], pad], axis=0), LANES // 2, 1), 0.0)
    home_pre = jnp.concatenate([home[:, LANES:] + b1, jnp.zeros((8 - per, hid), F32)], axis=0)
    home_dz2 = home_g.astype(BF16)
    home_dy = jnp.where(home_pre > 0, dot(home_dz2, w2t), 0.0)
    s2[...] = home_dy[:per]
    send_all(groups, me, [("b", s2, r2, snd[5], rcv[5])])

    back = jnp.where(half, r1[:, :, :LANES].reshape(halo, LANES), 0.0)
    dz2 = (g2_own + exact3(pick_t, split3(back))).astype(BF16)
    dy1 = jnp.where(live, dot(dz2, w2t), 0.0)
    home_hidden = jax.nn.relu(home_pre).astype(BF16)
    gw2 = dot(dz2, hidden, 0, 0) + dot(home_dz2, home_hidden, 0, 0)
    s3[...] = rows_to_blocks(gw2, groups)
    s4[:, :hid] = dy1.sum(axis=0, keepdims=True) + home_dy.sum(axis=0, keepdims=True)
    s4[:, hid:] = dy.sum(axis=0, keepdims=True)
    send_all(groups, me, [("a", s3, r3, snd[6], rcv[6]), ("b", s4, r4, snd[7], rcv[7])])
    for p, piece in enumerate(split3(dy1)):
        dy_ref[p, :own, :] = piece
    chunk = 256

    def own_part(i, carry):
        rows = pl.ds(pl.multiple_of(i * chunk, chunk), chunk)
        g1_ref[rows, :] = full6([a[rows, :own] for a in adj], [dy_ref[p, :own, :] for p in range(3)])
        return carry

    lax.fori_loop(0, slots // chunk, own_part, 0)
    wait_all(groups, r2, rcv[5], True)
    for p, piece in enumerate(split3(r2[...].reshape(hubs, hid))):
        dy_ref[p, own:, :] = piece

    def hub_part(rows):
        return g1_ref[rows, :] + full6([a[rows, own:] for a in adj], [dy_ref[p, own:, :] for p in range(3)])

    s5[:, :per, :] = rows_to_blocks(hub_part(slice(own, first_hub)), groups)
    s5[:, per:, :] = rows_to_blocks(hub_part(hub_slots), groups)
    send_all(groups, me, [("a", s5, r5, snd[8], rcv[8])])

    g1_ref[:chunk, :] = hub_part(slice(0, chunk))
    g1_ref[chunk:own, :] = hub_part(slice(chunk, own))
    wait_all(groups, r3, rcv[6], True)
    wait_all(groups, r4, rcv[7], True)
    bias_ref[...] = r4[...].sum(axis=0)
    s8[:, hid:] = r3[...].sum(axis=0)
    wait_all(groups, r5, rcv[8], True)
    home_dz1 = jnp.concatenate([r5[:, per:, :].sum(axis=0), jnp.zeros((8 - per, hid), F32)], axis=0).astype(BF16)
    back = r5[:, :per, :].reshape(halo, hid)
    dz1 = g1_ref[:own, :] + exact3(pick_t, split3(back))
    dz1 = jnp.where(plain, dz1, 0.0).astype(BF16)
    gw1 = dot(xt, dz1) + dot(home_x, home_dz1, 0, 0)
    s6[...] = rows_to_blocks(gw1, groups)
    s7[...] = dot(home_dz1, w1, 1, 1)[:per]
    send_all(groups, me, [("a", s6, r6, snd[9], rcv[9]), ("b", s7, r7, snd[10], rcv[10])])

    dxt = dot(w1, dz1, 1, 1)
    wait_all(groups, r6, rcv[9], True)
    s8[:, :hid] = r6[...].sum(axis=0)
    send_all(groups, me, [("b", s8, gw_ref, snd[11], rcv[11])])

    wait_all(groups, r7, rcv[10], True)
    hub_dx = r7[...].reshape(hubs, LANES).T
    dxt_ref[...] = dxt + exact3_right(split3(hub_dx), sel)
    for buf, sem in zip((rx, rd, gx, gd, r1, r2, r3, r4, r5, r6, r7, gw_ref), snd):
        wait_all(groups, buf, sem, False)
    wait_all(groups, gw_ref, rcv[11], True)


def main_call(groups, own, halo, hubs, *args):
    hid = args[5].shape[1]
    per = hubs // groups
    slots, dsts = own + halo + hubs, own + hubs
    cells = slots * dsts // DST_BLOCK
    vmem = pl.BlockSpec(memory_space=pltpu.VMEM)
    blocks = [
        ("a", (2 * per, LANES), BF16), ("a", (per, LANES), F32), ("b", (per, LANES), BF16), ("b", (per, LANES), F32),
        ("a", (per, LANES + hid), F32), ("b", (per, hid), F32), ("a", (1, hid), F32), ("b", (1, hid + LANES), F32),
        ("a", (2 * per, hid), F32), ("a", (1, hid), F32), ("b", (per, LANES), F32), ("b", (1, 2 * hid), F32)]
    sends = [pltpu.VMEM(((groups,) if k == "a" else ()) + b, t) for k, b, t in blocks]
    recvs = [pltpu.VMEM((groups,) + b, t) for _, b, t in blocks[:-1]]
    shape = jax.ShapeDtypeStruct
    return pl.pallas_call(
        functools.partial(main_kernel, groups, own, halo, hubs),
        out_shape=[shape((LANES, own), F32), shape((groups, 1, 2 * hid), F32), shape((1, hid + LANES), F32)],
        in_specs=[pl.BlockSpec(memory_space=pl.ANY)] + [vmem] * (len(args) - 1),
        out_specs=[vmem] * 3,
        scratch_shapes=sends + recvs + [
            pltpu.VMEM((cells, DST_BLOCK), F32),
            pltpu.VMEM((slots, dsts), BF16),
            pltpu.VMEM((slots, dsts), BF16),
            pltpu.VMEM((slots, dsts), BF16),
            pltpu.VMEM((hubs, dsts), F32),
            pltpu.VMEM((hid, dsts), F32),
            pltpu.VMEM((slots, LANES), F32),
            pltpu.VMEM((slots, hid), F32),
            pltpu.VMEM((3, dsts, hid), BF16),
            pltpu.VMEM((hid, slots), BF16),
        ] + [pltpu.SemaphoreType.DMA] * (1 + 2 * len(blocks)),
        compiler_params=pltpu.CompilerParams(collective_id=0, has_side_effects=True, vmem_limit_bytes=56 * 2 ** 20),
        name="main_exchange",
    )(*args)


def output_kernel(dxt_ref, gw_ref, bias_ref, dx_out, gw1_out, gw2_out, b1_out, b2_out):
    feat_in, feat_out, hid = dx_out.shape[0], gw2_out.shape[0], gw2_out.shape[1]
    dx_out[...] = dxt_ref[:feat_in, :]
    gw = gw_ref[...].reshape(gw_ref.shape[0], 2 * hid)
    gw1_out[...] = gw[:feat_in, :hid]
    gw2_out[...] = gw[:feat_out, hid:]
    b1_out[...] = bias_ref[:, :hid]
    b2_out[...] = bias_ref[:, hid:hid + feat_out]


def solution(mesh):
    groups = mesh.shape["graph"]

    def device_step(x, dst, src, w, send, hub_ids, w_first, b_first, w_second, dy):
        own, feat_in = x.shape
        feat_out = dy.shape[1]
        hid = w_first.shape[1]
        halo, hubs = send.shape[0], hub_ids.shape[0]
        slots, dsts = own + halo + hubs, own + hubs
        bucket = jnp.right_shift(src, SRC_BLOCK.bit_length() - 1) * (dsts // DST_BLOCK)
        bucket = bucket + jnp.right_shift(dst, DST_BLOCK.bit_length() - 1)
        keys = bucket * BUCKET + jnp.bitwise_and(src, SRC_BLOCK - 1) * DST_BLOCK + jnp.bitwise_and(dst, DST_BLOCK - 1)
        keys, weights = lax.sort((keys, w), num_keys=1, is_stable=False)
        cells = adjacency(keys, weights, slots, dsts)
        raw = main_call(
            groups, own, halo, hubs, cells, x.T, dy.T, send[None, :], hub_ids[None, :], b_first[None, :],
            w_first, w_second.T)
        dx, gw1, gw2, gb1, gb2 = pl.pallas_call(
            output_kernel,
            out_shape=[jax.ShapeDtypeStruct(shape, F32) for shape in (
                (feat_in, own), (feat_in, hid), (feat_out, hid), (1, hid), (1, feat_out))],
            name="outputs",
        )(*raw)
        return dx.T, gw1, gw2.T, gb1[0], gb2[0]

    rows, flat = P(("data", "graph"), None), P(("data", "graph"))
    return jax.shard_map(
        device_step,
        mesh=mesh,
        in_specs=(rows, flat, flat, flat, flat, P("data"), P(), P(), P(), rows),
        out_specs=(rows, P("data", None), P("data", None), P("data"), P("data")),
        check_vma=False,
    )
```

time: 124 us -> 98.8 us (0.80)
  Pallas kernels: 105 us -> 87.8 us
  local copies, waits for them, and re-layouts: 8.25 us -> 0 us
    pallas_call x1 -> x0, Pallas kernels: 30.9 us -> none  [first_call(): pl.pallas_call(functools.partial(first_kernel, groups, own, halo, hubs),...]
    pallas_call x1, Pallas kernels: 54.8 us -> 68.7 us  [main_call(): pl.pallas_call(functools.partial(main_kernel, groups, own, halo, hubs), o...]
    unnamed x5 -> x0, local copies, waits for them, and re-layouts: 8.25 us -> none
where the time goes in v4:
time: 98.8 us; the launch traced here: 98.9 us
  Pallas kernels  87.8 us (89%)
  other arithmetic  10.4 us (11%)
    pallas_call x1, Pallas kernels, main_call(): pl.pallas_call(functools.partial(main_kernel, groups, own, halo, hubs), o...  68.7 us
    pallas_call x1, Pallas kernels, adjacency(): pl.pallas_call(functools.partial(adjacency_kernel, slots, dsts), out_shap...  17.3 us
    sort x1, other arithmetic, device_step(): keys, weights = lax.sort((keys, w), num_keys=1, is_stable=False)  9.41 us

profile of v4, /device:TPU:1, one launch (start us, length us, event | category | flops | bytes accessed | tf_op | source)
XLA Modules:
  0.0 98.9 jit_solution(12829493849967407803)
XLA Ops:
  0.6 1.0 %and_add_fusion = s32[32768]{0:T(1024)S(1)} fusion(s32[32768]{0:T(1024)} %param.11, s32[32768]{0:T(1024)} %param.12), kind=kLoop, calls=%fused_computation | loop fusion | flops 327680 | bytes 393216 | tf_op jit(solution)/shard_map/add | solution.py:443
  1.6 9.4 %sort.15 = (s32[32768]{0:T(1024)}, f32[32768]{0:T(1024)}) sort(s32[32768]{0:T(1024)S(1)} %and_add_fusion, f32[32768]{0:T(1024)} %param.13), dimensions={0}, to_apply=%region_0.0 | sort | flops 491520 | bytes 524288 | tf_op jit(solution)/shard_map/sort | solution.py:444
  11.1 17.3 %adjacency.1.cells_ref = f32[3200,256]{1,0:T(8,128)} custom-call(s32[256,128]{1,0:T(8,128)} %bitcast.12, f32[256,128]{1,0:T(8,128)} %bitcast.13), custom_call_target="tpu_custom_call" | custom-call | tf_op jit(solution)/shard_map/adjacency/pallas_call | solution.py:171
  28.3 68.7 %main_exchange.1 = (f32[128,512]{1,0:T(8,128)}, f32[128,1,512]{2,1,0:T(1,128)}, f32[1,384]{1,0:T(1,128)}) custom-call(f32[3200,256]{1,0:T(8,128)} %adjacency.1.cells_ref, bf16[100,512]{1,0:T(8,128)(2,1)} %bitcast.14, f32[47,512]{1,0:T(8,128)} %bitcast.15, s32[1,256]{1,0:T(1,128)} %bitcast.17, s32[1,256]{1,0:T(1,128)} %bitcast.18, f32[1,256]{1,0:T(1,128)} %bitcast.19, ...), custom_call_target="tpu_custom_call" | custom-call | tf_op jit(solution)/shard_map/main_exchange/pallas_call | solution.py:400
  97.1 1.8 %outputs.1 = (f32[100,512]{1,0:T(8,128)}, f32[100,256]{1,0:T(8,128)}, f32[47,256]{1,0:T(8,128)}, f32[1,256]{1,0:T(1,128)}, f32[1,47]{1,0:T(1,128)}) custom-call(f32[128,512]{1,0:T(8,128)} %get-tuple-element.17.dxt_ref, f32[128,1,512]{2,1,0:T(1,128)} %get-tuple-element.18.gw_ref, f32[1,384]{1,0:T(1,128)} %get-tuple-element.19.bias_ref), custom_call_target="tpu_custom_call" | custom-call | tf_op jit(solution)/shard_map/outputs/pallas_call | solution.py:449

commit v5 on v4

--- a/solution.py
+++ b/solution.py
@@ -96,21 +96,11 @@
 SRC_BLOCK, DST_BLOCK = 128, 256
 BUCKET = SRC_BLOCK * DST_BLOCK
 CHUNK_ROWS, UNROLL = 2, 8
-
-
-def adjacency_kernel(slots, dsts, key_ref, w_ref, acc_ref, pair_ref, bound_ref):
-    tops = dsts // DST_BLOCK
-    buckets = slots // SRC_BLOCK * tops
+STEPS_BEFORE, STEPS_MIDDLE = 3, 10
+
+
+def plan_kernel(buckets, key_ref, plan_ref, bound_ref):
     size = CHUNK_ROWS * LANES
-    src_ids = lax.broadcasted_iota(jnp.int32, (SRC_BLOCK, LANES), 0).astype(F32).astype(BF16)
-    dst_ids = lax.broadcasted_iota(jnp.int32, (DST_BLOCK, LANES), 0).astype(F32).astype(BF16)
-    one, zero = jnp.ones((), BF16), jnp.zeros((), BF16)
-
-    def clear(i, carry):
-        acc_ref[pl.ds(pl.multiple_of(i * SRC_BLOCK, SRC_BLOCK), SRC_BLOCK), :] = jnp.zeros((SRC_BLOCK, DST_BLOCK), F32)
-        return carry
-
-    lax.fori_loop(0, buckets, clear, 0)
 
     def count(i, carry):
         bucket = jnp.right_shift(key_ref[pl.ds(pl.multiple_of(i * 8, 8), 8), :], BUCKET.bit_length() - 1)
@@ -122,27 +112,51 @@
     for b, c in enumerate(counts):
         bound_ref[b + 1] = jnp.sum(c.astype(F32)).astype(jnp.int32)
 
+    def put(at, bucket, chunk, same):
+        plan_ref[0, at] = bucket
+        plan_ref[1, at] = chunk
+        plan_ref[2, at] = same
+
     def list_pairs(b, at):
         low, high = bound_ref[b], bound_ref[b + 1]
         start = low // size
-        count = jnp.where(high > low, (high + size - 1) // size - start, 0)
-
-        def put(i, carry):
-            pair_ref[at + i] = b * 1024 + start + i
+        pairs = jnp.where(high > low, (high + size - 1) // size - start, 0)
+        plan_ref[3, b] = jnp.where(pairs > 0, at + pairs, 0)
+
+        def pair(i, carry):
+            put(at + i, b, start + i, jnp.where(i > 0, 1, 0))
             return carry
 
-        lax.fori_loop(0, count, put, 0)
-        return at + count
-
-    total = lax.fori_loop(0, buckets, list_pairs, 0)
-    for i in range(UNROLL - 1):
-        pair_ref[total + i] = buckets * 1024
+        lax.fori_loop(0, pairs, pair, 0)
+        return at + pairs
+
+    def rest(i, carry):
+        put(i, buckets, 0, 0)
+        return carry
+
+    lax.fori_loop(lax.fori_loop(0, buckets, list_pairs, 0), key_ref.shape[0] // CHUNK_ROWS + buckets, rest, 0)
+
+
+def edge_plan(keys, buckets):
+    return pl.pallas_call(
+        functools.partial(plan_kernel, buckets),
+        out_shape=jax.ShapeDtypeStruct((4, 256), jnp.int32),
+        in_specs=[pl.BlockSpec(memory_space=pltpu.VMEM)],
+        out_specs=pl.BlockSpec(memory_space=pltpu.SMEM),
+        scratch_shapes=[pltpu.SMEM((buckets + 1,), jnp.int32)],
+        name="edge_plan",
+    )(keys)
+
+
+def add_pairs(plan_ref, key_ref, w_ref, cum_ref, low, high):
+    src_ids = lax.broadcasted_iota(jnp.int32, (SRC_BLOCK, LANES), 0).astype(F32).astype(BF16)
+    dst_ids = lax.broadcasted_iota(jnp.int32, (DST_BLOCK, LANES), 0).astype(F32).astype(BF16)
+    one, zero = jnp.ones((), BF16), jnp.zeros((), BF16)
 
     def step(it, carry):
         work = []
         for u in range(UNROLL):
-            pair = pair_ref[it * UNROLL + u]
-            b, c = jnp.right_shift(pair, 10), jnp.bitwise_and(pair, 1023)
+            b, c = plan_ref[0, it * UNROLL + u], plan_ref[1, it * UNROLL + u]
             lhs, rhs = [], []
             for r in range(CHUNK_ROWS):
                 rel = key_ref[pl.ds(c * CHUNK_ROWS + r, 1), :] - b * BUCKET
@@ -154,42 +168,28 @@
                 lhs.append(jnp.concatenate(
                     [jnp.where(hit, jnp.broadcast_to(p, src_ids.shape), zero) for p in split3(weight)], axis=0))
                 rhs.append(jnp.where(dst_ids == jnp.broadcast_to(dst, dst_ids.shape), one, zero))
-            work.append((b, jnp.concatenate(lhs, axis=1), jnp.concatenate(rhs, axis=1)))
-        outs = [dot(lhs, rhs, 1, 1) for _, lhs, rhs in work]
-        for (b, _, _), out in zip(work, outs):
-            rows = pl.ds(pl.multiple_of(b * SRC_BLOCK, SRC_BLOCK), SRC_BLOCK)
-            acc_ref[rows, :] += out[2 * SRC_BLOCK:] + out[SRC_BLOCK:2 * SRC_BLOCK] + out[:SRC_BLOCK]
-        return carry
-
-    lax.fori_loop(0, (total + UNROLL - 1) // UNROLL, step, 0)
-
-
-def adjacency(keys, weights, slots, dsts):
-    edges = weights.shape[0]
-    buckets = slots // SRC_BLOCK * (dsts // DST_BLOCK)
-    vmem = pl.BlockSpec(memory_space=pltpu.VMEM)
-    return pl.pallas_call(
-        functools.partial(adjacency_kernel, slots, dsts),
-        out_shape=jax.ShapeDtypeStruct(((buckets + 1) * SRC_BLOCK, DST_BLOCK), F32),
-        in_specs=[vmem, vmem],
-        out_specs=vmem,
-        scratch_shapes=[
-            pltpu.SMEM((edges // (CHUNK_ROWS * LANES) + buckets + UNROLL,), jnp.int32),
-            pltpu.SMEM((buckets + 1,), jnp.int32),
-        ],
-        name="adjacency",
-    )(keys.reshape(-1, LANES), weights.reshape(-1, LANES))
+            work.append((jnp.concatenate(lhs, axis=1), jnp.concatenate(rhs, axis=1)))
+        outs = [dot(lhs, rhs, 1, 1) for lhs, rhs in work]
+        total = cum_ref[it * UNROLL]
+        for u, out in enumerate(outs):
+            same = jnp.broadcast_to(plan_ref[2, it * UNROLL + u], (1, DST_BLOCK)) > 0
+            out = out[2 * SRC_BLOCK:] + out[SRC_BLOCK:2 * SRC_BLOCK] + out[:SRC_BLOCK]
+            total = out + jnp.where(same, total, 0.0)
+            cum_ref[it * UNROLL + u + 1] = total
+        return carry
+
+    lax.fori_loop(low, high, step, 0)
 
 
 def rows_to_blocks(a, groups):
     return a.reshape(groups, a.shape[0] // groups, a.shape[1])
 
 
-def main_kernel(groups, own, halo, hubs, cells_ref, xt_ref, dyt_ref, send_ref, hub_ref, b1_ref, w1_ref, w2t_ref,
+def main_kernel(groups, own, halo, hubs, plan_ref, key_ref, w_ref, xt_ref, dyt_ref, send_ref, hub_ref, b1_ref, w1_ref, w2t_ref,
                 dxt_ref, gw_ref, bias_ref,
                 sx, sd, hx, hd, s1, s2, s3, s4, s5, s6, s7, s8,
                 rx, rd, gx, gd, r1, r2, r3, r4, r5, r6, r7,
-                raw_ref, hi_ref, mid_ref, low_ref, hubrow_ref, pt_ref, g2_ref, g1_ref, dy_ref, zt_ref, load_sem, *sems):
+                cum_ref, hi_ref, mid_ref, low_ref, hubrow_ref, pt_ref, g2_ref, g1_ref, dy_ref, zt_ref, *sems):
     count = len(sems) // 2
     snd, rcv = sems[:count], sems[count:]
     adj = (hi_ref, mid_ref, low_ref)
@@ -201,8 +201,9 @@
     tops = dsts // DST_BLOCK
     me = lax.axis_index("graph")
     barrier = greet_all(groups, me)
-    load = pltpu.make_async_copy(cells_ref.at[pl.ds(0, raw_ref.shape[0])], raw_ref, load_sem)
-    load.start()
+    steps = (cum_ref.shape[0] - 1) // UNROLL
+    before, middle = steps * STEPS_BEFORE // 19, steps * STEPS_MIDDLE // 19
+    cum_ref[0] = jnp.zeros((SRC_BLOCK, DST_BLOCK), F32)
 
     lane = lax.broadcasted_iota(jnp.int32, (1, LANES), 1)
     half = lane < LANES // 2
@@ -224,6 +225,7 @@
     sx[:, :per, :] = rows_to_blocks(picked[:LANES, :halo].T, groups).astype(BF16)
     sx[:, per:, :] = rows_to_blocks(picked[:LANES, halo:].T, groups).astype(BF16)
     sd[...] = rows_to_blocks(hub_dt.T, groups)
+    add_pairs(plan_ref, key_ref, w_ref, cum_ref, 0, before)
     pl.semaphore_wait(barrier, groups - 1)
     send_all(groups, me, [("a", sx, rx, snd[0], rcv[0]), ("a", sd, rd, snd[1], rcv[1])])
 
@@ -231,10 +233,27 @@
     w1_t = w1.astype(F32).T.astype(BF16)
     zt_ref[:, :own] = dot(w1_t, xt).astype(BF16)
     dy = dyt.T
-    load.wait()
+    add_pairs(plan_ref, key_ref, w_ref, cum_ref, before, middle)
+    wait_all(groups, rx, rcv[0], True)
+    wait_all(groups, rd, rcv[1], True)
+    got = rx[...].astype(F32)
+    home_x = got[:, per:, :].sum(axis=0)
+    hx[...] = home_x.astype(BF16)
+    hd[...] = rd[...].sum(axis=0)
+    send_all(groups, me, [("b", hx, gx, snd[2], rcv[2]), ("b", hd, gd, snd[3], rcv[3])])
+
+    home_x = jnp.concatenate([home_x, jnp.zeros((8 - per, LANES), F32)], axis=0).astype(BF16)
+    halo_x = got[:, :per, :].reshape(halo, LANES)
+    halo_code = halo_x[:, feat_in:feat_in + 1]
+    halo_x = halo_x.astype(BF16)
+    zt_ref[:, own:first_hub] = dot(w1_t, halo_x, 1, 1).astype(BF16)
+    column = jnp.broadcast_to(jnp.where(lane == feat_in, 1.0, 0.0), (8, LANES)).astype(BF16)
+    halo_row = dot(column, halo_x, 1, 1)[:1].astype(jnp.int32)
+    halo_sel = (lax.broadcasted_iota(jnp.int32, (hubs, 1), 0) + 1 == halo_row).astype(F32).astype(BF16)
+    add_pairs(plan_ref, key_ref, w_ref, cum_ref, middle, steps)
 
     def rename(i, carry):
-        cell = [raw_ref[pl.ds(pl.multiple_of((i * tops + j) * SRC_BLOCK, SRC_BLOCK), SRC_BLOCK), :] for j in range(tops)]
+        cell = [cum_ref[plan_ref[3, i * tops + j]] for j in range(tops)]
         mine = jnp.concatenate(cell[:own // DST_BLOCK], axis=1)
         hub = jnp.concatenate(cell[own // DST_BLOCK:], axis=1) + exact3_right(split3(mine), sel_t)
         rows = pl.ds(pl.multiple_of(i * SRC_BLOCK, SRC_BLOCK), SRC_BLOCK)
@@ -254,22 +273,6 @@
         hubrow_ref[:, cols] = old + exact3(sel, [a[:own, cols] for a in adj])
     for a in adj:
         a[:own, :] = jnp.where(plain, a[:own, :].astype(F32), 0.0).astype(BF16)
-    wait_all(groups, rx, rcv[0], True)
-    wait_all(groups, rd, rcv[1], True)
-    got = rx[...].astype(F32)
-    home_x = got[:, per:, :].sum(axis=0)
-    hx[...] = home_x.astype(BF16)
-    hd[...] = rd[...].sum(axis=0)
-    send_all(groups, me, [("b", hx, gx, snd[2], rcv[2]), ("b", hd, gd, snd[3], rcv[3])])
-
-    home_x = jnp.concatenate([home_x, jnp.zeros((8 - per, LANES), F32)], axis=0).astype(BF16)
-    halo_x = got[:, :per, :].reshape(halo, LANES)
-    halo_code = halo_x[:, feat_in:feat_in + 1]
-    halo_x = halo_x.astype(BF16)
-    zt_ref[:, own:first_hub] = dot(w1_t, halo_x, 1, 1).astype(BF16)
-    column = jnp.broadcast_to(jnp.where(lane == feat_in, 1.0, 0.0), (8, LANES)).astype(BF16)
-    halo_row = dot(column, halo_x, 1, 1)[:1].astype(jnp.int32)
-    halo_sel = (lax.broadcasted_iota(jnp.int32, (hubs, 1), 0) + 1 == halo_row).astype(F32).astype(BF16)
     for j in range(tops):
         cols = slice(j * DST_BLOCK, (j + 1) * DST_BLOCK)
         new = hubrow_ref[:, cols] + exact3(halo_sel, [a[own:first_hub, cols] for a in adj])
@@ -385,10 +388,10 @@
 
 
 def main_call(groups, own, halo, hubs, *args):
-    hid = args[5].shape[1]
+    hid = args[7].shape[1]
     per = hubs // groups
     slots, dsts = own + halo + hubs, own + hubs
-    cells = slots * dsts // DST_BLOCK
+    pairs = args[1].shape[0] // CHUNK_ROWS + slots // SRC_BLOCK * (dsts // DST_BLOCK)
     vmem = pl.BlockSpec(memory_space=pltpu.VMEM)
     blocks = [
         ("a", (2 * per, LANES), BF16), ("a", (per, LANES), F32), ("b", (per, LANES), BF16), ("b", (per, LANES), F32),
@@ -400,10 +403,10 @@
     return pl.pallas_call(
         functools.partial(main_kernel, groups, own, halo, hubs),
         out_shape=[shape((LANES, own), F32), shape((groups, 1, 2 * hid), F32), shape((1, hid + LANES), F32)],
-        in_specs=[pl.BlockSpec(memory_space=pl.ANY)] + [vmem] * (len(args) - 1),
+        in_specs=[pl.BlockSpec(memory_space=pltpu.SMEM)] + [vmem] * (len(args) - 1),
         out_specs=[vmem] * 3,
         scratch_shapes=sends + recvs + [
-            pltpu.VMEM((cells, DST_BLOCK), F32),
+            pltpu.VMEM((pairs + 1, SRC_BLOCK, DST_BLOCK), F32),
             pltpu.VMEM((slots, dsts), BF16),
             pltpu.VMEM((slots, dsts), BF16),
             pltpu.VMEM((slots, dsts), BF16),
@@ -413,7 +416,7 @@
             pltpu.VMEM((slots, hid), F32),
             pltpu.VMEM((3, dsts, hid), BF16),
             pltpu.VMEM((hid, slots), BF16),
-        ] + [pltpu.SemaphoreType.DMA] * (1 + 2 * len(blocks)),
+        ] + [pltpu.SemaphoreType.DMA] * (2 * len(blocks)),
         compiler_params=pltpu.CompilerParams(collective_id=0, has_side_effects=True, vmem_limit_bytes=56 * 2 ** 20),
         name="main_exchange",
     )(*args)
@@ -442,9 +445,10 @@
         bucket = bucket + jnp.right_shift(dst, DST_BLOCK.bit_length() - 1)
         keys = bucket * BUCKET + jnp.bitwise_and(src, SRC_BLOCK - 1) * DST_BLOCK + jnp.bitwise_and(dst, DST_BLOCK - 1)
         keys, weights = lax.sort((keys, w), num_keys=1, is_stable=False)
-        cells = adjacency(keys, weights, slots, dsts)
+        keys, weights = keys.reshape(-1, LANES), weights.reshape(-1, LANES)
+        plan = edge_plan(keys, slots // SRC_BLOCK * (dsts // DST_BLOCK))
         raw = main_call(
-            groups, own, halo, hubs, cells, x.T, dy.T, send[None, :], hub_ids[None, :], b_first[None, :],
+            groups, own, halo, hubs, plan, keys, weights, x.T, dy.T, send[None, :], hub_ids[None, :], b_first[None, :],
             w_first, w_second.T)
         dx, gw1, gw2, gb1, gb2 = pl.pallas_call(
             output_kernel,

time: 98.8 us -> 91.4 us (0.925)
  Pallas kernels: 87.8 us -> 80.5 us
    pallas_call x1, Pallas kernels: 17.3 us -> 4.11 us  [edge_plan(): pl.pallas_call(functools.partial(plan_kernel, buckets), out_shape=jax.Sha...]
    pallas_call x1, Pallas kernels: 68.7 us -> 74.6 us  [main_call(): pl.pallas_call(functools.partial(main_kernel, groups, own, halo, hubs), o...]
where the time goes in v5:
time: 91.4 us; the launch traced here: 90.7 us
  Pallas kernels  80.5 us (88%)
  other arithmetic  9.56 us (10%)
    pallas_call x1, Pallas kernels, main_call(): pl.pallas_call(functools.partial(main_kernel, groups, own, halo, hubs), o...  74.6 us
    sort x1, other arithmetic, device_step(): keys, weights = lax.sort((keys, w), num_keys=1, is_stable=False)  8.51 us
    pallas_call x1, Pallas kernels, edge_plan(): pl.pallas_call(functools.partial(plan_kernel, buckets), out_shape=jax.Sha...  4.11 us

profile of v5, /device:TPU:1, one launch (start us, length us, event | category | flops | bytes accessed | tf_op | source)
XLA Modules:
  0.0 90.7 jit_solution(12004645978084266991)
XLA Ops:
  0.6 0.0 copy-start
  0.6 1.1 %and_add_fusion = s32[32768]{0:T(1024)S(1)} fusion(s32[32768]{0:T(1024)} %param.11, s32[32768]{0:T(1024)} %param.12), kind=kLoop, calls=%fused_computation | loop fusion | flops 327680 | bytes 393216 | tf_op jit(solution)/shard_map/add | solution.py:446
  1.7 0.0 copy-done
  1.7 8.5 %sort.15 = (s32[32768]{0:T(1024)}, f32[32768]{0:T(1024)}) sort(s32[32768]{0:T(1024)S(1)} %and_add_fusion, f32[32768]{0:T(1024)S(1)} %copy-done), dimensions={0}, to_apply=%region_0.0 | sort | flops 491520 | bytes 524288 | tf_op jit(solution)/shard_map/sort | solution.py:447
  10.2 4.1 %edge_plan.1.plan_ref = s32[4,256]{1,0:T(4,128)} custom-call(s32[256,128]{1,0:T(8,128)} %bitcast.12), custom_call_target="tpu_custom_call" | custom-call | tf_op jit(solution)/shard_map/edge_plan/pallas_call | solution.py:141
  14.3 74.6 %main_exchange.1 = (f32[128,512]{1,0:T(8,128)}, f32[128,1,512]{2,1,0:T(1,128)}, f32[1,384]{1,0:T(1,128)}) custom-call(s32[4,256]{1,0:T(4,128)} %edge_plan.1.plan_ref, s32[256,128]{1,0:T(8,128)} %bitcast.13, f32[256,128]{1,0:T(8,128)} %bitcast.14, bf16[100,512]{1,0:T(8,128)(2,1)} %bitcast.15, f32[47,512]{1,0:T(8,128)} %bitcast.16, s32[1,256]{1,0:T(1,128)} %bitcast.18, ...), custom_call_target="tpu_custom_call" | custom-call | tf_op jit(solution)/shard_map/main_exchange/pallas_call | solution.py:403
  88.9 1.8 %outputs.1 = (f32[100,512]{1,0:T(8,128)}, f32[100,256]{1,0:T(8,128)}, f32[47,256]{1,0:T(8,128)}, f32[1,256]{1,0:T(1,128)}, f32[1,47]{1,0:T(1,128)}) custom-call(f32[128,512]{1,0:T(8,128)} %get-tuple-element.17.dxt_ref, f32[128,1,512]{2,1,0:T(1,128)} %get-tuple-element.18.gw_ref, f32[1,384]{1,0:T(1,128)} %get-tuple-element.19.bias_ref), custom_call_target="tpu_custom_call" | custom-call | tf_op jit(solution)/shard_map/outputs/pallas_call | solution.py:453
Async XLA Ops:
  0.6 1.1 %copy-start = (f32[32768]{0:T(1024)S(1)}, f32[32768]{0:T(1024)}, u32[]{:S(2)}) copy-start(f32[32768]{0:T(1024)} %param.13) | copy-start | bytes 393220

commit v6 on v5

--- a/solution.py
+++ b/solution.py
@@ -31,10 +31,6 @@
 
 def exact3_right(pieces, sel):
     return dot(pieces[2], sel) + dot(pieces[1], sel) + dot(pieces[0], sel)
-
-
-def sum3(pieces):
-    return pieces[2].astype(F32) + pieces[1].astype(F32) + pieces[0].astype(F32)
 
 
 def full6(a, b):
@@ -95,8 +91,7 @@
 
 SRC_BLOCK, DST_BLOCK = 128, 256
 BUCKET = SRC_BLOCK * DST_BLOCK
-CHUNK_ROWS, UNROLL = 2, 8
-STEPS_BEFORE, STEPS_MIDDLE = 3, 10
+CHUNK_ROWS, UNROLL = 2, 19
 
 
 def plan_kernel(buckets, key_ref, plan_ref, bound_ref):
@@ -202,7 +197,7 @@
     me = lax.axis_index("graph")
     barrier = greet_all(groups, me)
     steps = (cum_ref.shape[0] - 1) // UNROLL
-    before, middle = steps * STEPS_BEFORE // 19, steps * STEPS_MIDDLE // 19
+    before, middle = steps // 4, steps * 7 // 8
     cum_ref[0] = jnp.zeros((SRC_BLOCK, DST_BLOCK), F32)
 
     lane = lax.broadcasted_iota(jnp.int32, (1, LANES), 1)
@@ -231,7 +226,7 @@
 
     w1 = padded(w1_ref, LANES, hid)
     w1_t = w1.astype(F32).T.astype(BF16)
-    zt_ref[:, :own] = dot(w1_t, xt).astype(BF16)
+    zt_ref[:, :own] = jnp.where(plain_row, dot(w1_t, xt), 0.0).astype(BF16)
     dy = dyt.T
     add_pairs(plan_ref, key_ref, w_ref, cum_ref, before, middle)
     wait_all(groups, rx, rcv[0], True)
@@ -243,43 +238,42 @@
     send_all(groups, me, [("b", hx, gx, snd[2], rcv[2]), ("b", hd, gd, snd[3], rcv[3])])
 
     home_x = jnp.concatenate([home_x, jnp.zeros((8 - per, LANES), F32)], axis=0).astype(BF16)
-    halo_x = got[:, :per, :].reshape(halo, LANES)
-    halo_code = halo_x[:, feat_in:feat_in + 1]
-    halo_x = halo_x.astype(BF16)
-    zt_ref[:, own:first_hub] = dot(w1_t, halo_x, 1, 1).astype(BF16)
+    add_pairs(plan_ref, key_ref, w_ref, cum_ref, middle, steps)
+
+    def renamed(i):
+        cell = [cum_ref[plan_ref[3, i * tops + j]] for j in range(tops)]
+        mine = jnp.concatenate(cell[:own // DST_BLOCK], axis=1)
+        pieces = split3(mine)
+        return mine, pieces, jnp.concatenate(cell[own // DST_BLOCK:], axis=1) + exact3_right(pieces, sel_t)
+
+    def rename(i, carry):
+        _, pieces, hub = renamed(i)
+        rows = pl.ds(pl.multiple_of(i * SRC_BLOCK, SRC_BLOCK), SRC_BLOCK)
+        for ref, left, right in zip(adj, pieces, split3(hub)):
+            ref[rows, :own] = left
+            ref[rows, own:] = right
+        return carry
+
+    def rename_hub(i, carry):
+        mine, _, hub = renamed(first_hub // SRC_BLOCK + i)
+        rows = pl.ds(pl.multiple_of(i * SRC_BLOCK, SRC_BLOCK), SRC_BLOCK)
+        hubrow_ref[rows, :own] = mine
+        hubrow_ref[rows, own:] = hub
+        return carry
+
+    lax.fori_loop(0, first_hub // SRC_BLOCK, rename, 0)
+    lax.fori_loop(0, hubs // SRC_BLOCK, rename_hub, 0)
+    halo_x = got[:, :per, :].reshape(halo, LANES).astype(BF16)
     column = jnp.broadcast_to(jnp.where(lane == feat_in, 1.0, 0.0), (8, LANES)).astype(BF16)
     halo_row = dot(column, halo_x, 1, 1)[:1].astype(jnp.int32)
-    halo_sel = (lax.broadcasted_iota(jnp.int32, (hubs, 1), 0) + 1 == halo_row).astype(F32).astype(BF16)
-    add_pairs(plan_ref, key_ref, w_ref, cum_ref, middle, steps)
-
-    def rename(i, carry):
-        cell = [cum_ref[plan_ref[3, i * tops + j]] for j in range(tops)]
-        mine = jnp.concatenate(cell[:own // DST_BLOCK], axis=1)
-        hub = jnp.concatenate(cell[own // DST_BLOCK:], axis=1) + exact3_right(split3(mine), sel_t)
-        rows = pl.ds(pl.multiple_of(i * SRC_BLOCK, SRC_BLOCK), SRC_BLOCK)
-        new = jnp.concatenate([jnp.where(plain_row, mine, 0.0), hub], axis=1)
-        for ref, piece in zip(adj, split3(new)):
-            ref[rows, :] = piece
-        return carry
-
-    lax.fori_loop(0, slots // SRC_BLOCK, rename, 0)
-    sel = sel_f.T.astype(BF16)
+    zt_ref[:, own:first_hub] = jnp.where(halo_row == 0, dot(w1_t, halo_x, 1, 1), 0.0).astype(BF16)
+    halo_sel = (lax.broadcasted_iota(jnp.int32, (hubs, 1), 0) + 1 == halo_row).astype(F32)
+    moved = jnp.concatenate([sel_f.T, halo_sel], axis=1).astype(BF16)
     for j in range(tops):
         cols = slice(j * DST_BLOCK, (j + 1) * DST_BLOCK)
-        base = first_hub // SRC_BLOCK
-        old = jnp.concatenate(
-            [sum3([a[(base + k) * SRC_BLOCK:(base + k + 1) * SRC_BLOCK, cols] for a in adj])
-             for k in range(hubs // SRC_BLOCK)], axis=0)
-        hubrow_ref[:, cols] = old + exact3(sel, [a[:own, cols] for a in adj])
-    for a in adj:
-        a[:own, :] = jnp.where(plain, a[:own, :].astype(F32), 0.0).astype(BF16)
-    for j in range(tops):
-        cols = slice(j * DST_BLOCK, (j + 1) * DST_BLOCK)
-        new = hubrow_ref[:, cols] + exact3(halo_sel, [a[own:first_hub, cols] for a in adj])
+        new = hubrow_ref[:, cols] + exact3(moved, [a[:first_hub, cols] for a in adj])
         for a, piece in zip(adj, split3(new)):
             a[first_hub:, cols] = piece
-    for a in adj:
-        a[own:first_hub, :] = jnp.where(halo_code == 0, a[own:first_hub, :].astype(F32), 0.0).astype(BF16)
 
     def forward(rows, cols):
         zt = zt_ref[:, rows]
@@ -296,26 +290,26 @@
         return jnp.where(half, t + pltpu.roll(t, LANES // 2, 1), 0.0)
 
     own_cols, hub_cols = slice(0, own), slice(own, dsts)
-    pt_ref[...] = forward(slice(0, first_hub), slice(0, dsts))
-    d_own = pack(dy)
-    g2_ref[...] = grad_out_sums(slice(0, slots), own_cols, d_own)
+    pt_ref[...] = forward(slice(0, first_hub), hub_cols)
+    d_own = pack(jnp.where(plain, dy, 0.0))
+    g2_ref[...] = grad_out_sums(slice(own, slots), own_cols, d_own)
     wait_all(groups, gx, rcv[2], True)
     wait_all(groups, gd, rcv[3], True)
     hub_x = gx[...].astype(F32).reshape(hubs, LANES).astype(BF16)
     zt_ref[:, first_hub:] = dot(w1_t, hub_x, 1, 1).astype(BF16)
     d_hub = pack(gd[...].reshape(hubs, LANES))
     hub_slots = slice(first_hub, slots)
-    y_hub = (pt_ref[:, own:] + forward(hub_slots, hub_cols)).T
+    y_hub = (pt_ref[...] + forward(hub_slots, hub_cols)).T
     s1[:, :, LANES:] = rows_to_blocks(y_hub, groups)
-    g2_halo = g2_ref[own:first_hub, :] + grad_out_sums(slice(own, first_hub), hub_cols, d_hub)
-    g2_hub = g2_ref[first_hub:, :] + grad_out_sums(hub_slots, hub_cols, d_hub)
+    g2_halo = g2_ref[:halo, :] + grad_out_sums(slice(own, first_hub), hub_cols, d_hub)
+    g2_hub = g2_ref[halo:, :] + grad_out_sums(hub_slots, hub_cols, d_hub)
     s1[:, :, :LANES] = rows_to_blocks(g2_halo + pltpu.roll(g2_hub, LANES // 2, 1), groups)
     send_all(groups, me, [("a", s1, r1, snd[4], rcv[4])])
 
     b1 = b1_ref[...]
     w2t = padded(w2t_ref, LANES, hid)
-    pre = (pt_ref[:, :own] + forward(hub_slots, own_cols)).T + b1
-    g2_own = g2_ref[:own, :] + grad_out_sums(slice(0, own), hub_cols, d_hub)
+    pre = forward(slice(0, slots), own_cols).T + b1
+    g2_own = grad_out_sums(slice(0, own), own_cols, d_own) + grad_out_sums(slice(0, own), hub_cols, d_hub)
     hidden = jnp.where(plain, jax.nn.relu(pre), 0.0).astype(BF16)
     live = plain & (pre > 0)
     wait_all(groups, r1, rcv[4], True)
@@ -329,7 +323,7 @@
     send_all(groups, me, [("b", s2, r2, snd[5], rcv[5])])
 
     back = jnp.where(half, r1[:, :, :LANES].reshape(halo, LANES), 0.0)
-    dz2 = (g2_own + exact3(pick_t, split3(back))).astype(BF16)
+    dz2 = jnp.where(plain, g2_own + exact3(pick_t, split3(back)), 0.0).astype(BF16)
     dy1 = jnp.where(live, dot(dz2, w2t), 0.0)
     home_hidden = jax.nn.relu(home_pre).astype(BF16)
     gw2 = dot(dz2, hidden, 0, 0) + dot(home_dz2, home_hidden, 0, 0)
@@ -381,7 +375,7 @@
 
     wait_all(groups, r7, rcv[10], True)
     hub_dx = r7[...].reshape(hubs, LANES).T
-    dxt_ref[...] = dxt + exact3_right(split3(hub_dx), sel)
+    dxt_ref[...] = dxt + exact3_right(split3(hub_dx), sel_f.T.astype(BF16))
     for buf, sem in zip((rx, rd, gx, gd, r1, r2, r3, r4, r5, r6, r7, gw_ref), snd):
         wait_all(groups, buf, sem, False)
     wait_all(groups, gw_ref, rcv[11], True)
@@ -411,8 +405,8 @@
             pltpu.VMEM((slots, dsts), BF16),
             pltpu.VMEM((slots, dsts), BF16),
             pltpu.VMEM((hubs, dsts), F32),
-            pltpu.VMEM((hid, dsts), F32),
-            pltpu.VMEM((slots, LANES), F32),
+            pltpu.VMEM((hid, hubs), F32),
+            pltpu.VMEM((slots - own, LANES), F32),
             pltpu.VMEM((slots, hid), F32),
             pltpu.VMEM((3, dsts, hid), BF16),
             pltpu.VMEM((hid, slots), BF16),

time: 91.4 us -> 86.4 us (0.945)
  Pallas kernels: 80.5 us -> 75.9 us
    pallas_call x1, Pallas kernels: 74.6 us -> 70 us  [main_call(): pl.pallas_call(functools.partial(main_kernel, groups, own, halo, hubs), o...]
where the time goes in v6:
time: 86.4 us; the launch traced here: 86.1 us
  Pallas kernels  75.9 us (88%)
  other arithmetic  9.56 us (11%)
    pallas_call x1, Pallas kernels, main_call(): pl.pallas_call(functools.partial(main_kernel, groups, own, halo, hubs), o...  70 us
    sort x1, other arithmetic, device_step(): keys, weights = lax.sort((keys, w), num_keys=1, is_stable=False)  8.51 us
    pallas_call x1, Pallas kernels, edge_plan(): pl.pallas_call(functools.partial(plan_kernel, buckets), out_shape=jax.Sha...  4.11 us
    pallas_call x1, Pallas kernels, device_step(): pl.pallas_call(output_kernel, out_shape=[jax.ShapeDtypeStruct(shape, F32)...  1.8 us

profile of v6, /device:TPU:1, one launch (start us, length us, event | category | flops | bytes accessed | tf_op | source)
XLA Modules:
  0.0 86.1 jit_solution(16849472826738071525)
XLA Ops:
  0.6 0.0 copy-start
  0.6 1.1 %and_add_fusion = s32[32768]{0:T(1024)S(1)} fusion(s32[32768]{0:T(1024)} %param.11, s32[32768]{0:T(1024)} %param.12), kind=kLoop, calls=%fused_computation | loop fusion | flops 327680 | bytes 393216 | tf_op jit(solution)/shard_map/add | solution.py:440
  1.7 0.0 copy-done
  1.7 8.5 %sort.15 = (s32[32768]{0:T(1024)}, f32[32768]{0:T(1024)}) sort(s32[32768]{0:T(1024)S(1)} %and_add_fusion, f32[32768]{0:T(1024)S(1)} %copy-done), dimensions={0}, to_apply=%region_0.0 | sort | flops 491520 | bytes 524288 | tf_op jit(solution)/shard_map/sort | solution.py:441
  10.2 4.1 %edge_plan.1.plan_ref = s32[4,256]{1,0:T(4,128)} custom-call(s32[256,128]{1,0:T(8,128)} %bitcast.12), custom_call_target="tpu_custom_call" | custom-call | tf_op jit(solution)/shard_map/edge_plan/pallas_call | solution.py:136
  14.3 70.0 %main_exchange.1 = (f32[128,512]{1,0:T(8,128)}, f32[128,1,512]{2,1,0:T(1,128)}, f32[1,384]{1,0:T(1,128)}) custom-call(s32[4,256]{1,0:T(4,128)} %edge_plan.1.plan_ref, s32[256,128]{1,0:T(8,128)} %bitcast.13, f32[256,128]{1,0:T(8,128)} %bitcast.14, bf16[100,512]{1,0:T(8,128)(2,1)} %bitcast.15, f32[47,512]{1,0:T(8,128)} %bitcast.16, s32[1,256]{1,0:T(1,128)} %bitcast.18, ...), custom_call_target="tpu_custom_call" | custom-call | tf_op jit(solution)/shard_map/main_exchange/pallas_call | solution.py:397
  84.3 1.8 %outputs.1 = (f32[100,512]{1,0:T(8,128)}, f32[100,256]{1,0:T(8,128)}, f32[47,256]{1,0:T(8,128)}, f32[1,256]{1,0:T(1,128)}, f32[1,47]{1,0:T(1,128)}) custom-call(f32[128,512]{1,0:T(8,128)} %get-tuple-element.17.dxt_ref, f32[128,1,512]{2,1,0:T(1,128)} %get-tuple-element.18.gw_ref, f32[1,384]{1,0:T(1,128)} %get-tuple-element.19.bias_ref), custom_call_target="tpu_custom_call" | custom-call | tf_op jit(solution)/shard_map/outputs/pallas_call | solution.py:447
Async XLA Ops:
  0.6 1.1 %copy-start = (f32[32768]{0:T(1024)S(1)}, f32[32768]{0:T(1024)}, u32[]{:S(2)}) copy-start(f32[32768]{0:T(1024)} %param.13) | copy-start | bytes 393220

commit v7 on v6

--- a/solution.py
+++ b/solution.py
@@ -94,53 +94,45 @@
 CHUNK_ROWS, UNROLL = 2, 19
 
 
-def plan_kernel(buckets, key_ref, plan_ref, bound_ref):
+def ring_sum(a, axis):
+    step = a.shape[axis] // 2
+    while step:
+        a = a + pltpu.roll(a, step, axis)
+        step //= 2
+    return a
+
+
+def list_pairs(buckets, key_ref, plan_ref):
     size = CHUNK_ROWS * LANES
+    shift = size.bit_length() - 1
+    total = 1 << buckets.bit_length()
 
     def count(i, carry):
         bucket = jnp.right_shift(key_ref[pl.ds(pl.multiple_of(i * 8, 8), 8), :], BUCKET.bit_length() - 1)
-        return tuple(c + jnp.where(bucket < b + 1, 1, 0) for b, c in enumerate(carry))
-
-    zeros = jnp.zeros((8, LANES), jnp.int32)
-    counts = lax.fori_loop(0, key_ref.shape[0] // 8, count, (zeros,) * buckets)
-    bound_ref[0] = 0
-    for b, c in enumerate(counts):
-        bound_ref[b + 1] = jnp.sum(c.astype(F32)).astype(jnp.int32)
-
-    def put(at, bucket, chunk, same):
-        plan_ref[0, at] = bucket
-        plan_ref[1, at] = chunk
-        plan_ref[2, at] = same
-
-    def list_pairs(b, at):
-        low, high = bound_ref[b], bound_ref[b + 1]
-        start = low // size
-        pairs = jnp.where(high > low, (high + size - 1) // size - start, 0)
-        plan_ref[3, b] = jnp.where(pairs > 0, at + pairs, 0)
-
-        def pair(i, carry):
-            put(at + i, b, start + i, jnp.where(i > 0, 1, 0))
-            return carry
-
-        lax.fori_loop(0, pairs, pair, 0)
-        return at + pairs
-
-    def rest(i, carry):
-        put(i, buckets, 0, 0)
-        return carry
-
-    lax.fori_loop(lax.fori_loop(0, buckets, list_pairs, 0), key_ref.shape[0] // CHUNK_ROWS + buckets, rest, 0)
-
-
-def edge_plan(keys, buckets):
-    return pl.pallas_call(
-        functools.partial(plan_kernel, buckets),
-        out_shape=jax.ShapeDtypeStruct((4, 256), jnp.int32),
-        in_specs=[pl.BlockSpec(memory_space=pltpu.VMEM)],
-        out_specs=pl.BlockSpec(memory_space=pltpu.SMEM),
-        scratch_shapes=[pltpu.SMEM((buckets + 1,), jnp.int32)],
-        name="edge_plan",
-    )(keys)
+        return tuple(c + jnp.where(bucket <= b, 1, 0) for b, c in enumerate(carry))
+
+    counts = lax.fori_loop(0, key_ref.shape[0] // 8, count, (jnp.zeros((8, LANES), jnp.int32),) * buckets)
+    counts = [ring_sum(c, 0)[:1] for c in counts]
+    none = jnp.zeros((1, LANES), jnp.int32)
+    counts = [none] + counts + [counts[-1]] * (total - buckets)
+    low = ring_sum(jnp.concatenate(counts[:total], axis=0), 1)
+    high = ring_sum(jnp.concatenate(counts[1:], axis=0), 1)
+    start = jnp.right_shift(low, shift)
+    pairs = jnp.where(high > low, jnp.right_shift(high + size - 1, shift) - start, 0)
+    row = lax.broadcasted_iota(jnp.int32, (total, LANES), 0)
+    last, step = pairs, 1
+    while step < total:
+        last = last + jnp.where(row >= step, pltpu.roll(last, step, 0), 0)
+        step *= 2
+    first = last - pairs
+    for half in range(plan_ref.shape[1] // LANES):
+        at = lax.broadcasted_iota(jnp.int32, (total, LANES), 1) + half * LANES
+        inside = (first <= at) & (at < last)
+        rows = [
+            jnp.where(last <= at, 1, 0), jnp.where(inside, start + at - first, 0), jnp.where(inside & (at > first), 1, 0),
+            jnp.where((row == at) & (pairs > 0), last, 0)]
+        rows = [ring_sum(r, 0)[:1] for r in rows] + [none] * 4
+        plan_ref[:, half * LANES:(half + 1) * LANES] = jnp.concatenate(rows, axis=0)
 
 
 def add_pairs(plan_ref, key_ref, w_ref, cum_ref, low, high):
@@ -180,11 +172,11 @@
     return a.reshape(groups, a.shape[0] // groups, a.shape[1])
 
 
-def main_kernel(groups, own, halo, hubs, plan_ref, key_ref, w_ref, xt_ref, dyt_ref, send_ref, hub_ref, b1_ref, w1_ref, w2t_ref,
+def main_kernel(groups, own, halo, hubs, key_ref, w_ref, xt_ref, dyt_ref, send_ref, hub_ref, b1_ref, w1_ref, w2t_ref,
                 dxt_ref, gw_ref, bias_ref,
                 sx, sd, hx, hd, s1, s2, s3, s4, s5, s6, s7, s8,
                 rx, rd, gx, gd, r1, r2, r3, r4, r5, r6, r7,
-                cum_ref, hi_ref, mid_ref, low_ref, hubrow_ref, pt_ref, g2_ref, g1_ref, dy_ref, zt_ref, *sems):
+                list_ref, plan_ref, cum_ref, hi_ref, mid_ref, low_ref, hubrow_ref, pt_ref, g2_ref, g1_ref, dy_ref, zt_ref, plan_sem, *sems):
     count = len(sems) // 2
     snd, rcv = sems[:count], sems[count:]
     adj = (hi_ref, mid_ref, low_ref)
@@ -199,6 +191,9 @@
     steps = (cum_ref.shape[0] - 1) // UNROLL
     before, middle = steps // 4, steps * 7 // 8
     cum_ref[0] = jnp.zeros((SRC_BLOCK, DST_BLOCK), F32)
+    list_pairs(slots // SRC_BLOCK * tops, key_ref, list_ref)
+    plan = pltpu.make_async_copy(list_ref, plan_ref, plan_sem)
+    plan.start()
 
     lane = lax.broadcasted_iota(jnp.int32, (1, LANES), 1)
     half = lane < LANES // 2
@@ -220,6 +215,7 @@
     sx[:, :per, :] = rows_to_blocks(picked[:LANES, :halo].T, groups).astype(BF16)
     sx[:, per:, :] = rows_to_blocks(picked[:LANES, halo:].T, groups).astype(BF16)
     sd[...] = rows_to_blocks(hub_dt.T, groups)
+    plan.wait()
     add_pairs(plan_ref, key_ref, w_ref, cum_ref, 0, before)
     pl.semaphore_wait(barrier, groups - 1)
     send_all(groups, me, [("a", sx, rx, snd[0], rcv[0]), ("a", sd, rd, snd[1], rcv[1])])
@@ -382,10 +378,10 @@
 
 
 def main_call(groups, own, halo, hubs, *args):
-    hid = args[7].shape[1]
+    hid = args[6].shape[1]
     per = hubs // groups
     slots, dsts = own + halo + hubs, own + hubs
-    pairs = args[1].shape[0] // CHUNK_ROWS + slots // SRC_BLOCK * (dsts // DST_BLOCK)
+    pairs = args[0].shape[0] // CHUNK_ROWS + slots // SRC_BLOCK * (dsts // DST_BLOCK)
     vmem = pl.BlockSpec(memory_space=pltpu.VMEM)
     blocks = [
         ("a", (2 * per, LANES), BF16), ("a", (per, LANES), F32), ("b", (per, LANES), BF16), ("b", (per, LANES), F32),
@@ -397,9 +393,11 @@
     return pl.pallas_call(
         functools.partial(main_kernel, groups, own, halo, hubs),
         out_shape=[shape((LANES, own), F32), shape((groups, 1, 2 * hid), F32), shape((1, hid + LANES), F32)],
-        in_specs=[pl.BlockSpec(memory_space=pltpu.SMEM)] + [vmem] * (len(args) - 1),
+        in_specs=[vmem] * len(args),
         out_specs=[vmem] * 3,
         scratch_shapes=sends + recvs + [
+            pltpu.VMEM((8, 256), jnp.int32),
+            pltpu.SMEM((8, 256), jnp.int32),
             pltpu.VMEM((pairs + 1, SRC_BLOCK, DST_BLOCK), F32),
             pltpu.VMEM((slots, dsts), BF16),
             pltpu.VMEM((slots, dsts), BF16),
@@ -410,7 +408,7 @@
             pltpu.VMEM((slots, hid), F32),
             pltpu.VMEM((3, dsts, hid), BF16),
             pltpu.VMEM((hid, slots), BF16),
-        ] + [pltpu.SemaphoreType.DMA] * (2 * len(blocks)),
+        ] + [pltpu.SemaphoreType.DMA] * (1 + 2 * len(blocks)),
         compiler_params=pltpu.CompilerParams(collective_id=0, has_side_effects=True, vmem_limit_bytes=56 * 2 ** 20),
         name="main_exchange",
     )(*args)
@@ -440,9 +438,8 @@
         keys = bucket * BUCKET + jnp.bitwise_and(src, SRC_BLOCK - 1) * DST_BLOCK + jnp.bitwise_and(dst, DST_BLOCK - 1)
         keys, weights = lax.sort((keys, w), num_keys=1, is_stable=False)
         keys, weights = keys.reshape(-1, LANES), weights.reshape(-1, LANES)
-        plan = edge_plan(keys, slots // SRC_BLOCK * (dsts // DST_BLOCK))
         raw = main_call(
-            groups, own, halo, hubs, plan, keys, weights, x.T, dy.T, send[None, :], hub_ids[None, :], b_first[None, :],
+            groups, own, halo, hubs, keys, weights, x.T, dy.T, send[None, :], hub_ids[None, :], b_first[None, :],
             w_first, w_second.T)
         dx, gw1, gw2, gb1, gb2 = pl.pallas_call(
             output_kernel,

time: 86.4 us -> 82.8 us (0.958)
  Pallas kernels: 75.9 us -> 71.6 us
    pallas_call x1 -> x0, Pallas kernels: 4.11 us -> none  [edge_plan(): pl.pallas_call(functools.partial(plan_kernel, buckets), out_shape=jax.Sha...]
where the time goes in v7:
time: 82.8 us; the launch traced here: 81.8 us
  Pallas kernels  71.6 us (86%)
  other arithmetic  9.56 us (12%)
    pallas_call x1, Pallas kernels, main_call(): pl.pallas_call(functools.partial(main_kernel, groups, own, halo, hubs), o...  69.8 us
    sort x1, other arithmetic, device_step(): keys, weights = lax.sort((keys, w), num_keys=1, is_stable=False)  8.51 us
    pallas_call x1, Pallas kernels, device_step(): pl.pallas_call(output_kernel, out_shape=[jax.ShapeDtypeStruct(shape, F32)...  1.8 us

profile of v7, /device:TPU:1, one launch (start us, length us, event | category | flops | bytes accessed | tf_op | source)
XLA Modules:
  0.0 81.8 jit_solution(11476356984581195127)
XLA Ops:
  0.6 0.0 copy-start
  0.6 1.1 %and_add_fusion = s32[32768]{0:T(1024)S(1)} fusion(s32[32768]{0:T(1024)} %param.11, s32[32768]{0:T(1024)} %param.12), kind=kLoop, calls=%fused_computation | loop fusion | flops 327680 | bytes 393216 | tf_op jit(solution)/shard_map/add | solution.py:438
  1.7 0.0 copy-done
  1.7 8.5 %sort.15 = (s32[32768]{0:T(1024)}, f32[32768]{0:T(1024)}) sort(s32[32768]{0:T(1024)S(1)} %and_add_fusion, f32[32768]{0:T(1024)S(1)} %copy-done), dimensions={0}, to_apply=%region_0.0 | sort | flops 491520 | bytes 524288 | tf_op jit(solution)/shard_map/sort | solution.py:439
  10.2 69.8 %main_exchange.1 = (f32[128,512]{1,0:T(8,128)}, f32[128,1,512]{2,1,0:T(1,128)}, f32[1,384]{1,0:T(1,128)}) custom-call(s32[256,128]{1,0:T(8,128)} %bitcast.12, f32[256,128]{1,0:T(8,128)} %bitcast.13, bf16[100,512]{1,0:T(8,128)(2,1)} %bitcast.14, f32[47,512]{1,0:T(8,128)} %bitcast.15, s32[1,256]{1,0:T(1,128)} %bitcast.17, s32[1,256]{1,0:T(1,128)} %bitcast.18, ...), custom_call_target="tpu_custom_call" | custom-call | tf_op jit(solution)/shard_map/main_exchange/pallas_call | solution.py:393
  80.0 1.8 %outputs.1 = (f32[100,512]{1,0:T(8,128)}, f32[100,256]{1,0:T(8,128)}, f32[47,256]{1,0:T(8,128)}, f32[1,256]{1,0:T(1,128)}, f32[1,47]{1,0:T(1,128)}) custom-call(f32[128,512]{1,0:T(8,128)} %get-tuple-element.17.dxt_ref, f32[128,1,512]{2,1,0:T(1,128)} %get-tuple-element.18.gw_ref, f32[1,384]{1,0:T(1,128)} %get-tuple-element.19.bias_ref), custom_call_target="tpu_custom_call" | custom-call | tf_op jit(solution)/shard_map/outputs/pallas_call | solution.py:444
Async XLA Ops:
  0.6 1.1 %copy-start = (f32[32768]{0:T(1024)S(1)}, f32[32768]{0:T(1024)}, u32[]{:S(2)}) copy-start(f32[32768]{0:T(1024)} %param.13) | copy-start | bytes 393220

commit v8 on v7

--- a/solution.py
+++ b/solution.py
@@ -91,7 +91,52 @@
 
 SRC_BLOCK, DST_BLOCK = 128, 256
 BUCKET = SRC_BLOCK * DST_BLOCK
-CHUNK_ROWS, UNROLL = 2, 19
+CHUNK, UNROLL = 256, 19
+
+
+def bitonic(keys, weights, low, high):
+    vregs = keys.shape[0]
+    base = vregs.bit_length() - 1
+
+    def bit(shape, m):
+        axis, m = (len(shape) - 2, m - base) if m < base + 3 else (len(shape) - 1, m - base - 3)
+        return jnp.bitwise_and(jnp.right_shift(lax.broadcasted_iota(jnp.int32, shape, axis), m), 1)
+
+    def other(a, j):
+        if j >= base + 3:
+            lane = lax.broadcasted_iota(jnp.int32, (vregs * 8, LANES), 1)
+            return jnp.take_along_axis(
+                a.reshape(vregs * 8, LANES), jnp.bitwise_xor(lane, 1 << (j - base - 3)), axis=1).reshape(a.shape)
+        step = 1 << (j - base)
+        if step == 4:
+            return pltpu.roll(a, 4, 1)
+        return jnp.where(bit(a.shape, j) > 0, pltpu.roll(a, step, 1), pltpu.roll(a, 8 - step, 1))
+
+    full = keys.shape
+    for k in range(low, high + 1):
+        for j in range(k - 1, -1, -1):
+            if j < base:
+                near = 1 << j
+                parts = (vregs // (2 * near), 2, near, 8, LANES)
+                a, b = keys.reshape(parts)[:, 0], keys.reshape(parts)[:, 1]
+                wa, wb = weights.reshape(parts)[:, 0], weights.reshape(parts)[:, 1]
+                swap = a > b
+                if k < base:
+                    block = lax.broadcasted_iota(jnp.int32, a.shape, 0)
+                    swap = jnp.logical_xor(swap, jnp.bitwise_and(jnp.right_shift(block, k - j - 1), 1) > 0)
+                elif k < base + 10:
+                    swap = jnp.logical_xor(swap, bit(a.shape, k) > 0)
+                keys = jnp.stack([jnp.where(swap, b, a), jnp.where(swap, a, b)], axis=1).reshape(full)
+                weights = jnp.stack([jnp.where(swap, wb, wa), jnp.where(swap, wa, wb)], axis=1).reshape(full)
+            else:
+                keys2, weights2 = other(keys, j), other(weights, j)
+                upper = bit(full, j)
+                if k < base + 10:
+                    upper = jnp.bitwise_xor(upper, bit(full, k))
+                take = jnp.bitwise_xor(keys2, -upper) < jnp.bitwise_xor(keys, -upper)
+                keys = jnp.where(take, keys2, keys)
+                weights = jnp.where(take, weights2, weights)
+    return keys, weights
 
 
 def ring_sum(a, axis):
@@ -103,7 +148,7 @@
 
 
 def list_pairs(buckets, key_ref, plan_ref):
-    size = CHUNK_ROWS * LANES
+    size = CHUNK
     shift = size.bit_length() - 1
     total = 1 << buckets.bit_length()
 
@@ -144,11 +189,12 @@
         work = []
         for u in range(UNROLL):
             b, c = plan_ref[0, it * UNROLL + u], plan_ref[1, it * UNROLL + u]
+            rel_row = key_ref[pl.ds(c, 1), :] - b * BUCKET
+            w_row = w_ref[pl.ds(c, 1), :]
             lhs, rhs = [], []
-            for r in range(CHUNK_ROWS):
-                rel = key_ref[pl.ds(c * CHUNK_ROWS + r, 1), :] - b * BUCKET
-                weight = w_ref[pl.ds(c * CHUNK_ROWS + r, 1), :]
-                src = jnp.right_shift(rel, 8)
+            for r in range(0, CHUNK, LANES):
+                rel, weight = rel_row[:, r:r + LANES], w_row[:, r:r + LANES]
+                src = jnp.right_shift(rel, DST_BLOCK.bit_length() - 1)
                 src = jnp.where((src >= 0) & (src < SRC_BLOCK), src, 512).astype(F32).astype(BF16)
                 dst = jnp.bitwise_and(rel, DST_BLOCK - 1).astype(F32).astype(BF16)
                 hit = src_ids == jnp.broadcast_to(src, src_ids.shape)
@@ -172,11 +218,11 @@
     return a.reshape(groups, a.shape[0] // groups, a.shape[1])
 
 
-def main_kernel(groups, own, halo, hubs, key_ref, w_ref, xt_ref, dyt_ref, send_ref, hub_ref, b1_ref, w1_ref, w2t_ref,
+def main_kernel(groups, own, halo, hubs, dst_ref, src_ref, w_in_ref, xt_ref, dyt_ref, send_ref, hub_ref, b1_ref, w1_ref, w2t_ref,
                 dxt_ref, gw_ref, bias_ref,
                 sx, sd, hx, hd, s1, s2, s3, s4, s5, s6, s7, s8,
                 rx, rd, gx, gd, r1, r2, r3, r4, r5, r6, r7,
-                list_ref, plan_ref, cum_ref, hi_ref, mid_ref, low_ref, hubrow_ref, pt_ref, g2_ref, g1_ref, dy_ref, zt_ref, plan_sem, *sems):
+                list_ref, plan_ref, raw_ref, sort_k, sort_w, key_ref, w_ref, cum_ref, hi_ref, mid_ref, low_ref, hubrow_ref, pt_ref, g2_ref, g1_ref, dy_ref, zt_ref, plan_sem, *sems):
     count = len(sems) // 2
     snd, rcv = sems[:count], sems[count:]
     adj = (hi_ref, mid_ref, low_ref)
@@ -189,9 +235,13 @@
     me = lax.axis_index("graph")
     barrier = greet_all(groups, me)
     steps = (cum_ref.shape[0] - 1) // UNROLL
-    before, middle = steps // 4, steps * 7 // 8
+    middle = steps * 3 // 8
     cum_ref[0] = jnp.zeros((SRC_BLOCK, DST_BLOCK), F32)
-    list_pairs(slots // SRC_BLOCK * tops, key_ref, list_ref)
+    dst, src = dst_ref[...], src_ref[...]
+    bucket = jnp.right_shift(src, SRC_BLOCK.bit_length() - 1) * tops + jnp.right_shift(dst, DST_BLOCK.bit_length() - 1)
+    raw_ref[...] = (
+        bucket * BUCKET + jnp.bitwise_and(src, SRC_BLOCK - 1) * DST_BLOCK + jnp.bitwise_and(dst, DST_BLOCK - 1))
+    list_pairs(slots // SRC_BLOCK * tops, raw_ref, list_ref)
     plan = pltpu.make_async_copy(list_ref, plan_ref, plan_sem)
     plan.start()
 
@@ -215,8 +265,9 @@
     sx[:, :per, :] = rows_to_blocks(picked[:LANES, :halo].T, groups).astype(BF16)
     sx[:, per:, :] = rows_to_blocks(picked[:LANES, halo:].T, groups).astype(BF16)
     sd[...] = rows_to_blocks(hub_dt.T, groups)
-    plan.wait()
-    add_pairs(plan_ref, key_ref, w_ref, cum_ref, 0, before)
+    phases = raw_ref.size.bit_length() - 1
+    sort_k[...], sort_w[...] = bitonic(
+        raw_ref[...].reshape(sort_k.shape), w_in_ref[...].reshape(sort_w.shape), 1, phases - 4)
     pl.semaphore_wait(barrier, groups - 1)
     send_all(groups, me, [("a", sx, rx, snd[0], rcv[0]), ("a", sd, rd, snd[1], rcv[1])])
 
@@ -224,7 +275,11 @@
     w1_t = w1.astype(F32).T.astype(BF16)
     zt_ref[:, :own] = jnp.where(plain_row, dot(w1_t, xt), 0.0).astype(BF16)
     dy = dyt.T
-    add_pairs(plan_ref, key_ref, w_ref, cum_ref, before, middle)
+    keys, weights = bitonic(sort_k[...], sort_w[...], phases - 3, phases)
+    key_ref[...] = keys.reshape(raw_ref.shape).T
+    w_ref[...] = weights.reshape(raw_ref.shape).T
+    plan.wait()
+    add_pairs(plan_ref, key_ref, w_ref, cum_ref, 0, middle)
     wait_all(groups, rx, rcv[0], True)
     wait_all(groups, rd, rcv[1], True)
     got = rx[...].astype(F32)
@@ -378,10 +433,11 @@
 
 
 def main_call(groups, own, halo, hubs, *args):
-    hid = args[6].shape[1]
+    hid = args[7].shape[1]
     per = hubs // groups
     slots, dsts = own + halo + hubs, own + hubs
-    pairs = args[0].shape[0] // CHUNK_ROWS + slots // SRC_BLOCK * (dsts // DST_BLOCK)
+    edges = args[0].size
+    pairs = edges // CHUNK + slots // SRC_BLOCK * (dsts // DST_BLOCK)
     vmem = pl.BlockSpec(memory_space=pltpu.VMEM)
     blocks = [
         ("a", (2 * per, LANES), BF16), ("a", (per, LANES), F32), ("b", (per, LANES), BF16), ("b", (per, LANES), F32),
@@ -398,6 +454,11 @@
         scratch_shapes=sends + recvs + [
             pltpu.VMEM((8, 256), jnp.int32),
             pltpu.SMEM((8, 256), jnp.int32),
+            pltpu.VMEM((edges // LANES, LANES), jnp.int32),
+            pltpu.VMEM((edges // LANES // 8, 8, LANES), jnp.int32),
+            pltpu.VMEM((edges // LANES // 8, 8, LANES), F32),
+            pltpu.VMEM((edges // CHUNK, CHUNK), jnp.int32),
+            pltpu.VMEM((edges // CHUNK, CHUNK), F32),
             pltpu.VMEM((pairs + 1, SRC_BLOCK, DST_BLOCK), F32),
             pltpu.VMEM((slots, dsts), BF16),
             pltpu.VMEM((slots, dsts), BF16),
@@ -432,14 +493,9 @@
         feat_out = dy.shape[1]
         hid = w_first.shape[1]
         halo, hubs = send.shape[0], hub_ids.shape[0]
-        slots, dsts = own + halo + hubs, own + hubs
-        bucket = jnp.right_shift(src, SRC_BLOCK.bit_length() - 1) * (dsts // DST_BLOCK)
-        bucket = bucket + jnp.right_shift(dst, DST_BLOCK.bit_length() - 1)
-        keys = bucket * BUCKET + jnp.bitwise_and(src, SRC_BLOCK - 1) * DST_BLOCK + jnp.bitwise_and(dst, DST_BLOCK - 1)
-        keys, weights = lax.sort((keys, w), num_keys=1, is_stable=False)
-        keys, weights = keys.reshape(-1, LANES), weights.reshape(-1, LANES)
+        edges = [v.reshape(-1, LANES) for v in (dst, src, w)]
         raw = main_call(
-            groups, own, halo, hubs, keys, weights, x.T, dy.T, send[None, :], hub_ids[None, :], b_first[None, :],
+            groups, own, halo, hubs, *edges, x.T, dy.T, send[None, :], hub_ids[None, :], b_first[None, :],
             w_first, w_second.T)
         dx, gw1, gw2, gb1, gb2 = pl.pallas_call(
             output_kernel,

time: 82.8 us -> 77.7 us (0.938); the launches traced: 81.8 us -> 77.7 us
  other arithmetic: 9.56 us -> 0 us
  Pallas kernels: 71.6 us -> 77.1 us
    sort x1 -> x0, other arithmetic: 8.51 us -> none  [device_step(): keys, weights = lax.sort((keys, w), num_keys=1, is_stable=False)]
    pallas_call x1, Pallas kernels: 69.8 us -> 75.3 us  [main_call(): pl.pallas_call(functools.partial(main_kernel, groups, own, halo, hubs), o...]
    add x1 -> x0, other arithmetic: 1.05 us -> none  [device_step(): bucket * BUCKET + jnp.bitwise_and(src, SRC_BLOCK - 1) * DST_BLOCK]
where the time goes in v8:
time: 77.7 us
  Pallas kernels  77.1 us (99%)
    pallas_call x1, Pallas kernels, main_call(): pl.pallas_call(functools.partial(main_kernel, groups, own, halo, hubs), o...  75.3 us
    pallas_call x1, Pallas kernels, device_step(): pl.pallas_call(output_kernel, out_shape=[jax.ShapeDtypeStruct(shape, F32)...  1.8 us

profile of v8, /device:TPU:1, one launch (start us, length us, event | category | flops | bytes accessed | tf_op | source)
XLA Modules:
  0.0 77.7 jit_solution(1781547406041453976)
XLA Ops:
  0.6 75.3 %main_exchange.1 = (f32[128,512]{1,0:T(8,128)}, f32[128,1,512]{2,1,0:T(1,128)}, f32[1,384]{1,0:T(1,128)}) custom-call(s32[256,128]{1,0:T(8,128)} %bitcast.13, s32[256,128]{1,0:T(8,128)} %bitcast.14, f32[256,128]{1,0:T(8,128)} %bitcast.15, bf16[100,512]{1,0:T(8,128)(2,1)} %bitcast.16, f32[47,512]{1,0:T(8,128)} %bitcast.17, s32[1,256]{1,0:T(1,128)} %bitcast.19, ...), custom_call_target="tpu_custom_call" | custom-call | tf_op jit(solution)/shard_map/main_exchange/pallas_call | solution.py:449
  75.9 1.8 %outputs.1 = (f32[100,512]{1,0:T(8,128)}, f32[100,256]{1,0:T(8,128)}, f32[47,256]{1,0:T(8,128)}, f32[1,256]{1,0:T(1,128)}, f32[1,47]{1,0:T(1,128)}) custom-call(f32[128,512]{1,0:T(8,128)} %get-tuple-element.13.dxt_ref, f32[128,1,512]{2,1,0:T(1,128)} %get-tuple-element.14.gw_ref, f32[1,384]{1,0:T(1,128)} %get-tuple-element.15.bias_ref), custom_call_target="tpu_custom_call" | custom-call | tf_op jit(solution)/shard_map/outputs/pallas_call | solution.py:500

commit v9 on v8

--- a/solution.py
+++ b/solution.py
@@ -89,9 +89,9 @@
     return a
 
 
-SRC_BLOCK, DST_BLOCK = 128, 256
+SRC_BLOCK, DST_BLOCK = 64, 256
 BUCKET = SRC_BLOCK * DST_BLOCK
-CHUNK, UNROLL = 256, 19
+CHUNK, UNROLL = 256, 44
 
 
 def bitonic(keys, weights, low, high):
@@ -152,11 +152,14 @@
     shift = size.bit_length() - 1
     total = 1 << buckets.bit_length()
 
-    def count(i, carry):
+    def count(at, i, carry):
         bucket = jnp.right_shift(key_ref[pl.ds(pl.multiple_of(i * 8, 8), 8), :], BUCKET.bit_length() - 1)
-        return tuple(c + jnp.where(bucket <= b, 1, 0) for b, c in enumerate(carry))
-
-    counts = lax.fori_loop(0, key_ref.shape[0] // 8, count, (jnp.zeros((8, LANES), jnp.int32),) * buckets)
+        return tuple(c + jnp.where(bucket <= at + b, 1, 0) for b, c in enumerate(carry))
+
+    counts = ()
+    for at in range(0, buckets, 24):
+        zeros = (jnp.zeros((8, LANES), jnp.int32),) * min(24, buckets - at)
+        counts += lax.fori_loop(0, key_ref.shape[0] // 8, functools.partial(count, at), zeros)
     counts = [ring_sum(c, 0)[:1] for c in counts]
     none = jnp.zeros((1, LANES), jnp.int32)
     counts = [none] + counts + [counts[-1]] * (total - buckets)
@@ -180,29 +183,29 @@
         plan_ref[:, half * LANES:(half + 1) * LANES] = jnp.concatenate(rows, axis=0)
 
 
-def add_pairs(plan_ref, key_ref, w_ref, cum_ref, low, high):
+def add_pairs(plan_ref, key_ref, w_ref, column_ref, cum_ref, low, high):
     src_ids = lax.broadcasted_iota(jnp.int32, (SRC_BLOCK, LANES), 0).astype(F32).astype(BF16)
-    dst_ids = lax.broadcasted_iota(jnp.int32, (DST_BLOCK, LANES), 0).astype(F32).astype(BF16)
+    lane = lax.broadcasted_iota(jnp.int32, (CHUNK, LANES), 1)
+    dst_ids = [(lane + at).astype(F32).astype(BF16) for at in range(0, DST_BLOCK, LANES)]
     one, zero = jnp.ones((), BF16), jnp.zeros((), BF16)
 
     def step(it, carry):
         work = []
         for u in range(UNROLL):
             b, c = plan_ref[0, it * UNROLL + u], plan_ref[1, it * UNROLL + u]
-            rel_row = key_ref[pl.ds(c, 1), :] - b * BUCKET
+            src_row = jnp.right_shift(key_ref[pl.ds(c, 1), :] - b * BUCKET, DST_BLOCK.bit_length() - 1)
+            src_row = jnp.where((src_row >= 0) & (src_row < SRC_BLOCK), src_row, 512).astype(F32)
             w_row = w_ref[pl.ds(c, 1), :]
-            lhs, rhs = [], []
+            lhs = []
             for r in range(0, CHUNK, LANES):
-                rel, weight = rel_row[:, r:r + LANES], w_row[:, r:r + LANES]
-                src = jnp.right_shift(rel, DST_BLOCK.bit_length() - 1)
-                src = jnp.where((src >= 0) & (src < SRC_BLOCK), src, 512).astype(F32).astype(BF16)
-                dst = jnp.bitwise_and(rel, DST_BLOCK - 1).astype(F32).astype(BF16)
+                src, weight = src_row[:, r:r + LANES].astype(BF16), w_row[:, r:r + LANES]
                 hit = src_ids == jnp.broadcast_to(src, src_ids.shape)
                 lhs.append(jnp.concatenate(
                     [jnp.where(hit, jnp.broadcast_to(p, src_ids.shape), zero) for p in split3(weight)], axis=0))
-                rhs.append(jnp.where(dst_ids == jnp.broadcast_to(dst, dst_ids.shape), one, zero))
+            dst = jnp.take_along_axis(column_ref[...], jnp.broadcast_to(c, lane.shape), axis=1).astype(BF16)
+            rhs = [jnp.where(dst == ids, one, zero) for ids in dst_ids]
             work.append((jnp.concatenate(lhs, axis=1), jnp.concatenate(rhs, axis=1)))
-        outs = [dot(lhs, rhs, 1, 1) for lhs, rhs in work]
+        outs = [dot(lhs, rhs) for lhs, rhs in work]
         total = cum_ref[it * UNROLL]
         for u, out in enumerate(outs):
             same = jnp.broadcast_to(plan_ref[2, it * UNROLL + u], (1, DST_BLOCK)) > 0
@@ -222,7 +225,7 @@
                 dxt_ref, gw_ref, bias_ref,
                 sx, sd, hx, hd, s1, s2, s3, s4, s5, s6, s7, s8,
                 rx, rd, gx, gd, r1, r2, r3, r4, r5, r6, r7,
-                list_ref, plan_ref, raw_ref, sort_k, sort_w, key_ref, w_ref, cum_ref, hi_ref, mid_ref, low_ref, hubrow_ref, pt_ref, g2_ref, g1_ref, dy_ref, zt_ref, plan_sem, *sems):
+                list_ref, plan_ref, raw_ref, sort_k, sort_w, key_ref, w_ref, column_ref, cum_ref, hi_ref, mid_ref, low_ref, hubrow_ref, pt_ref, g2_ref, g1_ref, dy_ref, zt_ref, plan_sem, *sems):
     count = len(sems) // 2
     snd, rcv = sems[:count], sems[count:]
     adj = (hi_ref, mid_ref, low_ref)
@@ -235,7 +238,7 @@
     me = lax.axis_index("graph")
     barrier = greet_all(groups, me)
     steps = (cum_ref.shape[0] - 1) // UNROLL
-    middle = steps * 3 // 8
+    middle = steps // 2
     cum_ref[0] = jnp.zeros((SRC_BLOCK, DST_BLOCK), F32)
     dst, src = dst_ref[...], src_ref[...]
     bucket = jnp.right_shift(src, SRC_BLOCK.bit_length() - 1) * tops + jnp.right_shift(dst, DST_BLOCK.bit_length() - 1)
@@ -276,10 +279,12 @@
     zt_ref[:, :own] = jnp.where(plain_row, dot(w1_t, xt), 0.0).astype(BF16)
     dy = dyt.T
     keys, weights = bitonic(sort_k[...], sort_w[...], phases - 3, phases)
-    key_ref[...] = keys.reshape(raw_ref.shape).T
+    keys = keys.reshape(raw_ref.shape)
+    column_ref[...] = jnp.bitwise_and(keys, DST_BLOCK - 1).astype(F32)
+    key_ref[...] = keys.T
     w_ref[...] = weights.reshape(raw_ref.shape).T
     plan.wait()
-    add_pairs(plan_ref, key_ref, w_ref, cum_ref, 0, middle)
+    add_pairs(plan_ref, key_ref, w_ref, column_ref, cum_ref, 0, middle)
     wait_all(groups, rx, rcv[0], True)
     wait_all(groups, rd, rcv[1], True)
     got = rx[...].astype(F32)
@@ -289,31 +294,35 @@
     send_all(groups, me, [("b", hx, gx, snd[2], rcv[2]), ("b", hd, gd, snd[3], rcv[3])])
 
     home_x = jnp.concatenate([home_x, jnp.zeros((8 - per, LANES), F32)], axis=0).astype(BF16)
-    add_pairs(plan_ref, key_ref, w_ref, cum_ref, middle, steps)
+    add_pairs(plan_ref, key_ref, w_ref, column_ref, cum_ref, middle, steps)
+
+    group = LANES // SRC_BLOCK
 
     def renamed(i):
-        cell = [cum_ref[plan_ref[3, i * tops + j]] for j in range(tops)]
+        cell = [
+            jnp.concatenate([cum_ref[plan_ref[3, (i * group + g) * tops + j]] for g in range(group)], axis=0)
+            for j in range(tops)]
         mine = jnp.concatenate(cell[:own // DST_BLOCK], axis=1)
         pieces = split3(mine)
         return mine, pieces, jnp.concatenate(cell[own // DST_BLOCK:], axis=1) + exact3_right(pieces, sel_t)
 
     def rename(i, carry):
         _, pieces, hub = renamed(i)
-        rows = pl.ds(pl.multiple_of(i * SRC_BLOCK, SRC_BLOCK), SRC_BLOCK)
+        rows = pl.ds(pl.multiple_of(i * LANES, LANES), LANES)
         for ref, left, right in zip(adj, pieces, split3(hub)):
             ref[rows, :own] = left
             ref[rows, own:] = right
         return carry
 
     def rename_hub(i, carry):
-        mine, _, hub = renamed(first_hub // SRC_BLOCK + i)
-        rows = pl.ds(pl.multiple_of(i * SRC_BLOCK, SRC_BLOCK), SRC_BLOCK)
+        mine, _, hub = renamed(first_hub // LANES + i)
+        rows = pl.ds(pl.multiple_of(i * LANES, LANES), LANES)
         hubrow_ref[rows, :own] = mine
         hubrow_ref[rows, own:] = hub
         return carry
 
-    lax.fori_loop(0, first_hub // SRC_BLOCK, rename, 0)
-    lax.fori_loop(0, hubs // SRC_BLOCK, rename_hub, 0)
+    lax.fori_loop(0, first_hub // LANES, rename, 0)
+    lax.fori_loop(0, hubs // LANES, rename_hub, 0)
     halo_x = got[:, :per, :].reshape(halo, LANES).astype(BF16)
     column = jnp.broadcast_to(jnp.where(lane == feat_in, 1.0, 0.0), (8, LANES)).astype(BF16)
     halo_row = dot(column, halo_x, 1, 1)[:1].astype(jnp.int32)
@@ -459,6 +468,7 @@
             pltpu.VMEM((edges // LANES // 8, 8, LANES), F32),
             pltpu.VMEM((edges // CHUNK, CHUNK), jnp.int32),
             pltpu.VMEM((edges // CHUNK, CHUNK), F32),
+            pltpu.VMEM((edges // LANES, LANES), F32),
             pltpu.VMEM((pairs + 1, SRC_BLOCK, DST_BLOCK), F32),
             pltpu.VMEM((slots, dsts), BF16),
             pltpu.VMEM((slots, dsts), BF16),

time: 77.7 us -> 74.7 us (0.961)
  Pallas kernels: 77.1 us -> 73.7 us
    pallas_call x1, Pallas kernels: 75.3 us -> 71.9 us  [main_call(): pl.pallas_call(functools.partial(main_kernel, groups, own, halo, hubs), o...]
where the time goes in v9:
time: 74.7 us; the launch traced here: 74.4 us
  Pallas kernels  73.7 us (99%)
    pallas_call x1, Pallas kernels, main_call(): pl.pallas_call(functools.partial(main_kernel, groups, own, halo, hubs), o...  71.9 us
    pallas_call x1, Pallas kernels, device_step(): pl.pallas_call(output_kernel, out_shape=[jax.ShapeDtypeStruct(shape, F32)...  1.8 us

profile of v9, /device:TPU:1, one launch (start us, length us, event | category | flops | bytes accessed | tf_op | source)
XLA Modules:
  0.0 74.4 jit_solution(16402494552534928282)
XLA Ops:
  0.6 71.9 %main_exchange.1 = (f32[128,512]{1,0:T(8,128)}, f32[128,1,512]{2,1,0:T(1,128)}, f32[1,384]{1,0:T(1,128)}) custom-call(s32[256,128]{1,0:T(8,128)} %bitcast.13, s32[256,128]{1,0:T(8,128)} %bitcast.14, f32[256,128]{1,0:T(8,128)} %bitcast.15, bf16[100,512]{1,0:T(8,128)(2,1)} %bitcast.16, f32[47,512]{1,0:T(8,128)} %bitcast.17, s32[1,256]{1,0:T(1,128)} %bitcast.19, ...), custom_call_target="tpu_custom_call" | custom-call | tf_op jit(solution)/shard_map/main_exchange/pallas_call | solution.py:458
  72.6 1.8 %outputs.1 = (f32[100,512]{1,0:T(8,128)}, f32[100,256]{1,0:T(8,128)}, f32[47,256]{1,0:T(8,128)}, f32[1,256]{1,0:T(1,128)}, f32[1,47]{1,0:T(1,128)}) custom-call(f32[128,512]{1,0:T(8,128)} %get-tuple-element.13.dxt_ref, f32[128,1,512]{2,1,0:T(1,128)} %get-tuple-element.14.gw_ref, f32[1,384]{1,0:T(1,128)} %get-tuple-element.15.bias_ref), custom_call_target="tpu_custom_call" | custom-call | tf_op jit(solution)/shard_map/outputs/pallas_call | solution.py:510

commit v10 on v9

--- a/solution.py
+++ b/solution.py
@@ -222,8 +222,8 @@
 
 
 def main_kernel(groups, own, halo, hubs, dst_ref, src_ref, w_in_ref, xt_ref, dyt_ref, send_ref, hub_ref, b1_ref, w1_ref, w2t_ref,
-                dxt_ref, gw_ref, bias_ref,
-                sx, sd, hx, hd, s1, s2, s3, s4, s5, s6, s7, s8,
+                dxt_ref, gw1_ref, gw2_ref, bias_ref,
+                sx, sd, hx, hd, s1, s2, s3, s4, s5, s6, s7, s8, s9,
                 rx, rd, gx, gd, r1, r2, r3, r4, r5, r6, r7,
                 list_ref, plan_ref, raw_ref, sort_k, sort_w, key_ref, w_ref, column_ref, cum_ref, hi_ref, mid_ref, low_ref, hubrow_ref, pt_ref, g2_ref, g1_ref, dy_ref, zt_ref, plan_sem, *sems):
     count = len(sems) // 2
@@ -267,7 +267,8 @@
     hub_dt = picked[3 * LANES:, halo:] + picked[2 * LANES:3 * LANES, halo:] + picked[LANES:2 * LANES, halo:]
     sx[:, :per, :] = rows_to_blocks(picked[:LANES, :halo].T, groups).astype(BF16)
     sx[:, per:, :] = rows_to_blocks(picked[:LANES, halo:].T, groups).astype(BF16)
-    sd[...] = rows_to_blocks(hub_dt.T, groups)
+    hub_d = rows_to_blocks(hub_dt.T, groups)
+    sd[...] = hub_d[:, :1, :] + pltpu.roll(hub_d[:, 1:, :], LANES // 2, 2)
     phases = raw_ref.size.bit_length() - 1
     sort_k[...], sort_w[...] = bitonic(
         raw_ref[...].reshape(sort_k.shape), w_in_ref[...].reshape(sort_w.shape), 1, phases - 4)
@@ -357,7 +358,9 @@
     wait_all(groups, gd, rcv[3], True)
     hub_x = gx[...].astype(F32).reshape(hubs, LANES).astype(BF16)
     zt_ref[:, first_hub:] = dot(w1_t, hub_x, 1, 1).astype(BF16)
-    d_hub = pack(gd[...].reshape(hubs, LANES))
+    hub_d = gd[...].reshape(groups, LANES)
+    hub_d = jnp.stack([jnp.where(half, hub_d, 0.0), jnp.where(half, pltpu.roll(hub_d, LANES // 2, 1), 0.0)], axis=1)
+    d_hub = pack(hub_d.reshape(hubs, LANES))
     hub_slots = slice(first_hub, slots)
     y_hub = (pt_ref[...] + forward(hub_slots, hub_cols)).T
     s1[:, :, LANES:] = rows_to_blocks(y_hub, groups)
@@ -417,7 +420,8 @@
     wait_all(groups, r3, rcv[6], True)
     wait_all(groups, r4, rcv[7], True)
     bias_ref[...] = r4[...].sum(axis=0)
-    s8[:, hid:] = r3[...].sum(axis=0)
+    s9[...] = r3[...].sum(axis=0)
+    send_all(groups, me, [("b", s9, gw2_ref, snd[12], rcv[12])])
     wait_all(groups, r5, rcv[8], True)
     home_dz1 = jnp.concatenate([r5[:, per:, :].sum(axis=0), jnp.zeros((8 - per, hid), F32)], axis=0).astype(BF16)
     back = r5[:, :per, :].reshape(halo, hid)
@@ -425,20 +429,22 @@
     dz1 = jnp.where(plain, dz1, 0.0).astype(BF16)
     gw1 = dot(xt, dz1) + dot(home_x, home_dz1, 0, 0)
     s6[...] = rows_to_blocks(gw1, groups)
+    send_all(groups, me, [("a", s6, r6, snd[9], rcv[9])])
+
     s7[...] = dot(home_dz1, w1, 1, 1)[:per]
-    send_all(groups, me, [("a", s6, r6, snd[9], rcv[9]), ("b", s7, r7, snd[10], rcv[10])])
-
+    send_all(groups, me, [("b", s7, r7, snd[10], rcv[10])])
     dxt = dot(w1, dz1, 1, 1)
     wait_all(groups, r6, rcv[9], True)
-    s8[:, :hid] = r6[...].sum(axis=0)
-    send_all(groups, me, [("b", s8, gw_ref, snd[11], rcv[11])])
+    s8[...] = r6[...].sum(axis=0)
+    send_all(groups, me, [("b", s8, gw1_ref, snd[11], rcv[11])])
 
     wait_all(groups, r7, rcv[10], True)
     hub_dx = r7[...].reshape(hubs, LANES).T
     dxt_ref[...] = dxt + exact3_right(split3(hub_dx), sel_f.T.astype(BF16))
-    for buf, sem in zip((rx, rd, gx, gd, r1, r2, r3, r4, r5, r6, r7, gw_ref), snd):
+    wait_all(groups, gw2_ref, rcv[12], True)
+    for buf, sem in zip((rx, rd, gx, gd, r1, r2, r3, r4, r5, r6, r7, gw1_ref, gw2_ref), snd):
         wait_all(groups, buf, sem, False)
-    wait_all(groups, gw_ref, rcv[11], True)
+    wait_all(groups, gw1_ref, rcv[11], True)
 
 
 def main_call(groups, own, halo, hubs, *args):
@@ -449,17 +455,19 @@
     pairs = edges // CHUNK + slots // SRC_BLOCK * (dsts // DST_BLOCK)
     vmem = pl.BlockSpec(memory_space=pltpu.VMEM)
     blocks = [
-        ("a", (2 * per, LANES), BF16), ("a", (per, LANES), F32), ("b", (per, LANES), BF16), ("b", (per, LANES), F32),
+        ("a", (2 * per, LANES), BF16), ("a", (1, LANES), F32), ("b", (per, LANES), BF16), ("b", (1, LANES), F32),
         ("a", (per, LANES + hid), F32), ("b", (per, hid), F32), ("a", (1, hid), F32), ("b", (1, hid + LANES), F32),
-        ("a", (2 * per, hid), F32), ("a", (1, hid), F32), ("b", (per, LANES), F32), ("b", (1, 2 * hid), F32)]
+        ("a", (2 * per, hid), F32), ("a", (1, hid), F32), ("b", (per, LANES), F32), ("b", (1, hid), F32), ("b", (1, hid), F32)]
     sends = [pltpu.VMEM(((groups,) if k == "a" else ()) + b, t) for k, b, t in blocks]
-    recvs = [pltpu.VMEM((groups,) + b, t) for _, b, t in blocks[:-1]]
+    recvs = [pltpu.VMEM((groups,) + b, t) for _, b, t in blocks[:-2]]
     shape = jax.ShapeDtypeStruct
     return pl.pallas_call(
         functools.partial(main_kernel, groups, own, halo, hubs),
-        out_shape=[shape((LANES, own), F32), shape((groups, 1, 2 * hid), F32), shape((1, hid + LANES), F32)],
+        out_shape=[
+            shape((LANES, own), F32), shape((groups, 1, hid), F32), shape((groups, 1, hid), F32),
+            shape((1, hid + LANES), F32)],
         in_specs=[vmem] * len(args),
-        out_specs=[vmem] * 3,
+        out_specs=[vmem] * 4,
         scratch_shapes=sends + recvs + [
             pltpu.VMEM((8, 256), jnp.int32),
             pltpu.SMEM((8, 256), jnp.int32),
@@ -485,12 +493,11 @@
     )(*args)
 
 
-def output_kernel(dxt_ref, gw_ref, bias_ref, dx_out, gw1_out, gw2_out, b1_out, b2_out):
+def output_kernel(dxt_ref, gw1_ref, gw2_ref, bias_ref, dx_out, gw1_out, gw2_out, b1_out, b2_out):
     feat_in, feat_out, hid = dx_out.shape[0], gw2_out.shape[0], gw2_out.shape[1]
     dx_out[...] = dxt_ref[:feat_in, :]
-    gw = gw_ref[...].reshape(gw_ref.shape[0], 2 * hid)
-    gw1_out[...] = gw[:feat_in, :hid]
-    gw2_out[...] = gw[:feat_out, hid:]
+    gw1_out[...] = gw1_ref[...].reshape(gw1_ref.shape[0], hid)[:feat_in, :]
+    gw2_out[...] = gw2_ref[...].reshape(gw2_ref.shape[0], hid)[:feat_out, :]
     b1_out[...] = bias_ref[:, :hid]
     b2_out[...] = bias_ref[:, hid:hid + feat_out]
 

time: 74.7 us -> 73.2 us (0.980)
  Pallas kernels: 73.7 us -> 72.5 us
    pallas_call x1, Pallas kernels: 71.9 us -> 70.7 us  [main_call(): pl.pallas_call(functools.partial(main_kernel, groups, own, halo, hubs), o...]
where the time goes in v10:
time: 73.2 us; the launch traced here: 73.1 us
  Pallas kernels  72.5 us (99%)
    pallas_call x1, Pallas kernels, main_call(): pl.pallas_call(functools.partial(main_kernel, groups, own, halo, hubs), o...  70.7 us
    pallas_call x1, Pallas kernels, device_step(): pl.pallas_call(output_kernel, out_shape=[jax.ShapeDtypeStruct(shape, F32)...  1.83 us

profile of v10, /device:TPU:1, one launch (start us, length us, event | category | flops | bytes accessed | tf_op | source)
XLA Modules:
  0.0 73.1 jit_solution(2591658930762430275)
XLA Ops:
  0.6 70.7 %main_exchange.1 = (f32[128,512]{1,0:T(8,128)}, f32[128,1,256]{2,1,0:T(1,128)}, f32[128,1,256]{2,1,0:T(1,128)}, f32[1,384]{1,0:T(1,128)}) custom-call(s32[256,128]{1,0:T(8,128)} %bitcast.13, s32[256,128]{1,0:T(8,128)} %bitcast.14, f32[256,128]{1,0:T(8,128)} %bitcast.15, bf16[100,512]{1,0:T(8,128)(2,1)} %bitcast.16, f32[47,512]{1,0:T(8,128)} %bitcast.17, ...), custom_call_target="tpu_custom_call" | custom-call | tf_op jit(solution)/shard_map/main_exchange/pallas_call | solution.py:464
  71.3 1.8 %outputs.1 = (f32[100,512]{1,0:T(8,128)}, f32[100,256]{1,0:T(8,128)}, f32[47,256]{1,0:T(8,128)}, f32[1,256]{1,0:T(1,128)}, f32[1,47]{1,0:T(1,128)}) custom-call(f32[128,512]{1,0:T(8,128)} %get-tuple-element.14.dxt_ref, f32[128,1,256]{2,1,0:T(1,128)} %get-tuple-element.15.gw1_ref, f32[128,1,256]{2,1,0:T(1,128)} %get-tuple-element.16.gw2_ref, ...), custom_call_target="tpu_custom_call" | custom-call | tf_op jit(solution)/shard_map/outputs/pallas_call | solution.py:517

commit v11 on v10

--- a/solution.py
+++ b/solution.py
@@ -91,7 +91,7 @@
 
 SRC_BLOCK, DST_BLOCK = 64, 256
 BUCKET = SRC_BLOCK * DST_BLOCK
-CHUNK, UNROLL = 256, 44
+CHUNK, UNROLL = 256, 88
 
 
 def bitonic(keys, weights, low, high):
@@ -153,13 +153,15 @@
     total = 1 << buckets.bit_length()
 
     def count(at, i, carry):
-        bucket = jnp.right_shift(key_ref[pl.ds(pl.multiple_of(i * 8, 8), 8), :], BUCKET.bit_length() - 1)
-        return tuple(c + jnp.where(bucket <= at + b, 1, 0) for b, c in enumerate(carry))
-
-    counts = ()
+        bucket = jnp.right_shift(key_ref[pl.ds(pl.multiple_of(i * block, block), block), :], BUCKET.bit_length() - 1)
+        return tuple(
+            c + jnp.sum(jnp.where(bucket <= at + b, 1, 0).reshape(block // 8, 8, LANES), axis=0)
+            for b, c in enumerate(carry))
+
+    counts, block = (), 32
     for at in range(0, buckets, 24):
         zeros = (jnp.zeros((8, LANES), jnp.int32),) * min(24, buckets - at)
-        counts += lax.fori_loop(0, key_ref.shape[0] // 8, functools.partial(count, at), zeros)
+        counts += lax.fori_loop(0, key_ref.shape[0] // block, functools.partial(count, at), zeros)
     counts = [ring_sum(c, 0)[:1] for c in counts]
     none = jnp.zeros((1, LANES), jnp.int32)
     counts = [none] + counts + [counts[-1]] * (total - buckets)

time: 73.2 us -> 74.5 us (1.018)
  Pallas kernels: 72.5 us -> 73.7 us
    pallas_call x1, Pallas kernels: 70.7 us -> 71.9 us  [main_call(): pl.pallas_call(functools.partial(main_kernel, groups, own, halo, hubs), o...]
where the time goes in v11:
time: 74.5 us; the launch traced here: 74.3 us
  Pallas kernels  73.7 us (99%)
    pallas_call x1, Pallas kernels, main_call(): pl.pallas_call(functools.partial(main_kernel, groups, own, halo, hubs), o...  71.9 us
    pallas_call x1, Pallas kernels, device_step(): pl.pallas_call(output_kernel, out_shape=[jax.ShapeDtypeStruct(shape, F32)...  1.83 us

profile of v11, /device:TPU:1, one launch (start us, length us, event | category | flops | bytes accessed | tf_op | source)
XLA Modules:
  0.0 74.3 jit_solution(10886094478325535374)
XLA Ops:
  0.6 71.9 %main_exchange.1 = (f32[128,512]{1,0:T(8,128)}, f32[128,1,256]{2,1,0:T(1,128)}, f32[128,1,256]{2,1,0:T(1,128)}, f32[1,384]{1,0:T(1,128)}) custom-call(s32[256,128]{1,0:T(8,128)} %bitcast.13, s32[256,128]{1,0:T(8,128)} %bitcast.14, f32[256,128]{1,0:T(8,128)} %bitcast.15, bf16[100,512]{1,0:T(8,128)(2,1)} %bitcast.16, f32[47,512]{1,0:T(8,128)} %bitcast.17, ...), custom_call_target="tpu_custom_call" | custom-call | tf_op jit(solution)/shard_map/main_exchange/pallas_call | solution.py:466
  72.5 1.8 %outputs.1 = (f32[100,512]{1,0:T(8,128)}, f32[100,256]{1,0:T(8,128)}, f32[47,256]{1,0:T(8,128)}, f32[1,256]{1,0:T(1,128)}, f32[1,47]{1,0:T(1,128)}) custom-call(f32[128,512]{1,0:T(8,128)} %get-tuple-element.14.dxt_ref, f32[128,1,256]{2,1,0:T(1,128)} %get-tuple-element.15.gw1_ref, f32[128,1,256]{2,1,0:T(1,128)} %get-tuple-element.16.gw2_ref, ...), custom_call_target="tpu_custom_call" | custom-call | tf_op jit(solution)/shard_map/outputs/pallas_call | solution.py:519

commit v12 on v11

--- a/solution.py
+++ b/solution.py
@@ -91,7 +91,7 @@
 
 SRC_BLOCK, DST_BLOCK = 64, 256
 BUCKET = SRC_BLOCK * DST_BLOCK
-CHUNK, UNROLL = 256, 88
+CHUNK, UNROLL = 256, 44
 
 
 def bitonic(keys, weights, low, high):
@@ -223,7 +223,17 @@
     return a.reshape(groups, a.shape[0] // groups, a.shape[1])
 
 
-def main_kernel(groups, own, halo, hubs, dst_ref, src_ref, w_in_ref, xt_ref, dyt_ref, send_ref, hub_ref, b1_ref, w1_ref, w2t_ref,
+def main_kernel(groups, own, halo, hubs, inputs, *refs):
+    given, refs = refs[:inputs], refs[inputs:]
+    outs, refs = refs[:4], refs[4:]
+    held, sems, refs = refs[:inputs], refs[inputs:2 * inputs], refs[2 * inputs:]
+    loads = [pltpu.make_async_copy(*item) for item in zip(given, held, sems)]
+    for load in loads:
+        load.start()
+    main_body(groups, own, halo, hubs, loads, *held, *outs, *refs)
+
+
+def main_body(groups, own, halo, hubs, loads, dst_ref, src_ref, w_in_ref, xt_ref, dyt_ref, send_ref, hub_ref, b1_ref, w1_ref, w2t_ref,
                 dxt_ref, gw1_ref, gw2_ref, bias_ref,
                 sx, sd, hx, hd, s1, s2, s3, s4, s5, s6, s7, s8, s9,
                 rx, rd, gx, gd, r1, r2, r3, r4, r5, r6, r7,
@@ -239,6 +249,8 @@
     tops = dsts // DST_BLOCK
     me = lax.axis_index("graph")
     barrier = greet_all(groups, me)
+    for load in loads:
+        load.wait()
     steps = (cum_ref.shape[0] - 1) // UNROLL
     middle = steps // 2
     cum_ref[0] = jnp.zeros((SRC_BLOCK, DST_BLOCK), F32)
@@ -464,13 +476,13 @@
     recvs = [pltpu.VMEM((groups,) + b, t) for _, b, t in blocks[:-2]]
     shape = jax.ShapeDtypeStruct
     return pl.pallas_call(
-        functools.partial(main_kernel, groups, own, halo, hubs),
+        functools.partial(main_kernel, groups, own, halo, hubs, len(args)),
         out_shape=[
             shape((LANES, own), F32), shape((groups, 1, hid), F32), shape((groups, 1, hid), F32),
             shape((1, hid + LANES), F32)],
-        in_specs=[vmem] * len(args),
+        in_specs=[pl.BlockSpec(memory_space=pl.ANY)] * len(args),
         out_specs=[vmem] * 4,
-        scratch_shapes=sends + recvs + [
+        scratch_shapes=[pltpu.VMEM(a.shape, a.dtype) for a in args] + [pltpu.SemaphoreType.DMA] * len(args) + sends + recvs + [
             pltpu.VMEM((8, 256), jnp.int32),
             pltpu.SMEM((8, 256), jnp.int32),
             pltpu.VMEM((edges // LANES, LANES), jnp.int32),

time: 74.5 us -> 72 us (0.966)
  Pallas kernels: 73.7 us -> 71.6 us
    pallas_call x1, Pallas kernels: 71.9 us -> 69.8 us  [main_call(): pl.pallas_call(functools.partial(main_kernel, groups, own, halo, hubs, le...]
where the time goes in v12:
time: 72 us; the launch traced here: 72.2 us
  Pallas kernels  71.6 us (99%)
    pallas_call x1, Pallas kernels, main_call(): pl.pallas_call(functools.partial(main_kernel, groups, own, halo, hubs, le...  69.8 us
    pallas_call x1, Pallas kernels, device_step(): pl.pallas_call(output_kernel, out_shape=[jax.ShapeDtypeStruct(shape, F32)...  1.83 us

profile of v12, /device:TPU:1, one launch (start us, length us, event | category | flops | bytes accessed | tf_op | source)
XLA Modules:
  0.0 72.2 jit_solution(9578953529923280010)
XLA Ops:
  0.6 69.8 %main_exchange.1 = (f32[128,512]{1,0:T(8,128)}, f32[128,1,256]{2,1,0:T(1,128)}, f32[128,1,256]{2,1,0:T(1,128)}, f32[1,384]{1,0:T(1,128)}) custom-call(s32[256,128]{1,0:T(8,128)} %bitcast.13, s32[256,128]{1,0:T(8,128)} %bitcast.14, f32[256,128]{1,0:T(8,128)} %bitcast.15, bf16[100,512]{1,0:T(8,128)(2,1)} %bitcast.16, f32[47,512]{1,0:T(8,128)} %bitcast.17, ...), custom_call_target="tpu_custom_call" | custom-call | tf_op jit(solution)/shard_map/main_exchange/pallas_call | solution.py:478
  70.4 1.8 %outputs.1 = (f32[100,512]{1,0:T(8,128)}, f32[100,256]{1,0:T(8,128)}, f32[47,256]{1,0:T(8,128)}, f32[1,256]{1,0:T(1,128)}, f32[1,47]{1,0:T(1,128)}) custom-call(f32[128,512]{1,0:T(8,128)} %get-tuple-element.14.dxt_ref, f32[128,1,256]{2,1,0:T(1,128)} %get-tuple-element.15.gw1_ref, f32[128,1,256]{2,1,0:T(1,128)} %get-tuple-element.16.gw2_ref, ...), custom_call_target="tpu_custom_call" | custom-call | tf_op jit(solution)/shard_map/outputs/pallas_call | solution.py:531
